TPU v7x, 32 devices: a whole 2x2x4 slice. The times are simulated.
32 devices in a mesh: cx: 4 (over y, core), cy: 8 (over z, x).
Axes of the slice: x: 2, y: 2, z: 4, core: 2. Of those that a mesh axis runs over, the one named last changes fastest.
Arguments:
- queries: bfloat16 [6144, 4096], P(('cx', 'cy')), may hold values from -300 to 300
- keys: bfloat16 [32768, 512], P(('cx', 'cy')), may hold values from -6 to 6
- values: bfloat16 [32768, 512], P(('cx', 'cy')), may hold values from -6 to 6
- d_out: bfloat16 [6144, 4096], P(('cx', 'cy')), may hold values from -6 to 6
- selection: int32 [96, 4, 16], replicated, may hold values from 0 to 415, as said below
Outputs:
- d_queries: float32 [6144, 4096], P(('cx', 'cy'))
- d_keys: float32 [32768, 512], P(('cx', 'cy'))
- d_values: float32 [32768, 512], P(('cx', 'cy'))
Inputs may be any that keep to these rules, and one draw needn't show every extreme that they name: `selection`: every entry is a block below 416. Over the 3 consecutive query blocks of one device (rows d * 3 to d * 3 + 2) all 192 entries differ, and at most 8 of them lie in the blocks k * 16 to k * 16 + 15 of any one k; that most is reached on every device.
All inputs are finite; a program needn't handle non-finite values.
Results may differ from a plain program's by a relative error of at most 0.0042.
Values may be sent and summed in bfloat16 or wider, within the bound.
No kernel may reach another device: no remote copies, remote signals or barrier semaphores. Data moves between devices by JAX's collectives and lax.ppermute only.
A program may use at most 192 MiB of HBM per device.

v0:
```python
import jax
import jax.numpy as jnp
from jax import lax
from jax.sharding import PartitionSpec as P

H = 32
KVH = 4
HD = 128
BLK = 64
TOPK = 16
QB_DEV = 3
KB_DEV = 16
GROUP = 8
PICKS = 192


def block_grads(q_rows, o_rows, key_rows, value_rows):
    scale = HD ** (-0.5)
    scores = (
        jnp.einsum("agzd,gkd->gzak", q_rows, key_rows, preferred_element_type=jnp.float32) * scale
    )
    probs = jax.nn.softmax(scores, axis=-1)
    probs_half = probs.astype(jnp.bfloat16)
    d_probs = jnp.einsum("agzd,gkd->gzak", o_rows, value_rows, preferred_element_type=jnp.float32)
    delta = jnp.sum(probs * d_probs, axis=-1, keepdims=True)
    d_scores = (probs * (d_probs - delta)).astype(jnp.bfloat16)
    d_query = (
        jnp.einsum("gzak,gkd->agzd", d_scores, key_rows, preferred_element_type=jnp.float32) * scale
    )
    d_key = (
        jnp.einsum("gzak,agzd->gkd", d_scores, q_rows, preferred_element_type=jnp.float32) * scale
    )
    d_value = jnp.einsum("gzak,agzd->gkd", probs_half, o_rows, preferred_element_type=jnp.float32)
    return (d_query, d_key, d_value)


def body(queries, keys, values, d_out, selection):
    outer = lax.axis_size("cx")
    inner = lax.axis_size("cy")
    devices = outer * inner
    myself = lax.axis_index("cx") * inner + lax.axis_index("cy")
    usable = devices * (KB_DEV - QB_DEV) // KB_DEV
    capacity = (PICKS + usable - 1) // usable
    slots = devices * capacity
    highest = lax.Precision.HIGHEST
    picks_all = selection.reshape(devices, PICKS)
    owner_all = picks_all // KB_DEV
    head_row = jnp.arange(PICKS, dtype=jnp.int32) // TOPK % KVH
    mine = (owner_all == myself).astype(jnp.float32)
    positions = jnp.arange(PICKS, dtype=jnp.int32)
    before = (positions[:, None] < positions[None, :]).astype(jnp.float32)
    ranks = jnp.dot(mine, before, precision=highest).astype(jnp.int32)
    copies = jnp.arange(capacity, dtype=jnp.int32)
    match = (mine[:, None, :] > 0.5) & (ranks[:, None, :] == copies[None, :, None])
    block_tab = jnp.sum(jnp.where(match, (picks_all % KB_DEV)[:, None, :], 0), axis=2).reshape(
        slots
    )
    head_tab = jnp.sum(jnp.where(match, head_row[None, None, :], 0), axis=2).reshape(slots)
    live = jnp.any(match, axis=2).reshape(slots)
    block_match = block_tab[:, None, None] == jnp.arange(KB_DEV, dtype=jnp.int32)[None, :, None]
    head_match = head_tab[:, None, None] == jnp.arange(KVH, dtype=jnp.int32)[None, None, :]
    chooser = block_match & head_match & live[:, None, None]
    chooser_half = chooser.astype(jnp.bfloat16)
    keys4 = keys.reshape(KB_DEV, BLK, KVH, HD)
    values4 = values.reshape(KB_DEV, BLK, KVH, HD)
    key_tiles = jnp.einsum(
        "sng,nbgd->sbd", chooser_half, keys4, preferred_element_type=jnp.float32
    ).astype(jnp.bfloat16)
    value_tiles = jnp.einsum(
        "sng,nbgd->sbd", chooser_half, values4, preferred_element_type=jnp.float32
    ).astype(jnp.bfloat16)
    got_keys, got_values = (
        lax.all_to_all(
            key_tiles.reshape(devices, capacity, BLK, HD),
            ("cx", "cy"),
            split_axis=0,
            concat_axis=0,
            tiled=True,
        ),
        lax.all_to_all(
            value_tiles.reshape(devices, capacity, BLK, HD),
            ("cx", "cy"),
            split_axis=0,
            concat_axis=0,
            tiled=True,
        ),
    )
    got_keys = got_keys.reshape(slots, BLK, HD)
    got_values = got_values.reshape(slots, BLK, HD)
    my_picks = lax.dynamic_slice_in_dim(picks_all, myself, 1, 0)[0]
    my_owner = my_picks // KB_DEV
    earlier = (my_owner[:, None] == my_owner[None, :]) & (positions[:, None] > positions[None, :])
    my_rank = jnp.sum(earlier.astype(jnp.int32), axis=1)
    my_slot = my_owner * capacity + my_rank
    pick_match = my_slot[:, None] == jnp.arange(slots, dtype=jnp.int32)[None, :]
    pick_half = pick_match.astype(jnp.bfloat16)
    pair_keys = (
        jnp.einsum("ps,sbd->pbd", pick_half, got_keys, preferred_element_type=jnp.float32)
        .astype(jnp.bfloat16)
        .reshape(QB_DEV, KVH, TOPK * BLK, HD)
    )
    pair_values = (
        jnp.einsum("ps,sbd->pbd", pick_half, got_values, preferred_element_type=jnp.float32)
        .astype(jnp.bfloat16)
        .reshape(QB_DEV, KVH, TOPK * BLK, HD)
    )
    q_blocks = queries.reshape(QB_DEV, BLK, KVH, GROUP, HD)
    o_blocks = d_out.reshape(QB_DEV, BLK, KVH, GROUP, HD)
    query_parts, key_parts, value_parts = ([], [], [])
    for block in range(QB_DEV):
        d_query, d_key, d_value = block_grads(
            q_blocks[block], o_blocks[block], pair_keys[block], pair_values[block]
        )
        query_parts.append(d_query)
        key_parts.append(d_key)
        value_parts.append(d_value)
    d_queries = jnp.stack(query_parts).reshape(QB_DEV * BLK, H * HD)
    pick_full = pick_match.astype(jnp.float32)
    key_terms = jnp.einsum(
        "ps,pbd->sbd", pick_full, jnp.stack(key_parts).reshape(PICKS, BLK, HD), precision=highest
    )
    value_terms = jnp.einsum(
        "ps,pbd->sbd", pick_full, jnp.stack(value_parts).reshape(PICKS, BLK, HD), precision=highest
    )
    back_keys, back_values = (
        lax.all_to_all(
            key_terms.reshape(devices, capacity, BLK, HD),
            ("cx", "cy"),
            split_axis=0,
            concat_axis=0,
            tiled=True,
        ),
        lax.all_to_all(
            value_terms.reshape(devices, capacity, BLK, HD),
            ("cx", "cy"),
            split_axis=0,
            concat_axis=0,
            tiled=True,
        ),
    )
    back_keys = back_keys.reshape(slots, BLK, HD)
    back_values = back_values.reshape(slots, BLK, HD)
    placement = chooser.astype(jnp.float32)
    d_keys = jnp.einsum("sng,sbd->nbgd", placement, back_keys, precision=highest).reshape(
        KB_DEV * BLK, KVH * HD
    )
    d_values = jnp.einsum("sng,sbd->nbgd", placement, back_values, precision=highest).reshape(
        KB_DEV * BLK, KVH * HD
    )
    return (d_queries, d_keys, d_values)


def solution(mesh):
    placed = (
        P(("cx", "cy"), None),
        P(("cx", "cy"), None),
        P(("cx", "cy"), None),
        P(("cx", "cy"), None),
        P(),
    )
    return jax.shard_map(
        body,
        mesh=mesh,
        in_specs=placed,
        out_specs=(P(("cx", "cy"), None), P(("cx", "cy"), None), P(("cx", "cy"), None)),
        check_vma=False,
    )
```

profile of v0, /device:TPU:3, one launch (start us, length us, event | category | flops | bytes accessed | tf_op | source)
XLA Modules:
  0.0 609.0 jit_solution(456576963429709534)
XLA Ops:
  0.6 0.9 copy.76
  1.9 0.6 fusion.123
  2.7 1.2 select_reduce_fusion.1
  4.0 1.3 reshape.279
  5.4 1.3 fusion.37
  6.8 3.2 copy.78
  9.9 6.5 %all-to-all-start = ((bf16[32,8,64,128]{3,1,2,0:T(8,128)(2,1)}), bf16[32,8,64,128]{3,1,2,0:T(8,128)(2,1)}, u32[]{:S(2)}, u32[]{:S(2)}) async-start(bf16[32,8,64,128]{3,1,2,0:T(8,128)(2,1)} %copy.78), calls=%async_computation | async-start | bytes 8388608 | tf_op jit(solution)/shard_map/all_to_all | solution.py:73
  16.7 1.3 fusion.38
  18.1 3.1 copy.83
  21.2 89.6 %all-to-all-done = bf16[32,8,64,128]{3,1,2,0:T(8,128)(2,1)} async-done(((bf16[32,8,64,128]{3,1,2,0:T(8,128)(2,1)}), bf16[32,8,64,128]{3,1,2,0:T(8,128)(2,1)}, u32[]{:S(2)}, u32[]{:S(2)}) %all-to-all-start) | async-done | bytes 4194336 | tf_op jit(solution)/shard_map/all_to_all | solution.py:73
  110.8 4.2 all-to-all-start.1
  115.2 0.9 copy.131
  116.1 0.9 copy.135
  117.0 0.9 copy.133
  118.0 0.9 copy.132
  119.0 0.9 copy.136
  119.9 0.9 copy.134
  121.0 3.2 fusion.54
  124.3 0.7 fusion.163
  125.0 0.7 copy.80
  125.7 0.7 copy.91
  126.4 0.7 copy.87
  127.1 7.4 %fusion.169 = (f32[4,8,64]{2,1,0:T(8,128)S(1)}, f32[4,8,64,1024]{3,2,1,0:T(8,128)}) fusion(bf16[4,1024,128,1]{2,1,3,0:T(8,128)(2,1)S(1)} %bitcast.270, bf16[64,4,8,128]{3,2,1,0:T(8,128)(2,1)} %bitcast.281), kind=kOutput, calls=%fused_computation.197 | convolution fusion | flops 543163392 | bytes 9969664 | tf_op jit(solution)/shard_map/sub | solution.py:22
  134.4 7.0 %fusion.164 = (f32[4,8,64]{2,1,0:T(8,128)S(1)}, f32[4,8,64,1024]{3,2,1,0:T(8,128)}) fusion(bf16[4,1024,128,1]{2,1,3,0:T(8,128)(2,1)S(1)} %bitcast.268, bf16[64,4,8,128]{3,2,1,0:T(8,128)(2,1)} %bitcast.277), kind=kOutput, calls=%fused_computation.196 | convolution fusion | flops 543163392 | bytes 9969664 | tf_op jit(solution)/shard_map/sub | solution.py:22
  141.4 7.3 %fusion.174 = (f32[4,8,64]{2,1,0:T(8,128)S(1)}, f32[4,8,64,1024]{3,2,1,0:T(8,128)}) fusion(bf16[4,1024,128,1]{2,1,3,0:T(8,128)(2,1)S(1)} %bitcast.266, bf16[64,4,8,128]{3,2,1,0:T(8,128)(2,1)} %bitcast.275), kind=kOutput, calls=%fused_computation.198 | convolution fusion | flops 543163392 | bytes 9969664 | tf_op jit(solution)/shard_map/sub | solution.py:22
  148.7 4.8 fusion.72
  153.6 1.0 copy-done.5
  154.6 2.4 fusion.75
  157.4 2.4 fusion.69
  160.2 11.6 %fusion.25 = f32[32,8,64,128]{3,1,2,0:T(8,128)} fusion(f32[192,64,128]{2,1,0:T(8,128)S(1)} %bitcast.255, s32[32,8]{1,0:T(8,128)S(1)} %multiply_add_fusion, s32[192]{0:T(256)S(1)} %multiply_add_fusion.1), kind=kOutput, calls=%fused_computation.41 | convolution fusion | flops 4831887360 | bytes 14681856 | tf_op jit(solution)/shard_map/ps,pbd->sbd/dot_general | solution.py:122
  171.8 37.7 %all-to-all-done.1 = bf16[32,8,64,128]{3,1,2,0:T(8,128)(2,1)} async-done(((bf16[32,8,64,128]{3,1,2,0:T(8,128)(2,1)}), bf16[32,8,64,128]{3,1,2,0:T(8,128)(2,1)}, u32[]{:S(2)}, u32[]{:S(2)}) %all-to-all-start.1) | async-done | bytes 4194336 | tf_op jit(solution)/shard_map/all_to_all | solution.py:80
  209.4 4.8 all-to-all-start.3
  214.2 3.4 fusion.57
  217.7 0.7 fusion.162
  218.4 1.7 copy.85
  220.0 1.6 copy.93
  221.7 0.7 copy.89
  222.4 2.2 fusion.12
  224.6 1.4 fusion.14
  226.0 4.7 fusion.61
  230.8 2.2 fusion.7
  232.9 1.4 fusion.9
  234.4 3.3 fusion.60
  237.7 2.2 fusion.17
  239.9 1.6 fusion.19
  241.5 2.0 copy-done.3
  243.5 1.7 fusion.62
  245.2 0.5 pad_maximum_fusion
  245.8 11.6 %fusion.27 = f32[32,8,64,128]{3,1,2,0:T(8,128)} fusion(f32[192,64,128]{2,1,0:T(8,128)S(1)} %bitcast.254, s32[32,8]{1,0:T(8,128)S(1)} %multiply_add_fusion, s32[192]{0:T(256)S(1)} %multiply_add_fusion.1), kind=kOutput, calls=%fused_computation.43 | convolution fusion | flops 4831887360 | bytes 14681856 | tf_op jit(solution)/shard_map/ps,pbd->sbd/dot_general | solution.py:119
  257.4 144.0 %all-to-all-done.3 = f32[32,8,64,128]{3,1,2,0:T(8,128)} async-done(((f32[32,8,64,128]{3,1,2,0:T(8,128)}), f32[32,8,64,128]{3,1,2,0:T(8,128)}, u32[]{:S(2)}, u32[]{:S(2)}) %all-to-all-start.3) | async-done | bytes 8388640 | tf_op jit(solution)/shard_map/all_to_all | solution.py:133
  401.4 3.6 all-to-all-start.2
  405.0 3.6 fusion.79
  408.6 1.3 fusion.78
  409.9 1.3 fusion.80
  411.4 1.8 copy.95
  413.2 2.5 reshape.285
  415.8 5.0 copy.107
  420.8 8.1 %fusion.66 = f32[16,64,4,128]{3,0,2,1:T(8,128)S(1)} fusion(f32[256,64,128,1]{2,1,0,3:T(8,128)S(1)} %bitcast.253, pred[256]{0:T(512)(128)(4,1)S(1)} %copy-done.28, pred[256,4]{0,1:T(4,128)(4,1)S(1)} %copy-done.26, pred[256,16]{0,1:T(8,128)(4,1)S(1)} %copy-done.24), kind=kOutput, calls=%fused_computation.79 | convolution fusion | flops 1610645504 | bytes 10491136 | tf_op jit(solution)/shard_map/sng,sbd->nbgd/dot_general | solution.py:147
  428.9 0.8 copy.109
  429.7 162.2 %all-to-all-done.2 = f32[32,8,64,128]{3,1,2,0:T(8,128)} async-done(((f32[32,8,64,128]{3,1,2,0:T(8,128)}), f32[32,8,64,128]{3,1,2,0:T(8,128)}, u32[]{:S(2)}, u32[]{:S(2)}) %all-to-all-start.2) | async-done | bytes 8388640 | tf_op jit(solution)/shard_map/all_to_all | solution.py:126
  591.9 5.0 copy.100
  596.9 8.3 %fusion.63 = f32[16,64,4,128]{3,0,2,1:T(8,128)S(1)} fusion(f32[256,64,128,1]{2,1,0,3:T(8,128)S(1)} %bitcast.252, pred[256]{0:T(512)(128)(4,1)S(1)} %copy-done.28, pred[256,4]{0,1:T(4,128)(4,1)S(1)} %copy-done.26, pred[256,16]{0,1:T(8,128)(4,1)S(1)} %copy-done.24), kind=kOutput, calls=%fused_computation.78 | convolution fusion | flops 1610645504 | bytes 10491136 | tf_op jit(solution)/shard_map/sng,sbd->nbgd/dot_general | solution.py:144
  605.3 0.8 copy.102
  606.1 2.5 copy_bitcast_fusion
  (96 shorter events, 2.5 us)
Async XLA Ops:
  2.6 14.1 %copy-start.27 = (pred[256]{0:T(512)(128)(4,1)}, pred[256]{0:T(512)(128)(4,1)S(1)}, u32[]{:S(2)}) copy-start(pred[256]{0:T(512)(128)(4,1)S(1)} %and.120) | copy-start | bytes 772
  4.0 12.7 %copy-start.25 = (pred[256,4]{0,1:T(4,128)(4,1)}, pred[256,4]{0,1:T(4,128)(4,1)S(1)}, u32[]{:S(2)}) copy-start(pred[256,4]{0,1:T(4,128)(4,1)S(1)} %iota_compare_fusion.6) | copy-start | bytes 3076
  4.0 12.7 %copy-start.23 = (pred[256,16]{0,1:T(8,128)(4,1)}, pred[256,16]{0,1:T(8,128)(4,1)S(1)}, u32[]{:S(2)}) copy-start(pred[256,16]{0,1:T(8,128)(4,1)S(1)} %iota_compare_fusion.5) | copy-start | bytes 12292
  6.8 9.6 %copy-start.13 = (bf16[1024,512]{1,0:T(8,128)(2,1)S(1)}, bf16[1024,512]{1,0:T(8,128)(2,1)}, u32[]{:S(2)}) copy-start(bf16[1024,512]{1,0:T(8,128)(2,1)} %param.7) | copy-start | bytes 3145732
  9.9 100.9 %all-to-all-start = ((bf16[32,8,64,128]{3,1,2,0:T(8,128)(2,1)}), bf16[32,8,64,128]{3,1,2,0:T(8,128)(2,1)}, u32[]{:S(2)}, u32[]{:S(2)}) async-start(bf16[32,8,64,128]{3,1,2,0:T(8,128)(2,1)} %copy.78), calls=%async_computation | async-start | bytes 8388608 | tf_op jit(solution)/shard_map/all_to_all | solution.py:73
  21.2 93.9 %copy-start.11 = (bf16[192,4096]{1,0:T(8,128)(2,1)S(1)}, bf16[192,4096]{1,0:T(8,128)(2,1)}, u32[]{:S(2)}) copy-start(bf16[192,4096]{1,0:T(8,128)(2,1)} %param.5) | copy-start | bytes 4718596
  21.2 96.7 %copy-start.12 = (bf16[192,4096]{1,0:T(8,128)(2,1)S(1)}, bf16[192,4096]{1,0:T(8,128)(2,1)}, u32[]{:S(2)}) copy-start(bf16[192,4096]{1,0:T(8,128)(2,1)} %param.8) | copy-start | bytes 4718596
  110.8 98.6 %all-to-all-start.1 = ((bf16[32,8,64,128]{3,1,2,0:T(8,128)(2,1)}), bf16[32,8,64,128]{3,1,2,0:T(8,128)(2,1)}, u32[]{:S(2)}, u32[]{:S(2)}) async-start(bf16[32,8,64,128]{3,1,2,0:T(8,128)(2,1)} %copy.83), calls=%async_computation.1 | async-start | bytes 8388608 | tf_op jit(solution)/shard_map/all_to_all | solution.py:80
  126.3 8.1 %copy-start.6 = (bf16[64,64,128]{2,1,0:T(8,128)(2,1)}, bf16[64,64,128]{2,1,0:T(8,128)(2,1)S(1)}, u32[]{:S(2)}) copy-start(bf16[64,64,128]{2,1,0:T(8,128)(2,1)S(1)} %copy.91) | copy-start | bytes 3145732
  127.0 14.4 %copy-start.8 = (bf16[64,64,128]{2,1,0:T(8,128)(2,1)}, bf16[64,64,128]{2,1,0:T(8,128)(2,1)S(1)}, u32[]{:S(2)}) copy-start(bf16[64,64,128]{2,1,0:T(8,128)(2,1)S(1)} %copy.87) | copy-start | bytes 3145732
  141.4 7.3 %copy-start.21 = (bf16[8,8,32,128]{3,2,1,0:T(8,128)(2,1)S(1)}, bf16[8,8,32,128]{3,2,1,0:T(8,128)(2,1)}, u32[]{:S(2)}) copy-start(bf16[8,8,32,128]{3,2,1,0:T(8,128)(2,1)} %copy.134) | copy-start | bytes 1572868
  148.7 5.8 copy-start.5
  148.7 5.9 copy-start.19
  148.7 8.3 %slice-start = ((s8[8388608]{0:T(1024)(128)(4,1)}), s8[4194304]{0:T(1024)(128)(4,1)S(1)}, s32[]{:S(2)}) async-start(s8[8388608]{0:T(1024)(128)(4,1)} %bitcast.256), calls=%async_computation.4 | async-start | bytes 8388608
  154.6 2.7 slice-start.1
  154.6 2.7 copy-start.17
  209.4 191.9 %all-to-all-start.3 = ((f32[32,8,64,128]{3,1,2,0:T(8,128)}), f32[32,8,64,128]{3,1,2,0:T(8,128)}, u32[]{:S(2)}, u32[]{:S(2)}) async-start(f32[32,8,64,128]{3,1,2,0:T(8,128)} %fusion.25), calls=%async_computation.3 | async-start | bytes 16777216 | tf_op jit(solution)/shard_map/all_to_all | solution.py:133
  214.2 8.1 %slice-start.6 = ((s8[8388608]{0:T(1024)(128)(4,1)}), s8[4194304]{0:T(1024)(128)(4,1)S(1)}, s32[]{:S(2)}) async-start(s8[8388608]{0:T(1024)(128)(4,1)} %bitcast.262), calls=%async_computation.10 | async-start | bytes 8388608
  217.6 4.7 slice-start.7
  217.6 4.7 copy-start.22
  220.0 10.7 %slice-start.4 = ((s8[8388608]{0:T(1024)(128)(4,1)}), s8[4194304]{0:T(1024)(128)(4,1)S(1)}, s32[]{:S(2)}) async-start(s8[8388608]{0:T(1024)(128)(4,1)} %bitcast.260), calls=%async_computation.8 | async-start | bytes 8388608
  222.4 8.3 %slice-start.5 = ((s8[8388608]{0:T(1024)(128)(4,1)}), s8[4194304]{0:T(1024)(128)(4,1)S(1)}, s32[]{:S(2)}) async-start(s8[8388608]{0:T(1024)(128)(4,1)} %bitcast.260), calls=%async_computation.9 | async-start | bytes 8388608
  226.0 6.9 %copy-start = (bf16[4,8,64,1024]{3,2,1,0:T(8,128)(2,1)}, bf16[4,8,64,1024]{3,2,1,0:T(8,128)(2,1)S(1)}, u32[]{:S(2)}) copy-start(bf16[4,8,64,1024]{3,2,1,0:T(8,128)(2,1)S(1)} %fusion.14) | copy-start | bytes 12582916
  226.0 4.7 copy-start.15
  226.0 4.7 copy-start.20
  226.0 11.7 %slice-start.2 = ((s8[8388608]{0:T(1024)(128)(4,1)}), s8[4194304]{0:T(1024)(128)(4,1)S(1)}, s32[]{:S(2)}) async-start(s8[8388608]{0:T(1024)(128)(4,1)} %bitcast.258), calls=%async_computation.6 | async-start | bytes 8388608
  230.7 7.0 %slice-start.3 = ((s8[8388608]{0:T(1024)(128)(4,1)}), s8[4194304]{0:T(1024)(128)(4,1)S(1)}, s32[]{:S(2)}) async-start(s8[8388608]{0:T(1024)(128)(4,1)} %bitcast.258), calls=%async_computation.7 | async-start | bytes 8388608
  234.4 5.5 copy-start.1
  234.4 3.3 copy-start.14
  234.4 3.3 copy-start.18
  239.9 3.6 copy-start.16
  241.5 2.0 copy-start.3
  243.5 1.8 copy-start.10
  257.4 147.6 %copy-start.9 = (bf16[64,64,128]{2,1,0:T(8,128)(2,1)S(1)}, bf16[64,64,128]{2,1,0:T(8,128)(2,1)}, u32[]{:S(2)}) copy-start(bf16[64,64,128]{2,1,0:T(8,128)(2,1)} %copy-done.8) | copy-start | bytes 3145732
  401.4 7.2 %copy-start.7 = (bf16[64,64,128]{2,1,0:T(8,128)(2,1)S(1)}, bf16[64,64,128]{2,1,0:T(8,128)(2,1)}, u32[]{:S(2)}) copy-start(bf16[64,64,128]{2,1,0:T(8,128)(2,1)} %copy-done.6) | copy-start | bytes 3145732
  401.4 190.5 %all-to-all-start.2 = ((f32[32,8,64,128]{3,1,2,0:T(8,128)}), f32[32,8,64,128]{3,1,2,0:T(8,128)}, u32[]{:S(2)}, u32[]{:S(2)}) async-start(f32[32,8,64,128]{3,1,2,0:T(8,128)} %fusion.27), calls=%async_computation.2 | async-start | bytes 16777216 | tf_op jit(solution)/shard_map/all_to_all | solution.py:126
  405.0 3.6 copy-start.2
  405.0 4.9 copy-start.4
  415.7 5.1 copy-start.24
  415.7 5.1 copy-start.26
  415.7 5.1 copy-start.28
where the time goes:
time: 615 us; the launch traced here: 609 us
  waiting for transfers between devices  433 us (70%)
  matrix products  103 us (17%)
  local copies, waits for them, and re-layouts  44.2 us (7%)
  starting transfers between devices  19 us (3%)
  other arithmetic  7.72 us (1%)
    all_to_all x1, waiting for transfers between devices, body(): lax.all_to_all(key_terms.reshape(devices, capacity, BLK, HD), ('cx', 'cy'...  162 us
    all_to_all x1, waiting for transfers between devices, body(): lax.all_to_all(value_terms.reshape(devices, capacity, BLK, HD), ('cx', 'c...  144 us
    all_to_all x1, waiting for transfers between devices, body(): lax.all_to_all(key_tiles.reshape(devices, capacity, BLK, HD), ('cx', 'cy'...  89.6 us
    all_to_all x1, waiting for transfers between devices, body(): lax.all_to_all(value_tiles.reshape(devices, capacity, BLK, HD), ('cx', 'c...  37.7 us
    sub x3, matrix products, block_grads(): probs = jax.nn.softmax(scores, axis=-1)  21.7 us
  transfers between devices with their start and end apart: 4, of which 4 were waited for; matrix products, arithmetic and copies ran while one was open for 21% of the time, Pallas kernels for 0%

commit v1 on v0

v1 whole, which is shorter than its diff:
```python
import functools

import jax
import jax.numpy as jnp
from jax import lax
from jax.experimental import pallas as pl
from jax.experimental.pallas import tpu as pltpu
from jax.sharding import PartitionSpec as P

H = 32
KVH = 4
HD = 128
BLK = 64
TOPK = 16
QB_DEV = 3
KB_DEV = 16
GROUP = 8
PICKS = 192
ROWS = GROUP * BLK
SPAN = TOPK * BLK
CHUNKS = 2
SCALE = HD ** (-0.5)
SMEM = pltpu.SMEM
VMEM = pltpu.VMEM
F32 = jnp.float32
BF16 = jnp.bfloat16


def params(**more):
    return pltpu.CompilerParams(vmem_limit_bytes=48 * 1024 * 1024, **more)


def tile_at(ref, code):
    row = pl.multiple_of(code // KVH * BLK, BLK)
    lane = pl.multiple_of(code % KVH * HD, HD)
    return ref.at[pl.ds(row, BLK), pl.ds(lane, HD)]


def pack_kernel(tab, shard, out):
    def step(slot, carry):
        code = tab[slot]

        @pl.when(code >= 0)
        def _():
            out[slot] = tile_at(shard, code)[...]

        return carry

    lax.fori_loop(0, tab.shape[0], step, 0)


def pack(tab, shard):
    slots = tab.shape[0]
    return pl.pallas_call(
        pack_kernel,
        out_shape=jax.ShapeDtypeStruct((slots, BLK, HD), shard.dtype),
        in_specs=[pl.BlockSpec(memory_space=SMEM), pl.BlockSpec(memory_space=VMEM)],
        out_specs=pl.BlockSpec(memory_space=VMEM),
        compiler_params=params(),
        cost_estimate=pl.CostEstimate(flops=2_000_000, bytes_accessed=4 * slots * BLK * HD, transcendentals=0),
        name="pack",
    )(tab, shard)


def add_slots(tab, slots, acc):
    def step(slot, carry):
        code = tab[slot]

        @pl.when(code >= 0)
        def _():
            spot = tile_at(acc, code)
            spot[...] += slots[slot].astype(F32)

        return carry

    lax.fori_loop(0, tab.shape[0], step, 0)


def relay_kernel(tab, slots, out, acc):
    acc[...] = jnp.zeros_like(acc)
    add_slots(tab, slots, acc)
    out[...] = acc[...].astype(out.dtype)


def relay(tab, slots):
    shape = (KB_DEV * BLK, KVH * HD)
    return pl.pallas_call(
        relay_kernel,
        out_shape=jax.ShapeDtypeStruct(shape, BF16),
        in_specs=[pl.BlockSpec(memory_space=SMEM), pl.BlockSpec(memory_space=VMEM)],
        out_specs=pl.BlockSpec(memory_space=VMEM),
        scratch_shapes=[VMEM(shape, F32)],
        compiler_params=params(),
        cost_estimate=pl.CostEstimate(flops=4_000_000, bytes_accessed=4 * slots.size, transcendentals=0),
        name="relay",
    )(tab, slots)


def own_kernel(tab, slots, other, out):
    out[...] = other[...].astype(F32)
    add_slots(tab, slots, out)


def own_sum(tab, slots, other):
    return pl.pallas_call(
        own_kernel,
        out_shape=jax.ShapeDtypeStruct(other.shape, F32),
        in_specs=[
            pl.BlockSpec(memory_space=SMEM),
            pl.BlockSpec(memory_space=VMEM),
            pl.BlockSpec(memory_space=VMEM),
        ],
        out_specs=pl.BlockSpec(memory_space=VMEM),
        compiler_params=params(),
        cost_estimate=pl.CostEstimate(flops=4_000_000, bytes_accessed=4 * slots.size, transcendentals=0),
        name="own_sum",
    )(tab, slots, other)


def load_slots(hbm_pair, dest, sems):
    size = hbm_pair[0].shape[0]
    copies = [
        pltpu.make_async_copy(hbm_pair[side], dest.at[pl.ds(side * size, size)], sems.at[side])
        for side in (0, 1)
    ]
    for copy in copies:
        copy.start()
    return copies


def gather_tiles(idx, base, table, dest):
    for pick in range(TOPK):
        dest[pick * BLK : (pick + 1) * BLK, :] = table[idx[base + pick]]


def store_tiles(idx, base, tiles, here, there):
    size = here.shape[0]
    for pick in range(TOPK):
        spot = idx[base + pick]
        tile = tiles[pick * BLK : (pick + 1) * BLK, :].astype(BF16)

        @pl.when(spot < size)
        def _():
            here[spot] = tile

        @pl.when(spot >= size)
        def _():
            there[spot - size] = tile


def heads(ref, chunk):
    per = GROUP // CHUNKS
    return jnp.concatenate(
        [ref[:, (chunk * per + z) * HD : (chunk * per + z + 1) * HD] for z in range(per)], axis=0
    )


def dot_nt(a, b):
    return lax.dot_general(a, b, (((1,), (1,)), ((), ())), preferred_element_type=F32)


def dot_nn(a, b):
    return lax.dot_general(a, b, (((1,), (0,)), ((), ())), preferred_element_type=F32)


def first_kernel(idx, q_ref, o_ref, k_here, k_there, dv_here, dv_there, stats, k_all, k_rows, acc, sems):
    task = pl.program_id(0) * KVH + pl.program_id(1)
    base = task * TOPK

    @pl.when(task == 0)
    def _():
        for copy in load_slots((k_here, k_there), k_all, sems):
            copy.wait()

    gather_tiles(idx, base, k_all, k_rows)
    width = ROWS // CHUNKS
    for chunk in range(CHUNKS):
        scores = dot_nt(k_rows[...], heads(q_ref, chunk)) * SCALE
        top = jnp.max(scores, axis=0, keepdims=True)
        weights = jnp.exp(scores - top)
        inverse = 1.0 / jnp.sum(weights, axis=0, keepdims=True)
        probs_half = (weights * inverse).astype(BF16)
        lanes = slice(chunk * width, (chunk + 1) * width)
        stats[0, 0:1, lanes] = top
        stats[0, 1:2, lanes] = inverse
        part = dot_nn(probs_half, heads(o_ref, chunk))
        if chunk == 0:
            acc[...] = part
        else:
            acc[...] += part
    store_tiles(idx, base, acc, dv_here, dv_there)


def task_specs():
    return [
        pl.BlockSpec((BLK, GROUP * HD), lambda r, g: (r, g)),
        pl.BlockSpec((BLK, GROUP * HD), lambda r, g: (r, g)),
    ]


def first(idx, queries, d_out, k_here, k_there):
    slots = k_here.shape[0]
    whole = pl.BlockSpec((slots, BLK, HD), lambda r, g: (0, 0, 0))
    flops = 4 * QB_DEV * KVH * ROWS * SPAN * HD
    return pl.pallas_call(
        first_kernel,
        grid=(QB_DEV, KVH),
        out_shape=(
            jax.ShapeDtypeStruct((slots, BLK, HD), BF16),
            jax.ShapeDtypeStruct((slots, BLK, HD), BF16),
            jax.ShapeDtypeStruct((QB_DEV * KVH, 8, ROWS), F32),
        ),
        in_specs=[pl.BlockSpec(memory_space=SMEM)]
        + task_specs()
        + [pl.BlockSpec(memory_space=pl.ANY), pl.BlockSpec(memory_space=pl.ANY)],
        out_specs=(whole, whole, pl.BlockSpec((1, 8, ROWS), lambda r, g: (r * KVH + g, 0, 0))),
        scratch_shapes=[
            VMEM((2 * slots, BLK, HD), BF16),
            VMEM((SPAN, HD), BF16),
            VMEM((SPAN, HD), F32),
            pltpu.SemaphoreType.DMA((2,)),
        ],
        compiler_params=params(dimension_semantics=("arbitrary", "arbitrary")),
        cost_estimate=pl.CostEstimate(
            flops=flops, bytes_accessed=8 * slots * BLK * HD, transcendentals=QB_DEV * KVH * ROWS * SPAN
        ),
        name="first",
    )(idx, queries, d_out, k_here, k_there)


def second_kernel(
    idx, q_ref, o_ref, stats, k_here, k_there, v_here, v_there, dk_here, dk_there, dq_ref,
    k_all, v_all, k_rows, v_rows, acc, sems_k, sems_v,
):
    task = pl.program_id(0) * KVH + pl.program_id(1)
    base = task * TOPK

    @pl.when(task == 0)
    def _():
        copies = load_slots((k_here, k_there), k_all, sems_k) + load_slots((v_here, v_there), v_all, sems_v)
        for copy in copies:
            copy.wait()

    gather_tiles(idx, base, k_all, k_rows)
    gather_tiles(idx, base, v_all, v_rows)
    keys_t = k_rows[...].T
    width = ROWS // CHUNKS
    per = GROUP // CHUNKS
    for chunk in range(CHUNKS):
        q = heads(q_ref, chunk)
        o = heads(o_ref, chunk)
        lanes = slice(chunk * width, (chunk + 1) * width)
        scores = dot_nt(k_rows[...], q) * SCALE
        probs = jnp.exp(scores - stats[0, 0:1, lanes]) * stats[0, 1:2, lanes]
        d_probs = dot_nt(v_rows[...], o)
        delta = jnp.sum(probs * d_probs, axis=0, keepdims=True)
        d_scores = (probs * (d_probs - delta)).astype(BF16)
        part = dot_nn(d_scores, q)
        if chunk == 0:
            acc[...] = part
        else:
            acc[...] += part
        d_query = dot_nn(keys_t, d_scores).T * SCALE
        for z in range(per):
            head = chunk * per + z
            dq_ref[:, head * HD : (head + 1) * HD] = d_query[z * BLK : (z + 1) * BLK, :]
    acc[...] = acc[...] * SCALE
    store_tiles(idx, base, acc, dk_here, dk_there)


def second(idx, queries, d_out, stats, k_here, k_there, v_here, v_there):
    slots = k_here.shape[0]
    whole = pl.BlockSpec((slots, BLK, HD), lambda r, g: (0, 0, 0))
    flops = 8 * QB_DEV * KVH * ROWS * SPAN * HD
    return pl.pallas_call(
        second_kernel,
        grid=(QB_DEV, KVH),
        out_shape=(
            jax.ShapeDtypeStruct((slots, BLK, HD), BF16),
            jax.ShapeDtypeStruct((slots, BLK, HD), BF16),
            jax.ShapeDtypeStruct(queries.shape, F32),
        ),
        in_specs=[pl.BlockSpec(memory_space=SMEM)]
        + task_specs()
        + [pl.BlockSpec((1, 8, ROWS), lambda r, g: (r * KVH + g, 0, 0))]
        + [pl.BlockSpec(memory_space=pl.ANY)] * 4,
        out_specs=(whole, whole, pl.BlockSpec((BLK, GROUP * HD), lambda r, g: (r, g))),
        scratch_shapes=[
            VMEM((2 * slots, BLK, HD), BF16),
            VMEM((2 * slots, BLK, HD), BF16),
            VMEM((SPAN, HD), BF16),
            VMEM((SPAN, HD), BF16),
            VMEM((SPAN, HD), F32),
            pltpu.SemaphoreType.DMA((2,)),
            pltpu.SemaphoreType.DMA((2,)),
        ],
        compiler_params=params(dimension_semantics=("arbitrary", "arbitrary")),
        cost_estimate=pl.CostEstimate(
            flops=flops, bytes_accessed=16 * slots * BLK * HD, transcendentals=QB_DEV * KVH * ROWS * SPAN
        ),
        name="second",
    )(idx, queries, d_out, stats, k_here, k_there, v_here, v_there)


def tables(selection, outer, inner, capacity, row, column):
    devices = outer * inner
    near = inner // 2
    half, place = column // near, column % near
    picks = selection.reshape(outer, 2, near, PICKS)
    mates = lax.dynamic_index_in_dim(picks, half, 1, keepdims=False).reshape(outer * near, PICKS)
    owners = row * inner + jnp.stack([half, 1 - half]) * near + place
    head = jnp.arange(PICKS, dtype=jnp.int32) // TOPK % KVH
    mine = mates[None] // KB_DEV == owners[:, None, None]
    positions = jnp.arange(PICKS, dtype=jnp.int32)
    before = (positions[:, None] < positions[None, :]).astype(BF16)
    ranks = jnp.dot(mine.astype(BF16), before, preferred_element_type=F32).astype(jnp.int32)
    copies = jnp.arange(capacity, dtype=jnp.int32)
    match = mine[:, :, None, :] & (ranks[:, :, None, :] == copies[None, None, :, None])
    codes = (mates % KB_DEV) * KVH + head[None] + 1
    tabs = jnp.sum(jnp.where(match, codes[None, :, None, :], 0), axis=3) - 1
    tabs = tabs.reshape(2, outer * near * capacity)
    myself = row * inner + column
    my_picks = lax.dynamic_index_in_dim(selection.reshape(devices, PICKS), myself, 0, keepdims=False)
    owner = my_picks // KB_DEV
    earlier = (owner[:, None] == owner[None, :]) & (positions[:, None] > positions[None, :])
    rank = jnp.sum(earlier.astype(jnp.int32), axis=1)
    across = (owner % inner // near != half).astype(jnp.int32)
    mate = owner // inner * near + owner % near
    slot = (across * outer * near + mate) * capacity + rank
    return tabs[0], tabs[1], slot


def body(queries, keys, values, d_out, selection):
    outer = lax.axis_size("cx")
    inner = lax.axis_size("cy")
    devices = outer * inner
    usable = devices * (KB_DEV - QB_DEV) // KB_DEV
    capacity = (PICKS + usable - 1) // usable
    near = inner // 2
    mates = outer * near
    tab_own, tab_far, slot = tables(
        selection, outer, inner, capacity, lax.axis_index("cx"), lax.axis_index("cy")
    )
    groups = [
        [a * inner + half * near + b for a in range(outer) for b in range(near)] for half in (0, 1)
    ]

    def across(x):
        return lax.ppermute(x, "cy", [(i, (i + near) % inner) for i in range(inner)])

    def among(x):
        y = lax.all_to_all(
            x.reshape(mates, capacity * BLK, HD),
            ("cx", "cy"),
            split_axis=0,
            concat_axis=0,
            tiled=True,
            axis_index_groups=groups,
        )
        return y.reshape(x.shape)

    far_keys = across(keys)
    k_here = among(pack(tab_own, keys))
    far_keys, values_next = lax.optimization_barrier((far_keys, values))
    far_values = across(values_next)
    k_there = among(pack(tab_far, far_keys))
    v_here = among(pack(tab_own, values))
    v_there = among(pack(tab_far, far_values))
    dv_here, dv_there, stats = first(slot, queries, d_out, k_here, k_there)
    dv_far = across(relay(tab_far, among(dv_there)))
    dv_near = among(dv_here)
    dk_here, dk_there, d_queries = second(slot, queries, d_out, stats, k_here, k_there, v_here, v_there)
    dk_far = across(relay(tab_far, among(dk_there)))
    dk_near = among(dk_here)
    d_values = own_sum(tab_own, dv_near, dv_far)
    d_keys = own_sum(tab_own, dk_near, dk_far)
    return (d_queries, d_keys, d_values)


def solution(mesh):
    placed = (
        P(("cx", "cy"), None),
        P(("cx", "cy"), None),
        P(("cx", "cy"), None),
        P(("cx", "cy"), None),
        P(),
    )
    return jax.shard_map(
        body,
        mesh=mesh,
        in_specs=placed,
        out_specs=(P(("cx", "cy"), None), P(("cx", "cy"), None), P(("cx", "cy"), None)),
        check_vma=False,
    )
```

time: 615 us -> 407 us (0.66)
  waiting for transfers between devices: 433 us -> 189 us
  matrix products: 103 us -> 0.14 us
  Pallas kernels: 0 us -> 94.4 us
  blocking collectives: 0 us -> 60.8 us
  local copies, waits for them, and re-layouts: 44.2 us -> 12.1 us
  starting transfers between devices: 19 us -> 45.6 us
  other arithmetic: 7.72 us -> 1.07 us
    all_to_all x4 -> x6, waiting for transfers between devices: 433 us -> 21 us  [among(): lax.all_to_all(x.reshape(mates, capacity * BLK, HD), ('cx', 'cy'), split_...]
    ppermute x0 -> x4, waiting for transfers between devices: none -> 168 us  [across(): lax.ppermute(x, 'cy', [(i, (i + near) % inner) for i in range(inner)])]
    pallas_call x0 -> x10, Pallas kernels: none -> 94.4 us  [the longest x1 30 us: second(): pl.pallas_call(second_kernel, grid=(QB_DEV, KVH), out_shape=(jax.ShapeDty...]
    dot_general x21 -> x1, matrix products: 81 us -> 0.14 us  [tables(): jnp.dot(mine.astype(BF16), before, preferred_element_type=F32)]
    all_to_all x0 -> x2, blocking collectives: none -> 60.8 us  [among(): lax.all_to_all(x.reshape(mates, capacity * BLK, HD), ('cx', 'cy'), split_...]
    sub x3 -> x0, matrix products: 21.7 us -> none  [block_grads(): probs = jax.nn.softmax(scores, axis=-1)]
    all_to_all x4 -> x6, starting transfers between devices: 19 us -> 38.9 us  [among(): lax.all_to_all(x.reshape(mates, capacity * BLK, HD), ('cx', 'cy'), split_...]
    reshape x7 -> x2, local copies, waits for them, and re-layouts: 13 us -> 0.3 us  [the longest x1 0.16 us: tables(): picks = selection.reshape(outer, 2, near, PICKS)]
  transfers between devices with their start and end apart: 4 -> 10, of which waited for: 4 -> 5; matrix products, arithmetic and copies ran while one was open for 21% -> 0% of each run, Pallas kernels for 0% -> 21%
where the time goes in v1:
time: 407 us; the launch traced here: 404 us
  waiting for transfers between devices  189 us (46%)
  Pallas kernels  94.4 us (23%)
  blocking collectives  60.8 us (15%)
  starting transfers between devices  45.6 us (11%)
  local copies, waits for them, and re-layouts  12.1 us (3%)
    ppermute x4, waiting for transfers between devices, across(): lax.ppermute(x, 'cy', [(i, (i + near) % inner) for i in range(inner)])  168 us
    all_to_all x2, blocking collectives, among(): lax.all_to_all(x.reshape(mates, capacity * BLK, HD), ('cx', 'cy'), split_...  60.8 us
    all_to_all x6, starting transfers between devices, among(): lax.all_to_all(x.reshape(mates, capacity * BLK, HD), ('cx', 'cy'), split_...  38.9 us
    pallas_call x1, Pallas kernels, second(): pl.pallas_call(second_kernel, grid=(QB_DEV, KVH), out_shape=(jax.ShapeDty...  30 us
    pallas_call x1, Pallas kernels, first(): pl.pallas_call(first_kernel, grid=(QB_DEV, KVH), out_shape=(jax.ShapeDtyp...  24.2 us
    all_to_all x6, waiting for transfers between devices, among(): lax.all_to_all(x.reshape(mates, capacity * BLK, HD), ('cx', 'cy'), split_...  21 us
    pallas_call x4, Pallas kernels, pack(): pl.pallas_call(pack_kernel, out_shape=jax.ShapeDtypeStruct((slots, BLK, H...  19.2 us
    pallas_call x2, Pallas kernels, own_sum(): pl.pallas_call(own_kernel, out_shape=jax.ShapeDtypeStruct(other.shape, F3...  11.8 us
  transfers between devices with their start and end apart: 10, of which 5 were waited for; matrix products, arithmetic and copies ran while one was open for 0% of the time, Pallas kernels for 21%

profile of v1, /device:TPU:3, one launch (start us, length us, event | category | flops | bytes accessed | tf_op | source)
XLA Modules:
  0.0 403.8 jit_solution(11092672275106268941)
XLA Ops:
  0.7 0.9 copy.10
  1.6 0.2 reshape.239
  1.8 0.1 fusion.14
  1.9 0.1 broadcast_compare_fusion
  2.0 0.1 convolution_convert_fusion
  2.1 0.6 select_reduce_fusion
  2.8 0.1 squeeze.13.tab
  2.8 0.0 copy-start.4
  2.9 1.2 copy-done.4
  4.1 4.8 %pack.6 = bf16[128,64,128]{2,1,0:T(8,128)(2,1)} custom-call(s32[128]{0:T(128)S(1)} %squeeze.13.tab, bf16[1024,512]{1,0:T(8,128)(2,1)S(1)} %copy-done.4), custom_call_target="tpu_custom_call" | custom-call | flops 2000000 | bytes 4194304 | tf_op jit(solution)/shard_map/pack/pallas_call | solution.py:54
  8.9 0.0 copy-start.3
  8.9 5.6 %all-to-all-start.2 = ((bf16[16,512,128]{2,1,0:T(8,128)(2,1)}), bf16[16,512,128]{2,1,0:T(8,128)(2,1)S(1)}, u32[]{:S(2)}, u32[]{:S(2)}) async-start(bf16[16,512,128]{2,1,0:T(8,128)(2,1)} %bitcast.9), calls=%async_computation.2 | async-start | bytes 4194304 | tf_op jit(solution)/shard_map/all_to_all | solution.py:352
  14.5 0.0 copy-done.3
  14.5 4.8 %pack.4 = bf16[128,64,128]{2,1,0:T(8,128)(2,1)} custom-call(s32[128]{0:T(128)S(1)} %squeeze.13.tab, bf16[1024,512]{1,0:T(8,128)(2,1)S(1)} %copy-done.3), custom_call_target="tpu_custom_call" | custom-call | flops 2000000 | bytes 4194304 | tf_op jit(solution)/shard_map/pack/pallas_call | solution.py:54
  19.3 20.9 %all-to-all-done.2 = bf16[16,512,128]{2,1,0:T(8,128)(2,1)S(1)} async-done(((bf16[16,512,128]{2,1,0:T(8,128)(2,1)}), bf16[16,512,128]{2,1,0:T(8,128)(2,1)S(1)}, u32[]{:S(2)}, u32[]{:S(2)}) %all-to-all-start.2) | async-done | bytes 2097184 | tf_op jit(solution)/shard_map/all_to_all | solution.py:352
  40.2 1.4 copy-done.10
  41.6 5.8 %all-to-all-start = ((bf16[16,512,128]{2,1,0:T(8,128)(2,1)}), bf16[16,512,128]{2,1,0:T(8,128)(2,1)}, u32[]{:S(2)}, u32[]{:S(2)}) async-start(bf16[16,512,128]{2,1,0:T(8,128)(2,1)} %bitcast.5), calls=%async_computation | async-start | bytes 4194304 | tf_op jit(solution)/shard_map/all_to_all | solution.py:352
  47.4 2.3 collective-permute-start
  49.7 0.1 squeeze.14.tab
  49.8 43.2 %collective-permute-done.shard = bf16[1024,512]{1,0:T(8,128)(2,1)S(1)} collective-permute-done((bf16[1024,512]{1,0:T(8,128)(2,1)S(1)}, bf16[1024,512]{1,0:T(8,128)(2,1)S(1)}, u32[]{:S(2)}, u32[]{:S(2)}) %collective-permute-start) | collective-permute-done | bytes 1048608 | tf_op jit(solution)/shard_map/ppermute | solution.py:349
  93.0 4.8 %pack.5 = bf16[128,64,128]{2,1,0:T(8,128)(2,1)} custom-call(s32[128]{0:T(128)S(1)} %squeeze.14.tab, bf16[1024,512]{1,0:T(8,128)(2,1)S(1)} %collective-permute-done.shard), custom_call_target="tpu_custom_call" | custom-call | flops 2000000 | bytes 4194304 | tf_op jit(solution)/shard_map/pack/pallas_call | solution.py:54
  97.8 0.0 all-to-all-done
  97.8 0.0 copy-start.5
  97.8 8.7 %all-to-all-start.1 = ((bf16[16,512,128]{2,1,0:T(8,128)(2,1)}), bf16[16,512,128]{2,1,0:T(8,128)(2,1)S(1)}, u32[]{:S(2)}, u32[]{:S(2)}) async-start(bf16[16,512,128]{2,1,0:T(8,128)(2,1)} %bitcast.7), calls=%async_computation.1 | async-start | bytes 4194304 | tf_op jit(solution)/shard_map/all_to_all | solution.py:352
  106.5 0.0 copy-done.5
  106.5 1.9 collective-permute-start.1
  108.4 43.6 %collective-permute-done.1.shard = bf16[1024,512]{1,0:T(8,128)(2,1)S(1)} collective-permute-done((bf16[1024,512]{1,0:T(8,128)(2,1)S(1)}, bf16[1024,512]{1,0:T(8,128)(2,1)S(1)}, u32[]{:S(2)}, u32[]{:S(2)}) %collective-permute-start.1) | collective-permute-done | bytes 1048608 | tf_op jit(solution)/shard_map/ppermute | solution.py:349
  152.0 4.8 %pack.7 = bf16[128,64,128]{2,1,0:T(8,128)(2,1)} custom-call(s32[128]{0:T(128)S(1)} %squeeze.14.tab, bf16[1024,512]{1,0:T(8,128)(2,1)S(1)} %collective-permute-done.1.shard), custom_call_target="tpu_custom_call" | custom-call | flops 2000000 | bytes 4194304 | tf_op jit(solution)/shard_map/pack/pallas_call | solution.py:54
  156.8 0.0 all-to-all-done.1
  156.8 0.0 copy-start.11
  156.8 1.3 copy-done.11
  158.1 0.0 copy-start.6
  158.1 8.2 %all-to-all-start.3 = ((bf16[16,512,128]{2,1,0:T(8,128)(2,1)}), bf16[16,512,128]{2,1,0:T(8,128)(2,1)}, u32[]{:S(2)}, u32[]{:S(2)}) async-start(bf16[16,512,128]{2,1,0:T(8,128)(2,1)} %bitcast.11), calls=%async_computation.3 | async-start | bytes 4194304 | tf_op jit(solution)/shard_map/all_to_all | solution.py:352
  166.3 0.1 reshape.238
  166.5 0.2 convert_reduce_fusion
  166.7 0.0 copy-done.6
  166.7 0.0 copy-start.8
  166.8 1.4 copy-done.8
  168.2 24.2 %first.1 = (bf16[128,64,128]{2,1,0:T(8,128)(2,1)S(1)}, bf16[128,64,128]{2,1,0:T(8,128)(2,1)}, f32[12,8,512]{2,1,0:T(8,128)S(1)}) custom-call(s32[192]{0:T(256)S(1)} %multiply_add_fusion.idx, bf16[192,4096]{1,0:T(8,128)(2,1)S(1)} %copy-done.6, bf16[192,4096]{1,0:T(8,128)(2,1)S(1)} %copy-done.8, bf16[128,64,128]{2,1,0:T(8,128)(2,1)} %bitcast.6.k_here, ...), custom_call_target="tpu_custom_call" | custom-call | flops 3221225472 | bytes 8388608 | tf_op jit(solution)/shard_map/first/pallas_call | solution.py:205
  192.3 0.0 copy-start.2
  192.3 1.3 copy-done.2
  193.7 0.0 all-to-all-done.3
  193.7 30.3 %all_to_all.40 = bf16[16,512,128]{2,1,0:T(8,128)(2,1)S(1)} all-to-all(bf16[16,512,128]{2,1,0:T(8,128)(2,1)} %bitcast.27), channel_id=1, replica_groups={{0,1,2,3,8,9,10,11,16,17,18,19,24,25,26,27},{4,5,6,7,12,13,14,15,20,21,..., dimensions={0} | all-to-all | bytes 4194304 | tf_op jit(solution)/shard_map/all_to_all | solution.py:352
  224.0 5.3 %all-to-all-start.7 = ((bf16[16,512,128]{2,1,0:T(8,128)(2,1)}), bf16[16,512,128]{2,1,0:T(8,128)(2,1)}, u32[]{:S(2)}, u32[]{:S(2)}) async-start(bf16[16,512,128]{2,1,0:T(8,128)(2,1)} %bitcast.31), calls=%async_computation.7 | async-start | bytes 4194304 | tf_op jit(solution)/shard_map/all_to_all | solution.py:352
  229.3 1.4 copy-done.7
  230.7 0.0 copy-start.9
  230.7 1.4 copy-done.9
  232.1 30.0 %second.1 = (bf16[128,64,128]{2,1,0:T(8,128)(2,1)S(1)}, bf16[128,64,128]{2,1,0:T(8,128)(2,1)}, f32[192,4096]{1,0:T(8,128)}) custom-call(s32[192]{0:T(256)S(1)} %multiply_add_fusion.idx, bf16[192,4096]{1,0:T(8,128)(2,1)S(1)} %copy-done.7, bf16[192,4096]{1,0:T(8,128)(2,1)S(1)} %copy-done.9, f32[12,8,512]{2,1,0:T(8,128)S(1)} %get-tuple-element.12.stats, ...), custom_call_target="tpu_custom_call" | custom-call | flops 6442450944 | bytes 16777216 | tf_op jit(solution)/shard_map/second/pallas_call | solution.py:275
  262.1 0.0 copy-start.1
  262.1 1.3 copy-done.1
  263.4 0.0 all-to-all-done.7
  263.4 30.5 %all_to_all.41 = bf16[16,512,128]{2,1,0:T(8,128)(2,1)} all-to-all(bf16[16,512,128]{2,1,0:T(8,128)(2,1)} %bitcast.32), channel_id=1, replica_groups={{0,1,2,3,8,9,10,11,16,17,18,19,24,25,26,27},{4,5,6,7,12,13,14,15,20,21,..., dimensions={0} | all-to-all | bytes 4194304 | tf_op jit(solution)/shard_map/all_to_all | solution.py:352
  293.9 5.3 %all-to-all-start.4 = ((bf16[16,512,128]{2,1,0:T(8,128)(2,1)}), bf16[16,512,128]{2,1,0:T(8,128)(2,1)}, u32[]{:S(2)}, u32[]{:S(2)}) async-start(bf16[16,512,128]{2,1,0:T(8,128)(2,1)} %bitcast.26), calls=%async_computation.4 | async-start | bytes 4194304 | tf_op jit(solution)/shard_map/all_to_all | solution.py:352
  299.2 0.0 copy-start
  299.2 5.2 %relay.3 = bf16[1024,512]{1,0:T(8,128)(2,1)S(1)} custom-call(s32[128]{0:T(128)S(1)} %squeeze.14.tab, bf16[128,64,128]{2,1,0:T(8,128)(2,1)} %bitcast.20.slots), custom_call_target="tpu_custom_call" | custom-call | flops 4000000 | bytes 4194304 | tf_op jit(solution)/shard_map/relay/pallas_call | solution.py:87
  304.4 2.0 collective-permute-start.3
  306.4 0.0 copy-done
  306.4 4.0 relay.2
  310.4 0.5 collective-permute-start.2
  310.9 63.7 %collective-permute-done.3.other = bf16[1024,512]{1,0:T(8,128)(2,1)S(1)} collective-permute-done((bf16[1024,512]{1,0:T(8,128)(2,1)S(1)}, bf16[1024,512]{1,0:T(8,128)(2,1)S(1)}, u32[]{:S(2)}, u32[]{:S(2)}) %collective-permute-start.3) | collective-permute-done | bytes 1048608 | tf_op jit(solution)/shard_map/ppermute | solution.py:349
  374.7 5.3 %own_sum.3 = f32[1024,512]{1,0:T(8,128)} custom-call(s32[128]{0:T(128)S(1)} %squeeze.13.tab, bf16[128,64,128]{2,1,0:T(8,128)(2,1)S(1)} %bitcast.24, bf16[1024,512]{1,0:T(8,128)(2,1)S(1)} %collective-permute-done.3.other), custom_call_target="tpu_custom_call" | custom-call | flops 4000000 | bytes 4194304 | tf_op jit(solution)/shard_map/own_sum/pallas_call | solution.py:105
  379.9 0.0 all-to-all-done.4
  379.9 17.3 %collective-permute-done.2.other = bf16[1024,512]{1,0:T(8,128)(2,1)} collective-permute-done((bf16[1024,512]{1,0:T(8,128)(2,1)S(1)}, bf16[1024,512]{1,0:T(8,128)(2,1)}, u32[]{:S(2)}, u32[]{:S(2)}) %collective-permute-start.2) | collective-permute-done | bytes 1048608 | tf_op jit(solution)/shard_map/ppermute | solution.py:349
  397.2 6.6 %own_sum.2 = f32[1024,512]{1,0:T(8,128)} custom-call(s32[128]{0:T(128)S(1)} %squeeze.13.tab, bf16[128,64,128]{2,1,0:T(8,128)(2,1)} %bitcast.14.slots, bf16[1024,512]{1,0:T(8,128)(2,1)} %collective-permute-done.2.other), custom_call_target="tpu_custom_call" | custom-call | flops 4000000 | bytes 4194304 | tf_op jit(solution)/shard_map/own_sum/pallas_call | solution.py:105
  (11 shorter events, 0.1 us)
Async XLA Ops:
  2.8 1.2 copy-start.4
  8.9 5.6 %copy-start.3 = (bf16[1024,512]{1,0:T(8,128)(2,1)S(1)}, bf16[1024,512]{1,0:T(8,128)(2,1)}, u32[]{:S(2)}) copy-start(bf16[1024,512]{1,0:T(8,128)(2,1)} %shard.2) | copy-start | bytes 3145732
  8.9 31.4 %all-to-all-start.2 = ((bf16[16,512,128]{2,1,0:T(8,128)(2,1)}), bf16[16,512,128]{2,1,0:T(8,128)(2,1)S(1)}, u32[]{:S(2)}, u32[]{:S(2)}) async-start(bf16[16,512,128]{2,1,0:T(8,128)(2,1)} %bitcast.9), calls=%async_computation.2 | async-start | bytes 4194304 | tf_op jit(solution)/shard_map/all_to_all | solution.py:352
  40.2 1.4 copy-start.10
  41.6 56.1 %all-to-all-start = ((bf16[16,512,128]{2,1,0:T(8,128)(2,1)}), bf16[16,512,128]{2,1,0:T(8,128)(2,1)}, u32[]{:S(2)}, u32[]{:S(2)}) async-start(bf16[16,512,128]{2,1,0:T(8,128)(2,1)} %bitcast.5), calls=%async_computation | async-start | bytes 4194304 | tf_op jit(solution)/shard_map/all_to_all | solution.py:352
  47.4 45.6 %collective-permute-start = (bf16[1024,512]{1,0:T(8,128)(2,1)S(1)}, bf16[1024,512]{1,0:T(8,128)(2,1)S(1)}, u32[]{:S(2)}, u32[]{:S(2)}) collective-permute-start(bf16[1024,512]{1,0:T(8,128)(2,1)S(1)} %copy-done.3), channel_id=1, source_target_pairs={{0,4},{1,5},{2,6},{3,7},{4,0},{5,1},{6,2},{7,3},{8,12},{9,13},{10,... | collective-permute-start | bytes 3145736 | tf_op jit(solution)/shard_map/ppermute | solution.py:349
  97.8 8.7 %copy-start.5 = (bf16[1024,512]{1,0:T(8,128)(2,1)S(1)}, bf16[1024,512]{1,0:T(8,128)(2,1)}, u32[]{:S(2)}) copy-start(bf16[1024,512]{1,0:T(8,128)(2,1)} %shard.3) | copy-start | bytes 3145732
  97.8 59.0 %all-to-all-start.1 = ((bf16[16,512,128]{2,1,0:T(8,128)(2,1)}), bf16[16,512,128]{2,1,0:T(8,128)(2,1)S(1)}, u32[]{:S(2)}, u32[]{:S(2)}) async-start(bf16[16,512,128]{2,1,0:T(8,128)(2,1)} %bitcast.7), calls=%async_computation.1 | async-start | bytes 4194304 | tf_op jit(solution)/shard_map/all_to_all | solution.py:352
  106.5 45.5 %collective-permute-start.1 = (bf16[1024,512]{1,0:T(8,128)(2,1)S(1)}, bf16[1024,512]{1,0:T(8,128)(2,1)S(1)}, u32[]{:S(2)}, u32[]{:S(2)}) collective-permute-start(bf16[1024,512]{1,0:T(8,128)(2,1)S(1)} %copy-done.5), channel_id=1, source_target_pairs={{0,4},{1,5},{2,6},{3,7},{4,0},{5,1},{6,2},{7,3},{8,12},{9,13},{10,... | collective-permute-start | bytes 3145736 | tf_op jit(solution)/shard_map/ppermute | solution.py:349
  156.8 1.3 copy-start.11
  158.1 8.6 %copy-start.6 = (bf16[192,4096]{1,0:T(8,128)(2,1)S(1)}, bf16[192,4096]{1,0:T(8,128)(2,1)}, u32[]{:S(2)}) copy-start(bf16[192,4096]{1,0:T(8,128)(2,1)} %q_ref.3) | copy-start | bytes 4718596
  158.1 35.5 %all-to-all-start.3 = ((bf16[16,512,128]{2,1,0:T(8,128)(2,1)}), bf16[16,512,128]{2,1,0:T(8,128)(2,1)}, u32[]{:S(2)}, u32[]{:S(2)}) async-start(bf16[16,512,128]{2,1,0:T(8,128)(2,1)} %bitcast.11), calls=%async_computation.3 | async-start | bytes 4194304 | tf_op jit(solution)/shard_map/all_to_all | solution.py:352
  166.7 1.4 copy-start.8
  192.3 1.3 copy-start.2
  224.0 39.4 %all-to-all-start.7 = ((bf16[16,512,128]{2,1,0:T(8,128)(2,1)}), bf16[16,512,128]{2,1,0:T(8,128)(2,1)}, u32[]{:S(2)}, u32[]{:S(2)}) async-start(bf16[16,512,128]{2,1,0:T(8,128)(2,1)} %bitcast.31), calls=%async_computation.7 | async-start | bytes 4194304 | tf_op jit(solution)/shard_map/all_to_all | solution.py:352
  229.3 1.4 copy-start.7
  230.7 1.4 copy-start.9
  262.1 1.3 copy-start.1
  293.9 86.0 %all-to-all-start.4 = ((bf16[16,512,128]{2,1,0:T(8,128)(2,1)}), bf16[16,512,128]{2,1,0:T(8,128)(2,1)}, u32[]{:S(2)}, u32[]{:S(2)}) async-start(bf16[16,512,128]{2,1,0:T(8,128)(2,1)} %bitcast.26), calls=%async_computation.4 | async-start | bytes 4194304 | tf_op jit(solution)/shard_map/all_to_all | solution.py:352
  299.2 7.2 %copy-start = (bf16[16,512,128]{2,1,0:T(8,128)(2,1)S(1)}, bf16[16,512,128]{2,1,0:T(8,128)(2,1)}, u32[]{:S(2)}) copy-start(bf16[16,512,128]{2,1,0:T(8,128)(2,1)} %all_to_all.41) | copy-start | bytes 6291460
  304.4 70.2 %collective-permute-start.3 = (bf16[1024,512]{1,0:T(8,128)(2,1)S(1)}, bf16[1024,512]{1,0:T(8,128)(2,1)S(1)}, u32[]{:S(2)}, u32[]{:S(2)}) collective-permute-start(bf16[1024,512]{1,0:T(8,128)(2,1)S(1)} %relay.3), channel_id=1, source_target_pairs={{0,4},{1,5},{2,6},{3,7},{4,0},{5,1},{6,2},{7,3},{8,12},{9,13},{10,... | collective-permute-start | bytes 3145736 | tf_op jit(solution)/shard_map/ppermute | solution.py:349
  310.4 86.8 %collective-permute-start.2 = (bf16[1024,512]{1,0:T(8,128)(2,1)S(1)}, bf16[1024,512]{1,0:T(8,128)(2,1)}, u32[]{:S(2)}, u32[]{:S(2)}) collective-permute-start(bf16[1024,512]{1,0:T(8,128)(2,1)S(1)} %relay.2), channel_id=1, source_target_pairs={{0,4},{1,5},{2,6},{3,7},{4,0},{5,1},{6,2},{7,3},{8,12},{9,13},{10,... | collective-permute-start | bytes 3145736 | tf_op jit(solution)/shard_map/ppermute | solution.py:349

commit v2 on v1

--- a/solution.py
+++ b/solution.py
@@ -1,5 +1,3 @@
-import functools
-
 import jax
 import jax.numpy as jnp
 from jax import lax
@@ -7,7 +5,6 @@
 from jax.experimental.pallas import tpu as pltpu
 from jax.sharding import PartitionSpec as P
 
-H = 32
 KVH = 4
 HD = 128
 BLK = 64
@@ -38,15 +35,36 @@
 
 def pack_kernel(tab, shard, out):
     def step(slot, carry):
-        code = tab[slot]
-
-        @pl.when(code >= 0)
+        out[slot] = tile_at(shard, jnp.maximum(tab[slot], 0))[...]
+        return carry
+
+    lax.fori_loop(0, tab.shape[0], step, 0, unroll=8)
+
+
+def pack_far_kernel(tab, pick, inner_part, outer_part, out, shard, sem):
+    for side, part in ((1, inner_part), (0, outer_part)):
+
+        @pl.when(pick[0] == side)
         def _():
-            out[slot] = tile_at(shard, code)[...]
-
-        return carry
-
-    lax.fori_loop(0, tab.shape[0], step, 0)
+            copy = pltpu.make_async_copy(part, shard, sem)
+            copy.start()
+            copy.wait()
+
+    pack_kernel(tab, shard, out)
+
+
+def pack_far(tab, pick, inner_part, outer_part):
+    slots = tab.shape[0]
+    return pl.pallas_call(
+        pack_far_kernel,
+        out_shape=jax.ShapeDtypeStruct((slots, BLK, HD), inner_part.dtype),
+        in_specs=[pl.BlockSpec(memory_space=SMEM)] * 2 + [pl.BlockSpec(memory_space=pl.ANY)] * 2,
+        out_specs=pl.BlockSpec(memory_space=VMEM),
+        scratch_shapes=[VMEM(inner_part.shape, inner_part.dtype), pltpu.SemaphoreType.DMA],
+        compiler_params=params(),
+        cost_estimate=pl.CostEstimate(flops=2_000_000, bytes_accessed=4 * slots * BLK * HD, transcendentals=0),
+        name="pack_far",
+    )(tab, pick, inner_part, outer_part)
 
 
 def pack(tab, shard):
@@ -65,15 +83,12 @@
 def add_slots(tab, slots, acc):
     def step(slot, carry):
         code = tab[slot]
-
-        @pl.when(code >= 0)
-        def _():
-            spot = tile_at(acc, code)
-            spot[...] += slots[slot].astype(F32)
-
+        spot = tile_at(acc, jnp.maximum(code, 0))
+        term = slots[slot].astype(F32)
+        spot[...] += jnp.where(code >= 0, term, jnp.zeros_like(term))
         return carry
 
-    lax.fori_loop(0, tab.shape[0], step, 0)
+    lax.fori_loop(0, tab.shape[0], step, 0, unroll=4)
 
 
 def relay_kernel(tab, slots, out, acc):
@@ -345,10 +360,25 @@
         [a * inner + half * near + b for a in range(outer) for b in range(near)] for half in (0, 1)
     ]
 
-    def across(x):
-        return lax.ppermute(x, "cy", [(i, (i + near) % inner) for i in range(inner)])
-
-    def among(x):
+    edge = near // 2
+    inside = [c for c in range(inner) if (c < near) == (c % near >= edge)]
+    outside = [c for c in range(inner) if c not in inside]
+    column = lax.axis_index("cy")
+    from_inside = ((column >= near) == (column % near >= edge)).astype(jnp.int32).reshape(1)
+
+    def across(x, senders=None, back=False):
+        senders = range(inner) if senders is None else senders
+        pairs = [
+            (a * inner + i, a * inner + (i + near) % inner)
+            for a in range(outer)
+            for i in senders
+            if a * inner + ((i + near) % inner if back else i) < usable
+        ]
+        return lax.ppermute(x, ("cx", "cy"), pairs)
+
+    def among(x, after=None):
+        if after is not None:
+            x = lax.optimization_barrier((x, after))[0]
         y = lax.all_to_all(
             x.reshape(mates, capacity * BLK, HD),
             ("cx", "cy"),
@@ -359,19 +389,20 @@
         )
         return y.reshape(x.shape)
 
-    far_keys = across(keys)
+    far_keys = across(keys, inside), across(keys, outside)
+    far_values = across(values, inside), across(values, outside)
     k_here = among(pack(tab_own, keys))
-    far_keys, values_next = lax.optimization_barrier((far_keys, values))
-    far_values = across(values_next)
-    k_there = among(pack(tab_far, far_keys))
-    v_here = among(pack(tab_own, values))
-    v_there = among(pack(tab_far, far_values))
+    v_here = among(pack(tab_own, values), k_here)
+    k_there = among(pack_far(tab_far, from_inside, *far_keys), v_here)
+    v_there = among(pack_far(tab_far, from_inside, *far_values), k_there)
     dv_here, dv_there, stats = first(slot, queries, d_out, k_here, k_there)
-    dv_far = across(relay(tab_far, among(dv_there)))
-    dv_near = among(dv_here)
+    dv_relay = among(dv_there, v_there)
+    dv_far = across(relay(tab_far, dv_relay), back=True)
     dk_here, dk_there, d_queries = second(slot, queries, d_out, stats, k_here, k_there, v_here, v_there)
-    dk_far = across(relay(tab_far, among(dk_there)))
-    dk_near = among(dk_here)
+    dk_relay = among(dk_there, dv_relay)
+    dv_near = among(dv_here, dk_relay)
+    dk_far = across(relay(tab_far, dk_relay), back=True)
+    dk_near = among(dk_here, dv_near)
     d_values = own_sum(tab_own, dv_near, dv_far)
     d_keys = own_sum(tab_own, dk_near, dk_far)
     return (d_queries, d_keys, d_values)

time: 407 us -> 405 us (level)
  Pallas kernels: 94.4 us -> 76.7 us
  waiting for transfers between devices: 189 us -> 202 us
    pallas_call x4 -> x2, Pallas kernels: 19.2 us -> 5.76 us  [pack(): pl.pallas_call(pack_kernel, out_shape=jax.ShapeDtypeStruct((slots, BLK, H...]
    ppermute x4 -> x6, waiting for transfers between devices: 168 us -> 179 us  [across(): return lax.ppermute(x, ('cx', 'cy'), pairs)]
    ppermute x4 -> x6, starting transfers between devices: 6.71 us -> 15.5 us  [across(): return lax.ppermute(x, ('cx', 'cy'), pairs)]
    all_to_all x6, starting transfers between devices: 38.9 us -> 32.3 us  [among(): lax.all_to_all(x.reshape(mates, capacity * BLK, HD), ('cx', 'cy'), split_...]
    pallas_call x0 -> x2, Pallas kernels: none -> 5.94 us  [pack_far(): pl.pallas_call(pack_far_kernel, out_shape=jax.ShapeDtypeStruct((slots, BL...]
    pallas_call x2, Pallas kernels: 11.8 us -> 6.62 us  [own_sum(): pl.pallas_call(own_kernel, out_shape=jax.ShapeDtypeStruct(other.shape, F3...]
    pallas_call x2, Pallas kernels: 9.17 us -> 4.19 us  [relay(): pl.pallas_call(relay_kernel, out_shape=jax.ShapeDtypeStruct(shape, BF16),...]
    unnamed x25 -> x35, local copies, waits for them, and re-layouts: 11.7 us -> 13.2 us
  transfers between devices with their start and end apart: 10 -> 12, of which waited for: 5 -> 7; matrix products, arithmetic and copies ran while one was open for 0% -> 0% of each run, Pallas kernels for 21% -> 18%
where the time goes in v2:
time: 405 us; the launch traced here: 403 us
  waiting for transfers between devices  202 us (50%)
  Pallas kernels  76.7 us (19%)
  blocking collectives  60.2 us (15%)
  starting transfers between devices  47.8 us (12%)
  local copies, waits for them, and re-layouts  13.7 us (3%)
    ppermute x6, waiting for transfers between devices, across(): return lax.ppermute(x, ('cx', 'cy'), pairs)  179 us
    all_to_all x2, blocking collectives, among(): lax.all_to_all(x.reshape(mates, capacity * BLK, HD), ('cx', 'cy'), split_...  60.2 us
    all_to_all x6, starting transfers between devices, among(): lax.all_to_all(x.reshape(mates, capacity * BLK, HD), ('cx', 'cy'), split_...  32.3 us
    pallas_call x1, Pallas kernels, second(): pl.pallas_call(second_kernel, grid=(QB_DEV, KVH), out_shape=(jax.ShapeDty...  29.9 us
    pallas_call x1, Pallas kernels, first(): pl.pallas_call(first_kernel, grid=(QB_DEV, KVH), out_shape=(jax.ShapeDtyp...  24.2 us
    all_to_all x6, waiting for transfers between devices, among(): lax.all_to_all(x.reshape(mates, capacity * BLK, HD), ('cx', 'cy'), split_...  22.9 us
    ppermute x6, starting transfers between devices, across(): return lax.ppermute(x, ('cx', 'cy'), pairs)  15.5 us
    unnamed x35, local copies, waits for them, and re-layouts  13.2 us
  transfers between devices with their start and end apart: 12, of which 7 were waited for; matrix products, arithmetic and copies ran while one was open for 0% of the time, Pallas kernels for 18%

profile of v2, /device:TPU:3, one launch (start us, length us, event | category | flops | bytes accessed | tf_op | source)
XLA Modules:
  0.0 402.6 jit_solution(5080584436734649749)
XLA Ops:
  0.7 0.9 copy.10
  1.6 0.2 reshape.244
  1.8 0.1 fusion.14
  1.9 0.1 broadcast_compare_fusion
  2.0 0.1 convolution_convert_fusion
  2.1 0.6 select_reduce_fusion
  2.8 0.1 squeeze.13.tab
  2.8 0.0 copy-start.7
  2.9 1.2 copy-done.7
  4.1 2.9 pack.2
  7.0 5.7 %all-to-all-start = ((bf16[16,512,128]{2,1,0:T(8,128)(2,1)}), bf16[16,512,128]{2,1,0:T(8,128)(2,1)S(1)}, u32[]{:S(2)}, u32[]{:S(2)}) async-start(bf16[16,512,128]{2,1,0:T(8,128)(2,1)} %bitcast.5), calls=%async_computation | async-start | bytes 4194304 | tf_op jit(solution)/shard_map/all_to_all | solution.py:382
  12.7 0.0 copy-done.9
  12.7 2.9 pack.3
  15.5 22.9 %all-to-all-done = bf16[16,512,128]{2,1,0:T(8,128)(2,1)S(1)} async-done(((bf16[16,512,128]{2,1,0:T(8,128)(2,1)}), bf16[16,512,128]{2,1,0:T(8,128)(2,1)S(1)}, u32[]{:S(2)}, u32[]{:S(2)}) %all-to-all-start) | async-done | bytes 2097184 | tf_op jit(solution)/shard_map/all_to_all | solution.py:382
  38.4 1.3 copy-done.15
  39.7 5.9 %all-to-all-start.1 = ((bf16[16,512,128]{2,1,0:T(8,128)(2,1)}), bf16[16,512,128]{2,1,0:T(8,128)(2,1)}, u32[]{:S(2)}, u32[]{:S(2)}) async-start(bf16[16,512,128]{2,1,0:T(8,128)(2,1)} %bitcast.8), calls=%async_computation.1 | async-start | bytes 4194304 | tf_op jit(solution)/shard_map/all_to_all | solution.py:382
  45.6 0.0 copy-done.8
  45.6 4.3 %collective-permute-start.1 = (bf16[1024,512]{1,0:T(8,128)(2,1)S(1)}, bf16[1024,512]{1,0:T(8,128)(2,1)S(1)}, u32[]{:S(2)}, u32[]{:S(2)}) collective-permute-start(bf16[1024,512]{1,0:T(8,128)(2,1)S(1)} %copy-done.8), channel_id=1, source_target_pairs={{0,4},{1,5},{6,2},{7,3},{8,12},{9,13},{14,10},{15,11},{16,20},{17,... | collective-permute-start | bytes 3145736 | tf_op jit(solution)/shard_map/ppermute | solution.py:377
  49.9 1.3 collective-permute-start
  51.2 0.1 squeeze.14.tab
  51.3 39.9 %collective-permute-done.1.outer_part = bf16[1024,512]{1,0:T(8,128)(2,1)S(1)} collective-permute-done((bf16[1024,512]{1,0:T(8,128)(2,1)S(1)}, bf16[1024,512]{1,0:T(8,128)(2,1)S(1)}, u32[]{:S(2)}, u32[]{:S(2)}) %collective-permute-start.1) | collective-permute-done | bytes 1048608 | tf_op jit(solution)/shard_map/ppermute | solution.py:377
  91.2 8.2 %collective-permute-done.inner_part = bf16[1024,512]{1,0:T(8,128)(2,1)S(1)} collective-permute-done((bf16[1024,512]{1,0:T(8,128)(2,1)S(1)}, bf16[1024,512]{1,0:T(8,128)(2,1)S(1)}, u32[]{:S(2)}, u32[]{:S(2)}) %collective-permute-start) | collective-permute-done | bytes 1048608 | tf_op jit(solution)/shard_map/ppermute | solution.py:377
  99.4 3.0 pack_far.2
  102.3 0.0 all-to-all-done.1
  102.3 0.0 copy-start.10
  102.4 5.1 %all-to-all-start.2 = ((bf16[16,512,128]{2,1,0:T(8,128)(2,1)}), bf16[16,512,128]{2,1,0:T(8,128)(2,1)S(1)}, u32[]{:S(2)}, u32[]{:S(2)}) async-start(bf16[16,512,128]{2,1,0:T(8,128)(2,1)} %bitcast.10), calls=%async_computation.2 | async-start | bytes 4194304 | tf_op jit(solution)/shard_map/all_to_all | solution.py:382
  107.5 0.0 copy-done.10
  107.5 2.3 collective-permute-start.3
  109.8 1.3 collective-permute-start.2
  111.1 41.9 %collective-permute-done.3.outer_part = bf16[1024,512]{1,0:T(8,128)(2,1)S(1)} collective-permute-done((bf16[1024,512]{1,0:T(8,128)(2,1)S(1)}, bf16[1024,512]{1,0:T(8,128)(2,1)S(1)}, u32[]{:S(2)}, u32[]{:S(2)}) %collective-permute-start.3) | collective-permute-done | bytes 1048608 | tf_op jit(solution)/shard_map/ppermute | solution.py:377
  153.1 6.2 %collective-permute-done.2.inner_part = bf16[1024,512]{1,0:T(8,128)(2,1)S(1)} collective-permute-done((bf16[1024,512]{1,0:T(8,128)(2,1)S(1)}, bf16[1024,512]{1,0:T(8,128)(2,1)S(1)}, u32[]{:S(2)}, u32[]{:S(2)}) %collective-permute-start.2) | collective-permute-done | bytes 1048608 | tf_op jit(solution)/shard_map/ppermute | solution.py:377
  159.2 3.0 pack_far.3
  162.2 0.0 all-to-all-done.2
  162.2 0.0 copy-start.16
  162.2 1.3 copy-done.16
  163.6 5.8 %all-to-all-start.3 = ((bf16[16,512,128]{2,1,0:T(8,128)(2,1)}), bf16[16,512,128]{2,1,0:T(8,128)(2,1)}, u32[]{:S(2)}, u32[]{:S(2)}) async-start(bf16[16,512,128]{2,1,0:T(8,128)(2,1)} %bitcast.12), calls=%async_computation.3 | async-start | bytes 4194304 | tf_op jit(solution)/shard_map/all_to_all | solution.py:382
  169.4 0.1 reshape.243
  169.5 0.2 convert_reduce_fusion
  169.8 0.0 copy-start.13
  169.8 1.4 copy-done.13
  171.2 24.2 %first.1 = (bf16[128,64,128]{2,1,0:T(8,128)(2,1)S(1)}, bf16[128,64,128]{2,1,0:T(8,128)(2,1)}, f32[12,8,512]{2,1,0:T(8,128)S(1)}) custom-call(s32[192]{0:T(256)S(1)} %multiply_add_fusion.idx, bf16[192,4096]{1,0:T(8,128)(2,1)S(1)} %copy-done.11, bf16[192,4096]{1,0:T(8,128)(2,1)S(1)} %copy-done.13, bf16[128,64,128]{2,1,0:T(8,128)(2,1)} %bitcast.31, ...), custom_call_target="tpu_custom_call" | custom-call | flops 3221225472 | bytes 8388608 | tf_op jit(solution)/shard_map/first/pallas_call | solution.py:220
  195.4 1.3 copy-done.5
  196.8 0.0 all-to-all-done.3
  196.8 5.2 %all-to-all-start.4 = ((bf16[16,512,128]{2,1,0:T(8,128)(2,1)}), bf16[16,512,128]{2,1,0:T(8,128)(2,1)S(1)}, u32[]{:S(2)}, u32[]{:S(2)}) async-start(bf16[16,512,128]{2,1,0:T(8,128)(2,1)} %bitcast.35), calls=%async_computation.4 | async-start | bytes 4194304 | tf_op jit(solution)/shard_map/all_to_all | solution.py:382
  201.9 1.4 copy-done.12
  203.3 1.4 copy-done.14
  204.7 29.9 %second.1 = (bf16[128,64,128]{2,1,0:T(8,128)(2,1)S(1)}, bf16[128,64,128]{2,1,0:T(8,128)(2,1)}, f32[192,4096]{1,0:T(8,128)}) custom-call(s32[192]{0:T(256)S(1)} %multiply_add_fusion.idx, bf16[192,4096]{1,0:T(8,128)(2,1)S(1)} %copy-done.12, bf16[192,4096]{1,0:T(8,128)(2,1)S(1)} %copy-done.14, f32[12,8,512]{2,1,0:T(8,128)S(1)} %get-tuple-element.18.stats, ...), custom_call_target="tpu_custom_call" | custom-call | flops 6442450944 | bytes 16777216 | tf_op jit(solution)/shard_map/second/pallas_call | solution.py:290
  234.7 0.0 copy-start.4
  234.7 1.3 copy-done.4
  236.0 0.0 all-to-all-done.4
  236.0 30.7 %all_to_all.40 = bf16[16,512,128]{2,1,0:T(8,128)(2,1)} all-to-all(bf16[16,512,128]{2,1,0:T(8,128)(2,1)} %bitcast.36), channel_id=1, replica_groups={{0,1,2,3,8,9,10,11,16,17,18,19,24,25,26,27},{4,5,6,7,12,13,14,15,20,21,..., dimensions={0} | all-to-all | bytes 4194304 | tf_op jit(solution)/shard_map/all_to_all | solution.py:382
  266.7 0.0 copy-done.6
  266.7 29.5 %all_to_all.41 = bf16[16,512,128]{2,1,0:T(8,128)(2,1)} all-to-all(bf16[16,512,128]{2,1,0:T(8,128)(2,1)S(1)} %bitcast.30), channel_id=1, replica_groups={{0,1,2,3,8,9,10,11,16,17,18,19,24,25,26,27},{4,5,6,7,12,13,14,15,20,21,..., dimensions={0} | all-to-all | bytes 4194304 | tf_op jit(solution)/shard_map/all_to_all | solution.py:382
  296.3 4.6 %all-to-all-start.7 = ((bf16[16,512,128]{2,1,0:T(8,128)(2,1)}), bf16[16,512,128]{2,1,0:T(8,128)(2,1)S(1)}, u32[]{:S(2)}, u32[]{:S(2)}) async-start(bf16[16,512,128]{2,1,0:T(8,128)(2,1)} %bitcast.29), calls=%async_computation.7 | async-start | bytes 4194304 | tf_op jit(solution)/shard_map/all_to_all | solution.py:382
  300.9 1.6 copy-done.1
  302.5 2.1 relay.3
  304.6 3.7 collective-permute-start.5
  308.3 2.1 relay.2
  310.4 2.6 collective-permute-start.4
  313.0 63.8 %collective-permute-done.5.other = bf16[1024,512]{1,0:T(8,128)(2,1)S(1)} collective-permute-done((bf16[1024,512]{1,0:T(8,128)(2,1)S(1)}, bf16[1024,512]{1,0:T(8,128)(2,1)S(1)}, u32[]{:S(2)}, u32[]{:S(2)}) %collective-permute-start.5) | collective-permute-done | bytes 1048608 | tf_op jit(solution)/shard_map/ppermute | solution.py:377
  376.9 3.3 own_sum.3
  380.2 19.2 %collective-permute-done.4.other = bf16[1024,512]{1,0:T(8,128)(2,1)S(1)} collective-permute-done((bf16[1024,512]{1,0:T(8,128)(2,1)S(1)}, bf16[1024,512]{1,0:T(8,128)(2,1)S(1)}, u32[]{:S(2)}, u32[]{:S(2)}) %collective-permute-start.4) | collective-permute-done | bytes 1048608 | tf_op jit(solution)/shard_map/ppermute | solution.py:377
  399.3 0.0 all-to-all-done.7
  399.3 3.3 own_sum.2
  (25 shorter events, 0.1 us)
Async XLA Ops:
  2.8 1.2 copy-start.7
  7.0 5.7 %copy-start.9 = (bf16[1024,512]{1,0:T(8,128)(2,1)S(1)}, bf16[1024,512]{1,0:T(8,128)(2,1)}, u32[]{:S(2)}) copy-start(bf16[1024,512]{1,0:T(8,128)(2,1)} %shard.3) | copy-start | bytes 3145732
  7.0 31.5 %all-to-all-start = ((bf16[16,512,128]{2,1,0:T(8,128)(2,1)}), bf16[16,512,128]{2,1,0:T(8,128)(2,1)S(1)}, u32[]{:S(2)}, u32[]{:S(2)}) async-start(bf16[16,512,128]{2,1,0:T(8,128)(2,1)} %bitcast.5), calls=%async_computation | async-start | bytes 4194304 | tf_op jit(solution)/shard_map/all_to_all | solution.py:382
  38.4 1.3 copy-start.15
  39.7 5.9 %copy-start.8 = (bf16[1024,512]{1,0:T(8,128)(2,1)S(1)}, bf16[1024,512]{1,0:T(8,128)(2,1)}, u32[]{:S(2)}) copy-start(bf16[1024,512]{1,0:T(8,128)(2,1)} %shard.2) | copy-start | bytes 3145732
  39.7 62.6 %all-to-all-start.1 = ((bf16[16,512,128]{2,1,0:T(8,128)(2,1)}), bf16[16,512,128]{2,1,0:T(8,128)(2,1)}, u32[]{:S(2)}, u32[]{:S(2)}) async-start(bf16[16,512,128]{2,1,0:T(8,128)(2,1)} %bitcast.8), calls=%async_computation.1 | async-start | bytes 4194304 | tf_op jit(solution)/shard_map/all_to_all | solution.py:382
  45.6 45.6 %collective-permute-start.1 = (bf16[1024,512]{1,0:T(8,128)(2,1)S(1)}, bf16[1024,512]{1,0:T(8,128)(2,1)S(1)}, u32[]{:S(2)}, u32[]{:S(2)}) collective-permute-start(bf16[1024,512]{1,0:T(8,128)(2,1)S(1)} %copy-done.8), channel_id=1, source_target_pairs={{0,4},{1,5},{6,2},{7,3},{8,12},{9,13},{14,10},{15,11},{16,20},{17,... | collective-permute-start | bytes 3145736 | tf_op jit(solution)/shard_map/ppermute | solution.py:377
  49.9 49.4 %collective-permute-start = (bf16[1024,512]{1,0:T(8,128)(2,1)S(1)}, bf16[1024,512]{1,0:T(8,128)(2,1)S(1)}, u32[]{:S(2)}, u32[]{:S(2)}) collective-permute-start(bf16[1024,512]{1,0:T(8,128)(2,1)S(1)} %copy-done.8), channel_id=1, source_target_pairs={{2,6},{3,7},{4,0},{5,1},{10,14},{11,15},{12,8},{13,9},{18,22},{19,... | collective-permute-start | bytes 3145736 | tf_op jit(solution)/shard_map/ppermute | solution.py:377
  102.3 5.1 %copy-start.10 = (bf16[1024,512]{1,0:T(8,128)(2,1)S(1)}, bf16[1024,512]{1,0:T(8,128)(2,1)}, u32[]{:S(2)}) copy-start(bf16[1024,512]{1,0:T(8,128)(2,1)} %shard.3) | copy-start | bytes 3145732
  102.4 59.9 %all-to-all-start.2 = ((bf16[16,512,128]{2,1,0:T(8,128)(2,1)}), bf16[16,512,128]{2,1,0:T(8,128)(2,1)S(1)}, u32[]{:S(2)}, u32[]{:S(2)}) async-start(bf16[16,512,128]{2,1,0:T(8,128)(2,1)} %bitcast.10), calls=%async_computation.2 | async-start | bytes 4194304 | tf_op jit(solution)/shard_map/all_to_all | solution.py:382
  107.5 45.6 %collective-permute-start.3 = (bf16[1024,512]{1,0:T(8,128)(2,1)S(1)}, bf16[1024,512]{1,0:T(8,128)(2,1)S(1)}, u32[]{:S(2)}, u32[]{:S(2)}) collective-permute-start(bf16[1024,512]{1,0:T(8,128)(2,1)S(1)} %copy-done.10), channel_id=1, source_target_pairs={{0,4},{1,5},{6,2},{7,3},{8,12},{9,13},{14,10},{15,11},{16,20},{17,... | collective-permute-start | bytes 3145736 | tf_op jit(solution)/shard_map/ppermute | solution.py:377
  109.8 49.4 %collective-permute-start.2 = (bf16[1024,512]{1,0:T(8,128)(2,1)S(1)}, bf16[1024,512]{1,0:T(8,128)(2,1)S(1)}, u32[]{:S(2)}, u32[]{:S(2)}) collective-permute-start(bf16[1024,512]{1,0:T(8,128)(2,1)S(1)} %copy-done.10), channel_id=1, source_target_pairs={{2,6},{3,7},{4,0},{5,1},{10,14},{11,15},{12,8},{13,9},{18,22},{19,... | collective-permute-start | bytes 3145736 | tf_op jit(solution)/shard_map/ppermute | solution.py:377
  162.2 1.3 copy-start.16
  163.5 6.2 %copy-start.11 = (bf16[192,4096]{1,0:T(8,128)(2,1)S(1)}, bf16[192,4096]{1,0:T(8,128)(2,1)}, u32[]{:S(2)}) copy-start(bf16[192,4096]{1,0:T(8,128)(2,1)} %q_ref.3) | copy-start | bytes 4718596
  163.6 33.2 %all-to-all-start.3 = ((bf16[16,512,128]{2,1,0:T(8,128)(2,1)}), bf16[16,512,128]{2,1,0:T(8,128)(2,1)}, u32[]{:S(2)}, u32[]{:S(2)}) async-start(bf16[16,512,128]{2,1,0:T(8,128)(2,1)} %bitcast.12), calls=%async_computation.3 | async-start | bytes 4194304 | tf_op jit(solution)/shard_map/all_to_all | solution.py:382
  169.8 1.4 copy-start.13
  195.4 1.3 copy-start.5
  196.8 39.2 %all-to-all-start.4 = ((bf16[16,512,128]{2,1,0:T(8,128)(2,1)}), bf16[16,512,128]{2,1,0:T(8,128)(2,1)S(1)}, u32[]{:S(2)}, u32[]{:S(2)}) async-start(bf16[16,512,128]{2,1,0:T(8,128)(2,1)} %bitcast.35), calls=%async_computation.4 | async-start | bytes 4194304 | tf_op jit(solution)/shard_map/all_to_all | solution.py:382
  201.9 1.4 copy-start.12
  203.3 1.4 copy-start.14
  234.7 1.3 copy-start.4
  236.0 30.7 %copy-start = (bf16[16,512,128]{2,1,0:T(8,128)(2,1)}, bf16[16,512,128]{2,1,0:T(8,128)(2,1)S(1)}, u32[]{:S(2)}) copy-start(bf16[16,512,128]{2,1,0:T(8,128)(2,1)S(1)} %all-to-all-done.4) | copy-start | bytes 6291460
  236.0 30.7 %copy-start.6 = (bf16[128,64,128]{2,1,0:T(8,128)(2,1)S(1)}, bf16[128,64,128]{2,1,0:T(8,128)(2,1)}, u32[]{:S(2)}) copy-start(bf16[128,64,128]{2,1,0:T(8,128)(2,1)} %copy-done.5) | copy-start | bytes 6291460
  296.3 103.1 %all-to-all-start.7 = ((bf16[16,512,128]{2,1,0:T(8,128)(2,1)}), bf16[16,512,128]{2,1,0:T(8,128)(2,1)S(1)}, u32[]{:S(2)}, u32[]{:S(2)}) async-start(bf16[16,512,128]{2,1,0:T(8,128)(2,1)} %bitcast.29), calls=%async_computation.7 | async-start | bytes 4194304 | tf_op jit(solution)/shard_map/all_to_all | solution.py:382
  300.9 1.6 copy-start.1
  302.5 5.8 %copy-start.3 = (bf16[16,512,128]{2,1,0:T(8,128)(2,1)S(1)}, bf16[16,512,128]{2,1,0:T(8,128)(2,1)}, u32[]{:S(2)}) copy-start(bf16[16,512,128]{2,1,0:T(8,128)(2,1)} %all_to_all.40) | copy-start | bytes 6291460
  304.6 72.3 %copy-start.2 = (bf16[16,512,128]{2,1,0:T(8,128)(2,1)S(1)}, bf16[16,512,128]{2,1,0:T(8,128)(2,1)}, u32[]{:S(2)}) copy-start(bf16[16,512,128]{2,1,0:T(8,128)(2,1)} %all_to_all.41) | copy-start | bytes 6291460
  304.6 72.3 %collective-permute-start.5 = (bf16[1024,512]{1,0:T(8,128)(2,1)S(1)}, bf16[1024,512]{1,0:T(8,128)(2,1)S(1)}, u32[]{:S(2)}, u32[]{:S(2)}) collective-permute-start(bf16[1024,512]{1,0:T(8,128)(2,1)S(1)} %relay.3), channel_id=1, source_target_pairs={{0,4},{1,5},{2,6},{3,7},{4,0},{5,1},{6,2},{7,3},{8,12},{9,13},{10,... | collective-permute-start | bytes 3145736 | tf_op jit(solution)/shard_map/ppermute | solution.py:377
  310.4 88.9 %collective-permute-start.4 = (bf16[1024,512]{1,0:T(8,128)(2,1)S(1)}, bf16[1024,512]{1,0:T(8,128)(2,1)S(1)}, u32[]{:S(2)}, u32[]{:S(2)}) collective-permute-start(bf16[1024,512]{1,0:T(8,128)(2,1)S(1)} %relay.2), channel_id=1, source_target_pairs={{0,4},{1,5},{2,6},{3,7},{4,0},{5,1},{6,2},{7,3},{8,12},{9,13},{10,... | collective-permute-start | bytes 3145736 | tf_op jit(solution)/shard_map/ppermute | solution.py:377

commit v3 on v2

v3 whole, which is shorter than its diff:
```python
import functools
import math

import jax
import jax.numpy as jnp
from jax import lax
from jax.experimental import pallas as pl
from jax.experimental.pallas import tpu as pltpu
from jax.sharding import PartitionSpec as P

KVH = 4
HD = 128
BLK = 64
TOPK = 16
QB_DEV = 3
KB_DEV = 16
GROUP = 8
PICKS = 192
ROWS = GROUP * BLK
SPAN = TOPK * BLK
SCALE = HD ** (-0.5)
SCALE_LOG2 = SCALE * math.log2(math.e)
SMEM = pltpu.SMEM
VMEM = pltpu.VMEM
F32 = jnp.float32
BF16 = jnp.bfloat16


def params(**more):
    return pltpu.CompilerParams(vmem_limit_bytes=48 * 1024 * 1024, **more)


def tile_at(ref, code):
    row = pl.multiple_of(code // KVH * BLK, BLK)
    lane = pl.multiple_of(code % KVH * HD, HD)
    return ref.at[pl.ds(row, BLK), pl.ds(lane, HD)]


def pack_kernel(tab, shard, out):
    def step(slot, carry):
        out[slot] = tile_at(shard, jnp.maximum(tab[slot], 0))[...]
        return carry

    lax.fori_loop(0, tab.shape[0], step, 0, unroll=8)


def pack_far_kernel(tab, pick, inner_part, outer_part, out, shard, sem):
    for side, part in ((1, inner_part), (0, outer_part)):

        @pl.when(pick[0] == side)
        def _():
            copy = pltpu.make_async_copy(part, shard, sem)
            copy.start()
            copy.wait()

    pack_kernel(tab, shard, out)


def pack_far(tab, pick, inner_part, outer_part):
    slots = tab.shape[0]
    return pl.pallas_call(
        pack_far_kernel,
        out_shape=jax.ShapeDtypeStruct((slots, BLK, HD), inner_part.dtype),
        in_specs=[pl.BlockSpec(memory_space=SMEM)] * 2 + [pl.BlockSpec(memory_space=pl.ANY)] * 2,
        out_specs=pl.BlockSpec(memory_space=VMEM),
        scratch_shapes=[VMEM(inner_part.shape, inner_part.dtype), pltpu.SemaphoreType.DMA],
        compiler_params=params(),
        cost_estimate=pl.CostEstimate(flops=2_000_000, bytes_accessed=4 * slots * BLK * HD, transcendentals=0),
        name="pack_far",
    )(tab, pick, inner_part, outer_part)


def pack(tab, shard):
    slots = tab.shape[0]
    return pl.pallas_call(
        pack_kernel,
        out_shape=jax.ShapeDtypeStruct((slots, BLK, HD), shard.dtype),
        in_specs=[pl.BlockSpec(memory_space=SMEM), pl.BlockSpec(memory_space=VMEM)],
        out_specs=pl.BlockSpec(memory_space=VMEM),
        compiler_params=params(),
        cost_estimate=pl.CostEstimate(flops=2_000_000, bytes_accessed=4 * slots * BLK * HD, transcendentals=0),
        name="pack",
    )(tab, shard)


def add_slots(tab, slots, acc):
    def step(slot, carry):
        code = tab[slot]
        spot = tile_at(acc, jnp.maximum(code, 0))
        term = slots[slot].astype(F32)
        spot[...] += jnp.where(code >= 0, term, jnp.zeros_like(term))
        return carry

    lax.fori_loop(0, tab.shape[0], step, 0, unroll=4)


def relay_kernel(tab, slots, out, acc):
    acc[...] = jnp.zeros_like(acc)
    add_slots(tab, slots, acc)
    out[...] = acc[...].astype(out.dtype)


def relay(tab, slots):
    shape = (KB_DEV * BLK, KVH * HD)
    return pl.pallas_call(
        relay_kernel,
        out_shape=jax.ShapeDtypeStruct(shape, BF16),
        in_specs=[pl.BlockSpec(memory_space=SMEM), pl.BlockSpec(memory_space=VMEM)],
        out_specs=pl.BlockSpec(memory_space=VMEM),
        scratch_shapes=[VMEM(shape, F32)],
        compiler_params=params(),
        cost_estimate=pl.CostEstimate(flops=4_000_000, bytes_accessed=4 * slots.size, transcendentals=0),
        name="relay",
    )(tab, slots)


def finish_kernel(capacity, tab, back, dv_inner, dv_outer, dk_inner, dk_outer, d_values, d_keys):
    d_values[...] = dv_inner[...].astype(F32) + dv_outer[...].astype(F32)
    d_keys[...] = dk_inner[...].astype(F32) + dk_outer[...].astype(F32)

    def step(slot, carry):
        code = tab[slot]
        spot = slot // capacity * (2 * capacity) + slot % capacity
        for shift, out in ((0, d_values), (capacity, d_keys)):
            tile = tile_at(out, jnp.maximum(code, 0))
            term = back[spot + shift].astype(F32)
            tile[...] += jnp.where(code >= 0, term, jnp.zeros_like(term))
        return carry

    lax.fori_loop(0, tab.shape[0], step, 0, unroll=4)


def finish(tab, capacity, back, dv_far, dk_far):
    shape = jax.ShapeDtypeStruct(dv_far[0].shape, F32)
    return pl.pallas_call(
        functools.partial(finish_kernel, capacity),
        out_shape=(shape, shape),
        in_specs=[pl.BlockSpec(memory_space=SMEM)] + [pl.BlockSpec(memory_space=VMEM)] * 5,
        out_specs=[pl.BlockSpec(memory_space=VMEM)] * 2,
        compiler_params=params(),
        cost_estimate=pl.CostEstimate(flops=8_000_000, bytes_accessed=12_000_000, transcendentals=0),
        name="finish",
    )(tab, back, *dv_far, *dk_far)


def slot_copies(hbm_pair, dest, sems):
    size = hbm_pair[0].shape[0]
    return [
        pltpu.make_async_copy(hbm_pair[side], dest.at[pl.ds(side * size, size)], sems.at[side])
        for side in (0, 1)
    ]


def on_first(task, copies, wait):
    @pl.when(task == 0)
    def _():
        for copy in copies:
            if wait:
                copy.wait()
            else:
                copy.start()


def gather_tiles(idx, base, table, dest):
    for pick in range(TOPK):
        dest[pick * BLK : (pick + 1) * BLK, :] = table[idx[base + pick]]


def store_tiles(idx, spots, base, tiles, back, shift, there):
    size = there.shape[0]
    for pick in range(TOPK):
        spot = idx[base + pick]
        tile = tiles[pick * BLK : (pick + 1) * BLK, :].astype(BF16)

        @pl.when(spot < size)
        def _():
            back[spots[base + pick] + shift] = tile

        @pl.when(spot >= size)
        def _():
            there[spot - size] = tile


def heads(ref):
    return jnp.concatenate([ref[:, z * HD : (z + 1) * HD] for z in range(GROUP)], axis=0)


def dot_nt(a, b):
    return lax.dot_general(a, b, (((1,), (1,)), ((), ())), preferred_element_type=F32)


def dot_nn(a, b):
    return lax.dot_general(a, b, (((1,), (0,)), ((), ())), preferred_element_type=F32)


def first_kernel(idx, spots, q_ref, o_ref, k_here, k_there, back, dv_there, stats, k_all, k_rows, acc, sems):
    task = pl.program_id(0) * KVH + pl.program_id(1)
    base = task * TOPK
    key_copies = slot_copies((k_here, k_there), k_all, sems)
    on_first(task, key_copies, wait=False)
    on_first(task, key_copies, wait=True)
    gather_tiles(idx, base, k_all, k_rows)
    scores = dot_nt(k_rows[...], heads(q_ref))
    top = jnp.max(scores, axis=0, keepdims=True)
    weights = jnp.exp2((scores - top) * SCALE_LOG2)
    inverse = 1.0 / jnp.sum(weights, axis=0, keepdims=True)
    stats[0, 0:1, :] = top
    stats[0, 1:2, :] = inverse
    acc[...] = dot_nn((weights * inverse).astype(BF16), heads(o_ref))
    store_tiles(idx, spots, base, acc, back, 0, dv_there)


def task_specs():
    return [
        pl.BlockSpec((BLK, GROUP * HD), lambda r, g: (r, g)),
        pl.BlockSpec((BLK, GROUP * HD), lambda r, g: (r, g)),
    ]


def first(idx, spots, queries, d_out, k_here, k_there):
    slots = k_here.shape[0]
    whole = pl.BlockSpec((slots, BLK, HD), lambda r, g: (0, 0, 0))
    both = pl.BlockSpec((2 * slots, BLK, HD), lambda r, g: (0, 0, 0))
    flops = 4 * QB_DEV * KVH * ROWS * SPAN * HD
    return pl.pallas_call(
        first_kernel,
        grid=(QB_DEV, KVH),
        out_shape=(
            jax.ShapeDtypeStruct((2 * slots, BLK, HD), BF16),
            jax.ShapeDtypeStruct((slots, BLK, HD), BF16),
            jax.ShapeDtypeStruct((QB_DEV * KVH, 8, ROWS), F32),
        ),
        in_specs=[pl.BlockSpec(memory_space=SMEM)] * 2
        + task_specs()
        + [pl.BlockSpec(memory_space=pl.ANY), pl.BlockSpec(memory_space=pl.ANY)],
        out_specs=(both, whole, pl.BlockSpec((1, 8, ROWS), lambda r, g: (r * KVH + g, 0, 0))),
        scratch_shapes=[
            VMEM((2 * slots, BLK, HD), BF16),
            VMEM((SPAN, HD), BF16),
            VMEM((SPAN, HD), F32),
            pltpu.SemaphoreType.DMA((2,)),
        ],
        compiler_params=pltpu.CompilerParams(dimension_semantics=("arbitrary", "arbitrary")),
        cost_estimate=pl.CostEstimate(
            flops=flops, bytes_accessed=8 * slots * BLK * HD, transcendentals=QB_DEV * KVH * ROWS * SPAN
        ),
        name="first",
    )(idx, spots, queries, d_out, k_here, k_there)


def second_kernel(
    capacity,
    idx, spots, q_ref, o_ref, stats, k_here, k_there, v_here, v_there, dv_back, back, dk_there, dq_ref,
    k_all, v_all, k_rows, v_rows, acc, sems_k, sems_v, sem,
):
    task = pl.program_id(0) * KVH + pl.program_id(1)
    base = task * TOPK
    key_copies = slot_copies((k_here, k_there), k_all, sems_k)
    value_copies = slot_copies((v_here, v_there), v_all, sems_v)
    kept = [pltpu.make_async_copy(dv_back, back, sem)]
    on_first(task, key_copies + value_copies + kept, wait=False)
    on_first(task, key_copies, wait=True)
    gather_tiles(idx, base, k_all, k_rows)
    on_first(task, value_copies, wait=True)
    gather_tiles(idx, base, v_all, v_rows)
    q = heads(q_ref)
    scores = dot_nt(k_rows[...], q)
    probs = jnp.exp2((scores - stats[0, 0:1, :]) * SCALE_LOG2) * stats[0, 1:2, :]
    d_probs = dot_nt(v_rows[...], heads(o_ref))
    delta = jnp.sum(probs * d_probs, axis=0, keepdims=True)
    d_scores = (probs * (d_probs - delta)).astype(BF16)
    acc[...] = dot_nn(d_scores, q) * SCALE
    d_query = dot_nn(k_rows[...].T, d_scores).T * SCALE
    for z in range(GROUP):
        dq_ref[:, z * HD : (z + 1) * HD] = d_query[z * BLK : (z + 1) * BLK, :]
    on_first(task, kept, wait=True)
    store_tiles(idx, spots, base, acc, back, capacity, dk_there)


def second(idx, spots, capacity, queries, d_out, stats, k_here, k_there, v_here, v_there, dv_back):
    slots = k_here.shape[0]
    whole = pl.BlockSpec((slots, BLK, HD), lambda r, g: (0, 0, 0))
    both = pl.BlockSpec((2 * slots, BLK, HD), lambda r, g: (0, 0, 0))
    flops = 8 * QB_DEV * KVH * ROWS * SPAN * HD
    return pl.pallas_call(
        functools.partial(second_kernel, capacity),
        grid=(QB_DEV, KVH),
        out_shape=(
            jax.ShapeDtypeStruct((2 * slots, BLK, HD), BF16),
            jax.ShapeDtypeStruct((slots, BLK, HD), BF16),
            jax.ShapeDtypeStruct(queries.shape, F32),
        ),
        in_specs=[pl.BlockSpec(memory_space=SMEM)] * 2
        + task_specs()
        + [pl.BlockSpec((1, 8, ROWS), lambda r, g: (r * KVH + g, 0, 0))]
        + [pl.BlockSpec(memory_space=pl.ANY)] * 5,
        out_specs=(both, whole, pl.BlockSpec((BLK, GROUP * HD), lambda r, g: (r, g))),
        scratch_shapes=[
            VMEM((2 * slots, BLK, HD), BF16),
            VMEM((2 * slots, BLK, HD), BF16),
            VMEM((SPAN, HD), BF16),
            VMEM((SPAN, HD), BF16),
            VMEM((SPAN, HD), F32),
            pltpu.SemaphoreType.DMA((2,)),
            pltpu.SemaphoreType.DMA((2,)),
            pltpu.SemaphoreType.DMA,
        ],
        compiler_params=pltpu.CompilerParams(dimension_semantics=("arbitrary", "arbitrary")),
        cost_estimate=pl.CostEstimate(
            flops=flops, bytes_accessed=16 * slots * BLK * HD, transcendentals=QB_DEV * KVH * ROWS * SPAN
        ),
        name="second",
    )(idx, spots, queries, d_out, stats, k_here, k_there, v_here, v_there, dv_back)


def tables(selection, outer, inner, capacity, row, column):
    devices = outer * inner
    near = inner // 2
    half, place = column // near, column % near
    picks = selection.reshape(outer, 2, near, PICKS)
    mates = lax.dynamic_index_in_dim(picks, half, 1, keepdims=False).reshape(outer * near, PICKS)
    owners = row * inner + jnp.stack([half, 1 - half]) * near + place
    head = jnp.arange(PICKS, dtype=jnp.int32) // TOPK % KVH
    mine = mates[None] // KB_DEV == owners[:, None, None]
    positions = jnp.arange(PICKS, dtype=jnp.int32)
    before = (positions[:, None] < positions[None, :]).astype(BF16)
    ranks = jnp.dot(mine.astype(BF16), before, preferred_element_type=F32).astype(jnp.int32)
    copies = jnp.arange(capacity, dtype=jnp.int32)
    match = mine[:, :, None, :] & (ranks[:, :, None, :] == copies[None, None, :, None])
    codes = (mates % KB_DEV) * KVH + head[None] + 1
    tabs = jnp.sum(jnp.where(match, codes[None, :, None, :], 0), axis=3) - 1
    tabs = tabs.reshape(2, outer * near * capacity)
    myself = row * inner + column
    my_picks = lax.dynamic_index_in_dim(selection.reshape(devices, PICKS), myself, 0, keepdims=False)
    owner = my_picks // KB_DEV
    earlier = (owner[:, None] == owner[None, :]) & (positions[:, None] > positions[None, :])
    rank = jnp.sum(earlier.astype(jnp.int32), axis=1)
    across = (owner % inner // near != half).astype(jnp.int32)
    mate = owner // inner * near + owner % near
    slot = (across * outer * near + mate) * capacity + rank
    return tabs[0], tabs[1], slot, mate * 2 * capacity + rank


def body(queries, keys, values, d_out, selection):
    outer = lax.axis_size("cx")
    inner = lax.axis_size("cy")
    devices = outer * inner
    usable = devices * (KB_DEV - QB_DEV) // KB_DEV
    capacity = (PICKS + usable - 1) // usable
    near = inner // 2
    mates = outer * near
    tab_own, tab_far, slot, spots = tables(
        selection, outer, inner, capacity, lax.axis_index("cx"), lax.axis_index("cy")
    )
    groups = [
        [a * inner + half * near + b for a in range(outer) for b in range(near)] for half in (0, 1)
    ]

    edge = near // 2
    inside = [c for c in range(inner) if (c < near) == (c % near >= edge)]
    outside = [c for c in range(inner) if c not in inside]
    column = lax.axis_index("cy")
    from_inside = ((column >= near) == (column % near >= edge)).astype(jnp.int32).reshape(1)

    def across(x, back=False):
        parts = []
        for senders in (inside, outside):
            pairs = [
                (a * inner + i, a * inner + (i + near) % inner)
                for a in range(outer)
                for i in senders
                if a * inner + ((i + near) % inner if back else i) < usable
            ]
            parts.append(lax.ppermute(x, ("cx", "cy"), pairs))
        return parts

    def among(x, after=None):
        if after is not None:
            x = lax.optimization_barrier((x, after))[0]
        y = lax.all_to_all(
            x.reshape(mates, x.size // (mates * HD), HD),
            ("cx", "cy"),
            split_axis=0,
            concat_axis=0,
            tiled=True,
            axis_index_groups=groups,
        )
        return y.reshape(x.shape)

    far_keys = across(keys)
    far_values = across(values)
    k_here = among(pack(tab_own, keys))
    v_here = among(pack(tab_own, values), k_here)
    k_there = among(pack_far(tab_far, from_inside, *far_keys), v_here)
    v_there = among(pack_far(tab_far, from_inside, *far_values), k_there)
    dv_back, dv_there, stats = first(slot, spots, queries, d_out, k_here, k_there)
    dv_relay = among(dv_there, v_there)
    dv_far = across(relay(tab_far, dv_relay), back=True)
    back, dk_there, d_queries = second(
        slot, spots, capacity, queries, d_out, stats, k_here, k_there, v_here, v_there, dv_back
    )
    dk_relay = among(dk_there, dv_relay)
    dk_far = across(relay(tab_far, dk_relay), back=True)
    back = among(back, dk_relay)
    d_values, d_keys = finish(tab_own, capacity, back, dv_far, dk_far)
    return (d_queries, d_keys, d_values)


def solution(mesh):
    placed = (
        P(("cx", "cy"), None),
        P(("cx", "cy"), None),
        P(("cx", "cy"), None),
        P(("cx", "cy"), None),
        P(),
    )
    return jax.shard_map(
        body,
        mesh=mesh,
        in_specs=placed,
        out_specs=(P(("cx", "cy"), None), P(("cx", "cy"), None), P(("cx", "cy"), None)),
        check_vma=False,
    )
```

time: 405 us -> 379 us (0.936)
  blocking collectives: 60.2 us -> 30.4 us
  local copies, waits for them, and re-layouts: 13.7 us -> 7.44 us
  starting transfers between devices: 47.8 us -> 53.3 us
    all_to_all x2 -> x1, blocking collectives: 60.2 us -> 30.4 us  [among(): lax.all_to_all(x.reshape(mates, x.size // (mates * HD), HD), ('cx', 'cy')...]
    unnamed x35 -> x19, local copies, waits for them, and re-layouts: 13.2 us -> 6.95 us
    ppermute x6 -> x8, starting transfers between devices: 15.5 us -> 20.3 us  [across(): parts.append(lax.ppermute(x, ('cx', 'cy'), pairs))]
    ppermute x6 -> x8, waiting for transfers between devices: 179 us -> 181 us  [across(): parts.append(lax.ppermute(x, ('cx', 'cy'), pairs))]
    pallas_call x3 -> x2, Pallas kernels: 36.6 us -> 36.1 us  [the longest x1 29.4 us: second(): pl.pallas_call(functools.partial(second_kernel, capacity), grid=(QB_DEV,...]
  transfers between devices with their start and end apart: 12 -> 14, of which waited for: 7 -> 8; matrix products, arithmetic and copies ran while one was open for 0% -> 0% of each run, Pallas kernels for 18% -> 18%
where the time goes in v3:
time: 379 us; the launch traced here: 376 us
  waiting for transfers between devices  204 us (54%)
  Pallas kernels  77.5 us (20%)
  starting transfers between devices  53.3 us (14%)
  blocking collectives  30.4 us (8%)
  local copies, waits for them, and re-layouts  7.44 us (2%)
    ppermute x8, waiting for transfers between devices, across(): parts.append(lax.ppermute(x, ('cx', 'cy'), pairs))  181 us
    all_to_all x6, starting transfers between devices, among(): lax.all_to_all(x.reshape(mates, x.size // (mates * HD), HD), ('cx', 'cy')...  33 us
    all_to_all x1, blocking collectives, among(): lax.all_to_all(x.reshape(mates, x.size // (mates * HD), HD), ('cx', 'cy')...  30.4 us
    pallas_call x1, Pallas kernels, second(): pl.pallas_call(functools.partial(second_kernel, capacity), grid=(QB_DEV,...  29.4 us
    pallas_call x1, Pallas kernels, first(): pl.pallas_call(first_kernel, grid=(QB_DEV, KVH), out_shape=(jax.ShapeDtyp...  25.5 us
    all_to_all x6, waiting for transfers between devices, among(): lax.all_to_all(x.reshape(mates, x.size // (mates * HD), HD), ('cx', 'cy')...  22.9 us
    ppermute x8, starting transfers between devices, across(): parts.append(lax.ppermute(x, ('cx', 'cy'), pairs))  20.3 us
  transfers between devices with their start and end apart: 14, of which 8 were waited for; matrix products, arithmetic and copies ran while one was open for 0% of the time, Pallas kernels for 18%

profile of v3, /device:TPU:3, one launch (start us, length us, event | category | flops | bytes accessed | tf_op | source)
XLA Modules:
  0.0 375.6 jit_solution(11081428500888298365)
XLA Ops:
  0.7 0.9 copy.10
  1.6 0.2 reshape.238
  1.8 0.1 fusion.16
  1.9 0.1 broadcast_compare_fusion
  2.0 0.1 convolution_convert_fusion
  2.1 0.6 select_reduce_fusion
  2.8 0.1 squeeze.13.tab
  2.8 0.0 copy-start.3
  2.9 1.2 copy-done.3
  4.1 2.9 pack.2
  7.0 0.0 copy-start.5
  7.0 5.7 %all-to-all-start = ((bf16[16,512,128]{2,1,0:T(8,128)(2,1)}), bf16[16,512,128]{2,1,0:T(8,128)(2,1)S(1)}, u32[]{:S(2)}, u32[]{:S(2)}) async-start(bf16[16,512,128]{2,1,0:T(8,128)(2,1)} %bitcast.5), calls=%async_computation | async-start | bytes 4194304 | tf_op jit(solution)/shard_map/all_to_all | solution.py:380
  12.7 0.0 copy-done.5
  12.7 2.9 pack.3
  15.5 22.9 %all-to-all-done = bf16[16,512,128]{2,1,0:T(8,128)(2,1)S(1)} async-done(((bf16[16,512,128]{2,1,0:T(8,128)(2,1)}), bf16[16,512,128]{2,1,0:T(8,128)(2,1)S(1)}, u32[]{:S(2)}, u32[]{:S(2)}) %all-to-all-start) | async-done | bytes 2097184 | tf_op jit(solution)/shard_map/all_to_all | solution.py:380
  38.4 0.0 copy-start.7
  38.4 1.3 copy-done.7
  39.7 5.9 %all-to-all-start.1 = ((bf16[16,512,128]{2,1,0:T(8,128)(2,1)}), bf16[16,512,128]{2,1,0:T(8,128)(2,1)}, u32[]{:S(2)}, u32[]{:S(2)}) async-start(bf16[16,512,128]{2,1,0:T(8,128)(2,1)} %bitcast.8), calls=%async_computation.1 | async-start | bytes 4194304 | tf_op jit(solution)/shard_map/all_to_all | solution.py:380
  45.7 0.0 copy-done.4
  45.7 4.3 %collective-permute-start.1 = (bf16[1024,512]{1,0:T(8,128)(2,1)S(1)}, bf16[1024,512]{1,0:T(8,128)(2,1)S(1)}, u32[]{:S(2)}, u32[]{:S(2)}) collective-permute-start(bf16[1024,512]{1,0:T(8,128)(2,1)S(1)} %copy-done.4), channel_id=1, source_target_pairs={{0,4},{1,5},{6,2},{7,3},{8,12},{9,13},{14,10},{15,11},{16,20},{17,... | collective-permute-start | bytes 3145736 | tf_op jit(solution)/shard_map/ppermute | solution.py:374
  49.9 1.3 collective-permute-start
  51.3 0.1 squeeze.14.tab
  51.3 39.9 %collective-permute-done.1.outer_part = bf16[1024,512]{1,0:T(8,128)(2,1)S(1)} collective-permute-done((bf16[1024,512]{1,0:T(8,128)(2,1)S(1)}, bf16[1024,512]{1,0:T(8,128)(2,1)S(1)}, u32[]{:S(2)}, u32[]{:S(2)}) %collective-permute-start.1) | collective-permute-done | bytes 1048608 | tf_op jit(solution)/shard_map/ppermute | solution.py:374
  91.2 8.2 %collective-permute-done.inner_part = bf16[1024,512]{1,0:T(8,128)(2,1)S(1)} collective-permute-done((bf16[1024,512]{1,0:T(8,128)(2,1)S(1)}, bf16[1024,512]{1,0:T(8,128)(2,1)S(1)}, u32[]{:S(2)}, u32[]{:S(2)}) %collective-permute-start) | collective-permute-done | bytes 1048608 | tf_op jit(solution)/shard_map/ppermute | solution.py:374
  99.4 3.0 pack_far.2
  102.4 0.0 all-to-all-done.1
  102.4 0.0 copy-start.6
  102.4 5.1 %all-to-all-start.2 = ((bf16[16,512,128]{2,1,0:T(8,128)(2,1)}), bf16[16,512,128]{2,1,0:T(8,128)(2,1)S(1)}, u32[]{:S(2)}, u32[]{:S(2)}) async-start(bf16[16,512,128]{2,1,0:T(8,128)(2,1)} %bitcast.10), calls=%async_computation.2 | async-start | bytes 4194304 | tf_op jit(solution)/shard_map/all_to_all | solution.py:380
  107.5 0.0 copy-done.6
  107.5 2.3 collective-permute-start.3
  109.9 1.3 collective-permute-start.2
  111.2 41.9 %collective-permute-done.3.outer_part = bf16[1024,512]{1,0:T(8,128)(2,1)S(1)} collective-permute-done((bf16[1024,512]{1,0:T(8,128)(2,1)S(1)}, bf16[1024,512]{1,0:T(8,128)(2,1)S(1)}, u32[]{:S(2)}, u32[]{:S(2)}) %collective-permute-start.3) | collective-permute-done | bytes 1048608 | tf_op jit(solution)/shard_map/ppermute | solution.py:374
  153.1 6.2 %collective-permute-done.2.inner_part = bf16[1024,512]{1,0:T(8,128)(2,1)S(1)} collective-permute-done((bf16[1024,512]{1,0:T(8,128)(2,1)S(1)}, bf16[1024,512]{1,0:T(8,128)(2,1)S(1)}, u32[]{:S(2)}, u32[]{:S(2)}) %collective-permute-start.2) | collective-permute-done | bytes 1048608 | tf_op jit(solution)/shard_map/ppermute | solution.py:374
  159.3 3.0 pack_far.3
  162.2 0.0 all-to-all-done.2
  162.2 0.0 copy-start.8
  162.3 1.3 copy-done.8
  163.6 5.7 %all-to-all-start.3 = ((bf16[16,512,128]{2,1,0:T(8,128)(2,1)}), bf16[16,512,128]{2,1,0:T(8,128)(2,1)}, u32[]{:S(2)}, u32[]{:S(2)}) async-start(bf16[16,512,128]{2,1,0:T(8,128)(2,1)} %bitcast.12), calls=%async_computation.3 | async-start | bytes 4194304 | tf_op jit(solution)/shard_map/all_to_all | solution.py:380
  169.2 0.1 reshape.237
  169.4 0.2 convert_reduce_fusion
  169.6 0.6 multiply_add_fusion
  170.2 0.6 fusion.13.idx
  170.7 25.5 %first.1 = (bf16[256,64,128]{2,1,0:T(8,128)(2,1)}, bf16[128,64,128]{2,1,0:T(8,128)(2,1)}, f32[12,8,512]{2,1,0:T(8,128)}) custom-call(s32[192]{0:T(256)} %fusion.13.idx, s32[192]{0:T(256)} %get-tuple-element.31.spots, bf16[192,4096]{1,0:T(8,128)(2,1)} %q_ref.3, bf16[192,4096]{1,0:T(8,128)(2,1)} %o_ref.3, bf16[128,64,128]{2,1,0:T(8,128)(2,1)} %bitcast.26, ...), custom_call_target="tpu_custom_call" | custom-call | flops 3221225472 | bytes 8388608 | tf_op jit(solution)/shard_map/first/pallas_call | solution.py:225
  196.3 0.0 all-to-all-done.3
  196.3 5.2 %all-to-all-start.4 = ((bf16[16,512,128]{2,1,0:T(8,128)(2,1)}), bf16[16,512,128]{2,1,0:T(8,128)(2,1)S(1)}, u32[]{:S(2)}, u32[]{:S(2)}) async-start(bf16[16,512,128]{2,1,0:T(8,128)(2,1)} %bitcast.30), calls=%async_computation.4 | async-start | bytes 4194304 | tf_op jit(solution)/shard_map/all_to_all | solution.py:380
  201.5 29.4 %second.1 = (bf16[256,64,128]{2,1,0:T(8,128)(2,1)}, bf16[128,64,128]{2,1,0:T(8,128)(2,1)}, f32[192,4096]{1,0:T(8,128)}) custom-call(s32[192]{0:T(256)} %fusion.13.idx, s32[192]{0:T(256)} %get-tuple-element.31.spots, bf16[192,4096]{1,0:T(8,128)(2,1)} %q_ref.3, bf16[192,4096]{1,0:T(8,128)(2,1)} %o_ref.3, f32[12,8,512]{2,1,0:T(8,128)} %get-tuple-element.19.stats, ...), custom_call_target="tpu_custom_call" | custom-call | flops 6442450944 | bytes 16777216 | tf_op jit(solution)/shard_map/second/pallas_call | solution.py:285
  230.8 0.0 all-to-all-done.4
  230.8 30.4 %all_to_all.35 = bf16[16,512,128]{2,1,0:T(8,128)(2,1)} all-to-all(bf16[16,512,128]{2,1,0:T(8,128)(2,1)} %bitcast.31), channel_id=1, replica_groups={{0,1,2,3,8,9,10,11,16,17,18,19,24,25,26,27},{4,5,6,7,12,13,14,15,20,21,..., dimensions={0} | all-to-all | bytes 4194304 | tf_op jit(solution)/shard_map/all_to_all | solution.py:380
  261.3 5.4 %all-to-all-start.6 = ((bf16[16,1024,128]{2,1,0:T(8,128)(2,1)}), bf16[16,1024,128]{2,1,0:T(8,128)(2,1)}, u32[]{:S(2)}, u32[]{:S(2)}) async-start(bf16[16,1024,128]{2,1,0:T(8,128)(2,1)} %bitcast.25), calls=%async_computation.6 | async-start | bytes 8388608 | tf_op jit(solution)/shard_map/all_to_all | solution.py:380
  266.7 2.1 relay.2
  268.8 3.5 collective-permute-start.5
  272.3 1.3 collective-permute-start.4
  273.6 0.0 copy-done
  273.6 2.1 relay.3
  275.7 5.0 %collective-permute-start.7 = (bf16[1024,512]{1,0:T(8,128)(2,1)S(1)}, bf16[1024,512]{1,0:T(8,128)(2,1)S(1)}, u32[]{:S(2)}, u32[]{:S(2)}) collective-permute-start(bf16[1024,512]{1,0:T(8,128)(2,1)S(1)} %relay.3), channel_id=1, source_target_pairs={{0,4},{1,5},{6,2},{7,3},{8,12},{9,13},{14,10},{15,11},{16,20},{17,... | collective-permute-start | bytes 3145736 | tf_op jit(solution)/shard_map/ppermute | solution.py:374
  280.8 1.3 collective-permute-start.6
  282.1 55.0 %collective-permute-done.5.dv_outer = bf16[1024,512]{1,0:T(8,128)(2,1)S(1)} collective-permute-done((bf16[1024,512]{1,0:T(8,128)(2,1)S(1)}, bf16[1024,512]{1,0:T(8,128)(2,1)S(1)}, u32[]{:S(2)}, u32[]{:S(2)}) %collective-permute-start.5) | collective-permute-done | bytes 1048608 | tf_op jit(solution)/shard_map/ppermute | solution.py:374
  337.0 0.0 collective-permute-done.4.dv_inner
  337.1 22.5 %collective-permute-done.7.dk_outer = bf16[1024,512]{1,0:T(8,128)(2,1)S(1)} collective-permute-done((bf16[1024,512]{1,0:T(8,128)(2,1)S(1)}, bf16[1024,512]{1,0:T(8,128)(2,1)S(1)}, u32[]{:S(2)}, u32[]{:S(2)}) %collective-permute-start.7) | collective-permute-done | bytes 1048608 | tf_op jit(solution)/shard_map/ppermute | solution.py:374
  359.5 7.2 %collective-permute-done.6.dk_inner = bf16[1024,512]{1,0:T(8,128)(2,1)S(1)} collective-permute-done((bf16[1024,512]{1,0:T(8,128)(2,1)S(1)}, bf16[1024,512]{1,0:T(8,128)(2,1)S(1)}, u32[]{:S(2)}, u32[]{:S(2)}) %collective-permute-start.6) | collective-permute-done | bytes 1048608 | tf_op jit(solution)/shard_map/ppermute | solution.py:374
  366.7 1.0 copy-done.1
  367.7 0.0 all-to-all-done.6
  367.7 1.2 copy-done.2
  368.9 6.7 %finish.1 = (f32[1024,512]{1,0:T(8,128)}, f32[1024,512]{1,0:T(8,128)}) custom-call(s32[128]{0:T(128)S(1)} %squeeze.13.tab, bf16[256,64,128]{2,1,0:T(8,128)(2,1)} %bitcast.19.back, bf16[1024,512]{1,0:T(8,128)(2,1)S(1)} %collective-permute-done.4.dv_inner, bf16[1024,512]{1,0:T(8,128)(2,1)S(1)} %collective-permute-done.5.dv_outer, ...), custom_call_target="tpu_custom_call" | custom-call | flops 8000000 | bytes 12000000 | tf_op jit(solution)/shard_map/finish/pallas_call | solution.py:135
  (12 shorter events, 0.1 us)
Async XLA Ops:
  2.8 1.2 copy-start.3
  7.0 5.7 %copy-start.5 = (bf16[1024,512]{1,0:T(8,128)(2,1)S(1)}, bf16[1024,512]{1,0:T(8,128)(2,1)}, u32[]{:S(2)}) copy-start(bf16[1024,512]{1,0:T(8,128)(2,1)} %shard.3) | copy-start | bytes 3145732
  7.0 31.5 %all-to-all-start = ((bf16[16,512,128]{2,1,0:T(8,128)(2,1)}), bf16[16,512,128]{2,1,0:T(8,128)(2,1)S(1)}, u32[]{:S(2)}, u32[]{:S(2)}) async-start(bf16[16,512,128]{2,1,0:T(8,128)(2,1)} %bitcast.5), calls=%async_computation | async-start | bytes 4194304 | tf_op jit(solution)/shard_map/all_to_all | solution.py:380
  38.4 1.3 copy-start.7
  39.7 5.9 %copy-start.4 = (bf16[1024,512]{1,0:T(8,128)(2,1)S(1)}, bf16[1024,512]{1,0:T(8,128)(2,1)}, u32[]{:S(2)}) copy-start(bf16[1024,512]{1,0:T(8,128)(2,1)} %shard.2) | copy-start | bytes 3145732
  39.7 62.6 %all-to-all-start.1 = ((bf16[16,512,128]{2,1,0:T(8,128)(2,1)}), bf16[16,512,128]{2,1,0:T(8,128)(2,1)}, u32[]{:S(2)}, u32[]{:S(2)}) async-start(bf16[16,512,128]{2,1,0:T(8,128)(2,1)} %bitcast.8), calls=%async_computation.1 | async-start | bytes 4194304 | tf_op jit(solution)/shard_map/all_to_all | solution.py:380
  45.7 45.6 %collective-permute-start.1 = (bf16[1024,512]{1,0:T(8,128)(2,1)S(1)}, bf16[1024,512]{1,0:T(8,128)(2,1)S(1)}, u32[]{:S(2)}, u32[]{:S(2)}) collective-permute-start(bf16[1024,512]{1,0:T(8,128)(2,1)S(1)} %copy-done.4), channel_id=1, source_target_pairs={{0,4},{1,5},{6,2},{7,3},{8,12},{9,13},{14,10},{15,11},{16,20},{17,... | collective-permute-start | bytes 3145736 | tf_op jit(solution)/shard_map/ppermute | solution.py:374
  49.9 49.4 %collective-permute-start = (bf16[1024,512]{1,0:T(8,128)(2,1)S(1)}, bf16[1024,512]{1,0:T(8,128)(2,1)S(1)}, u32[]{:S(2)}, u32[]{:S(2)}) collective-permute-start(bf16[1024,512]{1,0:T(8,128)(2,1)S(1)} %copy-done.4), channel_id=1, source_target_pairs={{2,6},{3,7},{4,0},{5,1},{10,14},{11,15},{12,8},{13,9},{18,22},{19,... | collective-permute-start | bytes 3145736 | tf_op jit(solution)/shard_map/ppermute | solution.py:374
  102.4 5.1 %copy-start.6 = (bf16[1024,512]{1,0:T(8,128)(2,1)S(1)}, bf16[1024,512]{1,0:T(8,128)(2,1)}, u32[]{:S(2)}) copy-start(bf16[1024,512]{1,0:T(8,128)(2,1)} %shard.3) | copy-start | bytes 3145732
  102.4 59.9 %all-to-all-start.2 = ((bf16[16,512,128]{2,1,0:T(8,128)(2,1)}), bf16[16,512,128]{2,1,0:T(8,128)(2,1)S(1)}, u32[]{:S(2)}, u32[]{:S(2)}) async-start(bf16[16,512,128]{2,1,0:T(8,128)(2,1)} %bitcast.10), calls=%async_computation.2 | async-start | bytes 4194304 | tf_op jit(solution)/shard_map/all_to_all | solution.py:380
  107.5 45.6 %collective-permute-start.3 = (bf16[1024,512]{1,0:T(8,128)(2,1)S(1)}, bf16[1024,512]{1,0:T(8,128)(2,1)S(1)}, u32[]{:S(2)}, u32[]{:S(2)}) collective-permute-start(bf16[1024,512]{1,0:T(8,128)(2,1)S(1)} %copy-done.6), channel_id=1, source_target_pairs={{0,4},{1,5},{6,2},{7,3},{8,12},{9,13},{14,10},{15,11},{16,20},{17,... | collective-permute-start | bytes 3145736 | tf_op jit(solution)/shard_map/ppermute | solution.py:374
  109.9 49.4 %collective-permute-start.2 = (bf16[1024,512]{1,0:T(8,128)(2,1)S(1)}, bf16[1024,512]{1,0:T(8,128)(2,1)S(1)}, u32[]{:S(2)}, u32[]{:S(2)}) collective-permute-start(bf16[1024,512]{1,0:T(8,128)(2,1)S(1)} %copy-done.6), channel_id=1, source_target_pairs={{2,6},{3,7},{4,0},{5,1},{10,14},{11,15},{12,8},{13,9},{18,22},{19,... | collective-permute-start | bytes 3145736 | tf_op jit(solution)/shard_map/ppermute | solution.py:374
  162.2 1.3 copy-start.8
  163.6 32.7 %all-to-all-start.3 = ((bf16[16,512,128]{2,1,0:T(8,128)(2,1)}), bf16[16,512,128]{2,1,0:T(8,128)(2,1)}, u32[]{:S(2)}, u32[]{:S(2)}) async-start(bf16[16,512,128]{2,1,0:T(8,128)(2,1)} %bitcast.12), calls=%async_computation.3 | async-start | bytes 4194304 | tf_op jit(solution)/shard_map/all_to_all | solution.py:380
  196.3 34.5 %all-to-all-start.4 = ((bf16[16,512,128]{2,1,0:T(8,128)(2,1)}), bf16[16,512,128]{2,1,0:T(8,128)(2,1)S(1)}, u32[]{:S(2)}, u32[]{:S(2)}) async-start(bf16[16,512,128]{2,1,0:T(8,128)(2,1)} %bitcast.30), calls=%async_computation.4 | async-start | bytes 4194304 | tf_op jit(solution)/shard_map/all_to_all | solution.py:380
  261.3 106.4 %all-to-all-start.6 = ((bf16[16,1024,128]{2,1,0:T(8,128)(2,1)}), bf16[16,1024,128]{2,1,0:T(8,128)(2,1)}, u32[]{:S(2)}, u32[]{:S(2)}) async-start(bf16[16,1024,128]{2,1,0:T(8,128)(2,1)} %bitcast.25), calls=%async_computation.6 | async-start | bytes 8388608 | tf_op jit(solution)/shard_map/all_to_all | solution.py:380
  266.7 6.9 %copy-start = (bf16[16,512,128]{2,1,0:T(8,128)(2,1)S(1)}, bf16[16,512,128]{2,1,0:T(8,128)(2,1)}, u32[]{:S(2)}) copy-start(bf16[16,512,128]{2,1,0:T(8,128)(2,1)} %all_to_all.35) | copy-start | bytes 6291460
  268.8 68.3 %collective-permute-start.5 = (bf16[1024,512]{1,0:T(8,128)(2,1)S(1)}, bf16[1024,512]{1,0:T(8,128)(2,1)S(1)}, u32[]{:S(2)}, u32[]{:S(2)}) collective-permute-start(bf16[1024,512]{1,0:T(8,128)(2,1)S(1)} %relay.2), channel_id=1, source_target_pairs={{0,4},{1,5},{6,2},{7,3},{8,12},{9,13},{14,10},{15,11},{16,20},{17,... | collective-permute-start | bytes 3145736 | tf_op jit(solution)/shard_map/ppermute | solution.py:374
  272.3 64.7 %collective-permute-start.4 = (bf16[1024,512]{1,0:T(8,128)(2,1)S(1)}, bf16[1024,512]{1,0:T(8,128)(2,1)S(1)}, u32[]{:S(2)}, u32[]{:S(2)}) collective-permute-start(bf16[1024,512]{1,0:T(8,128)(2,1)S(1)} %relay.2), channel_id=1, source_target_pairs={{2,6},{3,7},{4,0},{5,1},{10,14},{11,15},{12,8},{13,9},{18,22},{19,... | collective-permute-start | bytes 3145736 | tf_op jit(solution)/shard_map/ppermute | solution.py:374
  275.7 83.8 %collective-permute-start.7 = (bf16[1024,512]{1,0:T(8,128)(2,1)S(1)}, bf16[1024,512]{1,0:T(8,128)(2,1)S(1)}, u32[]{:S(2)}, u32[]{:S(2)}) collective-permute-start(bf16[1024,512]{1,0:T(8,128)(2,1)S(1)} %relay.3), channel_id=1, source_target_pairs={{0,4},{1,5},{6,2},{7,3},{8,12},{9,13},{14,10},{15,11},{16,20},{17,... | collective-permute-start | bytes 3145736 | tf_op jit(solution)/shard_map/ppermute | solution.py:374
  280.8 85.9 %collective-permute-start.6 = (bf16[1024,512]{1,0:T(8,128)(2,1)S(1)}, bf16[1024,512]{1,0:T(8,128)(2,1)S(1)}, u32[]{:S(2)}, u32[]{:S(2)}) collective-permute-start(bf16[1024,512]{1,0:T(8,128)(2,1)S(1)} %relay.3), channel_id=1, source_target_pairs={{2,6},{3,7},{4,0},{5,1},{10,14},{11,15},{12,8},{13,9},{18,22},{19,... | collective-permute-start | bytes 3145736 | tf_op jit(solution)/shard_map/ppermute | solution.py:374
  366.7 1.0 copy-start.1
  367.7 1.2 copy-start.2

commit v4 on v3

--- a/solution.py
+++ b/solution.py
@@ -166,19 +166,29 @@
         dest[pick * BLK : (pick + 1) * BLK, :] = table[idx[base + pick]]
 
 
-def store_tiles(idx, spots, base, tiles, back, shift, there):
+def store_tiles(idx, base, tiles, table):
+    for pick in range(TOPK):
+        table[idx[base + pick]] = tiles[pick * BLK : (pick + 1) * BLK, :].astype(BF16)
+
+
+def flush(task, table, back, shift, capacity, there, sems):
     size = there.shape[0]
-    for pick in range(TOPK):
-        spot = idx[base + pick]
-        tile = tiles[pick * BLK : (pick + 1) * BLK, :].astype(BF16)
-
-        @pl.when(spot < size)
-        def _():
-            back[spots[base + pick] + shift] = tile
-
-        @pl.when(spot >= size)
-        def _():
-            there[spot - size] = tile
+    copies = [
+        pltpu.make_async_copy(
+            table.at[pl.ds(mate * capacity, capacity)],
+            back.at[pl.ds(mate * 2 * capacity + shift, capacity)],
+            sems.at[mate],
+        )
+        for mate in range(size // capacity)
+    ]
+    copies.append(pltpu.make_async_copy(table.at[pl.ds(size, size)], there, sems.at[size // capacity]))
+
+    @pl.when(task == QB_DEV * KVH - 1)
+    def _():
+        for copy in copies:
+            copy.start()
+        for copy in copies:
+            copy.wait()
 
 
 def heads(ref):
@@ -193,7 +203,9 @@
     return lax.dot_general(a, b, (((1,), (0,)), ((), ())), preferred_element_type=F32)
 
 
-def first_kernel(idx, spots, q_ref, o_ref, k_here, k_there, back, dv_there, stats, k_all, k_rows, acc, sems):
+def first_kernel(
+    capacity, idx, q_ref, o_ref, k_here, k_there, back, dv_there, stats, k_all, k_rows, acc, sent, sems, sems_out
+):
     task = pl.program_id(0) * KVH + pl.program_id(1)
     base = task * TOPK
     key_copies = slot_copies((k_here, k_there), k_all, sems)
@@ -207,7 +219,8 @@
     stats[0, 0:1, :] = top
     stats[0, 1:2, :] = inverse
     acc[...] = dot_nn((weights * inverse).astype(BF16), heads(o_ref))
-    store_tiles(idx, spots, base, acc, back, 0, dv_there)
+    store_tiles(idx, base, acc, sent)
+    flush(task, sent, back, 0, capacity, dv_there, sems_out)
 
 
 def task_specs():
@@ -217,48 +230,48 @@
     ]
 
 
-def first(idx, spots, queries, d_out, k_here, k_there):
+def first(idx, capacity, queries, d_out, k_here, k_there):
     slots = k_here.shape[0]
-    whole = pl.BlockSpec((slots, BLK, HD), lambda r, g: (0, 0, 0))
-    both = pl.BlockSpec((2 * slots, BLK, HD), lambda r, g: (0, 0, 0))
+    held = pl.BlockSpec(memory_space=pl.ANY)
     flops = 4 * QB_DEV * KVH * ROWS * SPAN * HD
     return pl.pallas_call(
-        first_kernel,
+        functools.partial(first_kernel, capacity),
         grid=(QB_DEV, KVH),
         out_shape=(
             jax.ShapeDtypeStruct((2 * slots, BLK, HD), BF16),
             jax.ShapeDtypeStruct((slots, BLK, HD), BF16),
             jax.ShapeDtypeStruct((QB_DEV * KVH, 8, ROWS), F32),
         ),
-        in_specs=[pl.BlockSpec(memory_space=SMEM)] * 2
+        in_specs=[pl.BlockSpec(memory_space=SMEM)]
         + task_specs()
         + [pl.BlockSpec(memory_space=pl.ANY), pl.BlockSpec(memory_space=pl.ANY)],
-        out_specs=(both, whole, pl.BlockSpec((1, 8, ROWS), lambda r, g: (r * KVH + g, 0, 0))),
+        out_specs=(held, held, pl.BlockSpec((1, 8, ROWS), lambda r, g: (r * KVH + g, 0, 0))),
         scratch_shapes=[
             VMEM((2 * slots, BLK, HD), BF16),
             VMEM((SPAN, HD), BF16),
             VMEM((SPAN, HD), F32),
+            VMEM((2 * slots, BLK, HD), BF16),
             pltpu.SemaphoreType.DMA((2,)),
+            pltpu.SemaphoreType.DMA((slots // capacity + 1,)),
         ],
         compiler_params=pltpu.CompilerParams(dimension_semantics=("arbitrary", "arbitrary")),
         cost_estimate=pl.CostEstimate(
             flops=flops, bytes_accessed=8 * slots * BLK * HD, transcendentals=QB_DEV * KVH * ROWS * SPAN
         ),
         name="first",
-    )(idx, spots, queries, d_out, k_here, k_there)
+    )(idx, queries, d_out, k_here, k_there)
 
 
 def second_kernel(
     capacity,
-    idx, spots, q_ref, o_ref, stats, k_here, k_there, v_here, v_there, dv_back, back, dk_there, dq_ref,
-    k_all, v_all, k_rows, v_rows, acc, sems_k, sems_v, sem,
+    idx, q_ref, o_ref, stats, k_here, k_there, v_here, v_there, dv_back, back, dk_there, dq_ref,
+    k_all, v_all, k_rows, v_rows, acc, sent, sems_k, sems_v, sems_out,
 ):
     task = pl.program_id(0) * KVH + pl.program_id(1)
     base = task * TOPK
     key_copies = slot_copies((k_here, k_there), k_all, sems_k)
     value_copies = slot_copies((v_here, v_there), v_all, sems_v)
-    kept = [pltpu.make_async_copy(dv_back, back, sem)]
-    on_first(task, key_copies + value_copies + kept, wait=False)
+    on_first(task, key_copies + value_copies, wait=False)
     on_first(task, key_copies, wait=True)
     gather_tiles(idx, base, k_all, k_rows)
     on_first(task, value_copies, wait=True)
@@ -273,14 +286,13 @@
     d_query = dot_nn(k_rows[...].T, d_scores).T * SCALE
     for z in range(GROUP):
         dq_ref[:, z * HD : (z + 1) * HD] = d_query[z * BLK : (z + 1) * BLK, :]
-    on_first(task, kept, wait=True)
-    store_tiles(idx, spots, base, acc, back, capacity, dk_there)
-
-
-def second(idx, spots, capacity, queries, d_out, stats, k_here, k_there, v_here, v_there, dv_back):
+    store_tiles(idx, base, acc, sent)
+    flush(task, sent, back, capacity, capacity, dk_there, sems_out)
+
+
+def second(idx, capacity, queries, d_out, stats, k_here, k_there, v_here, v_there, dv_back):
     slots = k_here.shape[0]
-    whole = pl.BlockSpec((slots, BLK, HD), lambda r, g: (0, 0, 0))
-    both = pl.BlockSpec((2 * slots, BLK, HD), lambda r, g: (0, 0, 0))
+    held = pl.BlockSpec(memory_space=pl.ANY)
     flops = 8 * QB_DEV * KVH * ROWS * SPAN * HD
     return pl.pallas_call(
         functools.partial(second_kernel, capacity),
@@ -290,27 +302,29 @@
             jax.ShapeDtypeStruct((slots, BLK, HD), BF16),
             jax.ShapeDtypeStruct(queries.shape, F32),
         ),
-        in_specs=[pl.BlockSpec(memory_space=SMEM)] * 2
+        in_specs=[pl.BlockSpec(memory_space=SMEM)]
         + task_specs()
         + [pl.BlockSpec((1, 8, ROWS), lambda r, g: (r * KVH + g, 0, 0))]
         + [pl.BlockSpec(memory_space=pl.ANY)] * 5,
-        out_specs=(both, whole, pl.BlockSpec((BLK, GROUP * HD), lambda r, g: (r, g))),
+        out_specs=(held, held, pl.BlockSpec((BLK, GROUP * HD), lambda r, g: (r, g))),
         scratch_shapes=[
             VMEM((2 * slots, BLK, HD), BF16),
             VMEM((2 * slots, BLK, HD), BF16),
             VMEM((SPAN, HD), BF16),
             VMEM((SPAN, HD), BF16),
             VMEM((SPAN, HD), F32),
+            VMEM((2 * slots, BLK, HD), BF16),
             pltpu.SemaphoreType.DMA((2,)),
             pltpu.SemaphoreType.DMA((2,)),
-            pltpu.SemaphoreType.DMA,
+            pltpu.SemaphoreType.DMA((slots // capacity + 1,)),
         ],
+        input_output_aliases={8: 0},
         compiler_params=pltpu.CompilerParams(dimension_semantics=("arbitrary", "arbitrary")),
         cost_estimate=pl.CostEstimate(
             flops=flops, bytes_accessed=16 * slots * BLK * HD, transcendentals=QB_DEV * KVH * ROWS * SPAN
         ),
         name="second",
-    )(idx, spots, queries, d_out, stats, k_here, k_there, v_here, v_there, dv_back)
+    )(idx, queries, d_out, stats, k_here, k_there, v_here, v_there, dv_back)
 
 
 def tables(selection, outer, inner, capacity, row, column):
@@ -338,7 +352,7 @@
     across = (owner % inner // near != half).astype(jnp.int32)
     mate = owner // inner * near + owner % near
     slot = (across * outer * near + mate) * capacity + rank
-    return tabs[0], tabs[1], slot, mate * 2 * capacity + rank
+    return tabs[0], tabs[1], slot
 
 
 def body(queries, keys, values, d_out, selection):
@@ -349,7 +363,7 @@
     capacity = (PICKS + usable - 1) // usable
     near = inner // 2
     mates = outer * near
-    tab_own, tab_far, slot, spots = tables(
+    tab_own, tab_far, slot = tables(
         selection, outer, inner, capacity, lax.axis_index("cx"), lax.axis_index("cy")
     )
     groups = [
@@ -393,12 +407,10 @@
     v_here = among(pack(tab_own, values), k_here)
     k_there = among(pack_far(tab_far, from_inside, *far_keys), v_here)
     v_there = among(pack_far(tab_far, from_inside, *far_values), k_there)
-    dv_back, dv_there, stats = first(slot, spots, queries, d_out, k_here, k_there)
+    dv_back, dv_there, stats = first(slot, capacity, queries, d_out, k_here, k_there)
     dv_relay = among(dv_there, v_there)
     dv_far = across(relay(tab_far, dv_relay), back=True)
-    back, dk_there, d_queries = second(
-        slot, spots, capacity, queries, d_out, stats, k_here, k_there, v_here, v_there, dv_back
-    )
+    back, dk_there, d_queries = second(slot, capacity, queries, d_out, stats, k_here, k_there, v_here, v_there, dv_back)
     dk_relay = among(dk_there, dv_relay)
     dk_far = across(relay(tab_far, dk_relay), back=True)
     back = among(back, dk_relay)

time: 379 us -> 375 us (0.989)
  Pallas kernels: 77.5 us -> 72 us
  transfers between devices with their start and end apart: 14 -> 14, of which waited for: 8 -> 9; matrix products, arithmetic and copies ran while one was open for 0% -> 0% of each run, Pallas kernels for 18% -> 17%
where the time goes in v4:
time: 375 us; the launch traced here: 371 us
  waiting for transfers between devices  205 us (55%)
  Pallas kernels  72 us (19%)
  starting transfers between devices  53.3 us (14%)
  blocking collectives  30.9 us (8%)
  local copies, waits for them, and re-layouts  7.44 us (2%)
    ppermute x8, waiting for transfers between devices, across(): parts.append(lax.ppermute(x, ('cx', 'cy'), pairs))  181 us
    all_to_all x6, starting transfers between devices, among(): lax.all_to_all(x.reshape(mates, x.size // (mates * HD), HD), ('cx', 'cy')...  32.9 us
    all_to_all x1, blocking collectives, among(): lax.all_to_all(x.reshape(mates, x.size // (mates * HD), HD), ('cx', 'cy')...  30.9 us
    pallas_call x1, Pallas kernels, second(): pl.pallas_call(functools.partial(second_kernel, capacity), grid=(QB_DEV,...  25.9 us
    all_to_all x6, waiting for transfers between devices, among(): lax.all_to_all(x.reshape(mates, x.size // (mates * HD), HD), ('cx', 'cy')...  24.4 us
    pallas_call x1, Pallas kernels, first(): pl.pallas_call(functools.partial(first_kernel, capacity), grid=(QB_DEV, K...  23.4 us
    ppermute x8, starting transfers between devices, across(): parts.append(lax.ppermute(x, ('cx', 'cy'), pairs))  20.4 us
  transfers between devices with their start and end apart: 14, of which 9 were waited for; matrix products, arithmetic and copies ran while one was open for 0% of the time, Pallas kernels for 17%

profile of v4, /device:TPU:3, one launch (start us, length us, event | category | flops | bytes accessed | tf_op | source)
XLA Modules:
  0.0 371.5 jit_solution(6356383903120078007)
XLA Ops:
  0.7 0.9 copy.11
  1.6 0.2 reshape.238
  1.8 0.1 fusion.14
  1.9 0.1 broadcast_compare_fusion
  2.0 0.1 convolution_convert_fusion
  2.1 0.6 select_reduce_fusion
  2.8 0.1 squeeze.13.tab
  2.8 0.0 copy-start.3
  2.9 1.2 copy-done.3
  4.1 2.9 pack.2
  7.0 0.0 copy-start.5
  7.0 5.7 %all-to-all-start = ((bf16[16,512,128]{2,1,0:T(8,128)(2,1)}), bf16[16,512,128]{2,1,0:T(8,128)(2,1)S(1)}, u32[]{:S(2)}, u32[]{:S(2)}) async-start(bf16[16,512,128]{2,1,0:T(8,128)(2,1)} %bitcast.5), calls=%async_computation | async-start | bytes 4194304 | tf_op jit(solution)/shard_map/all_to_all | solution.py:394
  12.7 0.0 copy-done.5
  12.7 2.9 pack.3
  15.5 22.9 %all-to-all-done = bf16[16,512,128]{2,1,0:T(8,128)(2,1)S(1)} async-done(((bf16[16,512,128]{2,1,0:T(8,128)(2,1)}), bf16[16,512,128]{2,1,0:T(8,128)(2,1)S(1)}, u32[]{:S(2)}, u32[]{:S(2)}) %all-to-all-start) | async-done | bytes 2097184 | tf_op jit(solution)/shard_map/all_to_all | solution.py:394
  38.4 0.0 copy-start.7
  38.4 1.3 copy-done.7
  39.7 0.0 copy-start.4
  39.7 5.9 %all-to-all-start.1 = ((bf16[16,512,128]{2,1,0:T(8,128)(2,1)}), bf16[16,512,128]{2,1,0:T(8,128)(2,1)}, u32[]{:S(2)}, u32[]{:S(2)}) async-start(bf16[16,512,128]{2,1,0:T(8,128)(2,1)} %bitcast.8), calls=%async_computation.1 | async-start | bytes 4194304 | tf_op jit(solution)/shard_map/all_to_all | solution.py:394
  45.6 0.0 copy-done.4
  45.7 4.3 %collective-permute-start.1 = (bf16[1024,512]{1,0:T(8,128)(2,1)S(1)}, bf16[1024,512]{1,0:T(8,128)(2,1)S(1)}, u32[]{:S(2)}, u32[]{:S(2)}) collective-permute-start(bf16[1024,512]{1,0:T(8,128)(2,1)S(1)} %copy-done.4), channel_id=1, source_target_pairs={{0,4},{1,5},{6,2},{7,3},{8,12},{9,13},{14,10},{15,11},{16,20},{17,... | collective-permute-start | bytes 3145736 | tf_op jit(solution)/shard_map/ppermute | solution.py:388
  49.9 1.3 collective-permute-start
  51.3 0.1 squeeze.14.tab
  51.3 39.9 %collective-permute-done.1.outer_part = bf16[1024,512]{1,0:T(8,128)(2,1)S(1)} collective-permute-done((bf16[1024,512]{1,0:T(8,128)(2,1)S(1)}, bf16[1024,512]{1,0:T(8,128)(2,1)S(1)}, u32[]{:S(2)}, u32[]{:S(2)}) %collective-permute-start.1) | collective-permute-done | bytes 1048608 | tf_op jit(solution)/shard_map/ppermute | solution.py:388
  91.2 8.2 %collective-permute-done.inner_part = bf16[1024,512]{1,0:T(8,128)(2,1)S(1)} collective-permute-done((bf16[1024,512]{1,0:T(8,128)(2,1)S(1)}, bf16[1024,512]{1,0:T(8,128)(2,1)S(1)}, u32[]{:S(2)}, u32[]{:S(2)}) %collective-permute-start) | collective-permute-done | bytes 1048608 | tf_op jit(solution)/shard_map/ppermute | solution.py:388
  99.4 3.0 pack_far.2
  102.3 0.0 all-to-all-done.1
  102.4 0.0 copy-start.6
  102.4 5.1 %all-to-all-start.2 = ((bf16[16,512,128]{2,1,0:T(8,128)(2,1)}), bf16[16,512,128]{2,1,0:T(8,128)(2,1)S(1)}, u32[]{:S(2)}, u32[]{:S(2)}) async-start(bf16[16,512,128]{2,1,0:T(8,128)(2,1)} %bitcast.10), calls=%async_computation.2 | async-start | bytes 4194304 | tf_op jit(solution)/shard_map/all_to_all | solution.py:394
  107.5 0.0 copy-done.6
  107.5 2.3 collective-permute-start.3
  109.8 1.3 collective-permute-start.2
  111.1 41.9 %collective-permute-done.3.outer_part = bf16[1024,512]{1,0:T(8,128)(2,1)S(1)} collective-permute-done((bf16[1024,512]{1,0:T(8,128)(2,1)S(1)}, bf16[1024,512]{1,0:T(8,128)(2,1)S(1)}, u32[]{:S(2)}, u32[]{:S(2)}) %collective-permute-start.3) | collective-permute-done | bytes 1048608 | tf_op jit(solution)/shard_map/ppermute | solution.py:388
  153.1 6.2 %collective-permute-done.2.inner_part = bf16[1024,512]{1,0:T(8,128)(2,1)S(1)} collective-permute-done((bf16[1024,512]{1,0:T(8,128)(2,1)S(1)}, bf16[1024,512]{1,0:T(8,128)(2,1)S(1)}, u32[]{:S(2)}, u32[]{:S(2)}) %collective-permute-start.2) | collective-permute-done | bytes 1048608 | tf_op jit(solution)/shard_map/ppermute | solution.py:388
  159.2 3.0 pack_far.3
  162.2 0.0 all-to-all-done.2
  162.2 0.0 copy-start.8
  162.2 1.3 copy-done.8
  163.6 5.7 %all-to-all-start.3 = ((bf16[16,512,128]{2,1,0:T(8,128)(2,1)}), bf16[16,512,128]{2,1,0:T(8,128)(2,1)}, u32[]{:S(2)}, u32[]{:S(2)}) async-start(bf16[16,512,128]{2,1,0:T(8,128)(2,1)} %bitcast.12), calls=%async_computation.3 | async-start | bytes 4194304 | tf_op jit(solution)/shard_map/all_to_all | solution.py:394
  169.2 0.1 reshape.237
  169.4 0.2 convert_reduce_fusion
  169.6 0.6 multiply_add_fusion.idx
  170.2 23.4 %first.1 = (bf16[256,64,128]{2,1,0:T(8,128)(2,1)}, bf16[128,64,128]{2,1,0:T(8,128)(2,1)}, f32[12,8,512]{2,1,0:T(8,128)}) custom-call(s32[192]{0:T(256)} %multiply_add_fusion.idx, bf16[192,4096]{1,0:T(8,128)(2,1)} %q_ref.3, bf16[192,4096]{1,0:T(8,128)(2,1)} %o_ref.3, bf16[128,64,128]{2,1,0:T(8,128)(2,1)} %bitcast.26, bf16[128,64,128]{2,1,0:T(8,128)(2,1)} %bitcast.28), custom_call_target="tpu_custom_call" | custom-call | flops 3221225472 | bytes 8388608 | tf_op jit(solution)/shard_map/first/pallas_call | solution.py:237
  193.6 1.5 all-to-all-done.3
  195.2 5.1 %all-to-all-start.4 = ((bf16[16,512,128]{2,1,0:T(8,128)(2,1)}), bf16[16,512,128]{2,1,0:T(8,128)(2,1)S(1)}, u32[]{:S(2)}, u32[]{:S(2)}) async-start(bf16[16,512,128]{2,1,0:T(8,128)(2,1)} %bitcast.30), calls=%async_computation.4 | async-start | bytes 4194304 | tf_op jit(solution)/shard_map/all_to_all | solution.py:394
  200.2 25.9 %second.1 = (bf16[256,64,128]{2,1,0:T(8,128)(2,1)}, bf16[128,64,128]{2,1,0:T(8,128)(2,1)}, f32[192,4096]{1,0:T(8,128)}) custom-call(s32[192]{0:T(256)} %multiply_add_fusion.idx, bf16[192,4096]{1,0:T(8,128)(2,1)} %q_ref.3, bf16[192,4096]{1,0:T(8,128)(2,1)} %o_ref.3, f32[12,8,512]{2,1,0:T(8,128)} %get-tuple-element.19.stats, ...), custom_call_target="tpu_custom_call", output_to_operand_aliasing={{0}: (8, {})} | custom-call | flops 6442450944 | bytes 16777216 | tf_op jit(solution)/shard_map/second/pallas_call | solution.py:297
  226.2 0.0 all-to-all-done.4
  226.2 30.9 %all_to_all.35 = bf16[16,512,128]{2,1,0:T(8,128)(2,1)} all-to-all(bf16[16,512,128]{2,1,0:T(8,128)(2,1)} %bitcast.31), channel_id=1, replica_groups={{0,1,2,3,8,9,10,11,16,17,18,19,24,25,26,27},{4,5,6,7,12,13,14,15,20,21,..., dimensions={0} | all-to-all | bytes 4194304 | tf_op jit(solution)/shard_map/all_to_all | solution.py:394
  257.1 5.4 %all-to-all-start.6 = ((bf16[16,1024,128]{2,1,0:T(8,128)(2,1)}), bf16[16,1024,128]{2,1,0:T(8,128)(2,1)}, u32[]{:S(2)}, u32[]{:S(2)}) async-start(bf16[16,1024,128]{2,1,0:T(8,128)(2,1)} %bitcast.25), calls=%async_computation.6 | async-start | bytes 8388608 | tf_op jit(solution)/shard_map/all_to_all | solution.py:394
  262.5 2.1 relay.2
  264.6 3.6 collective-permute-start.5
  268.2 1.3 collective-permute-start.4
  269.5 0.0 copy-done
  269.5 2.1 relay.3
  271.6 5.0 %collective-permute-start.7 = (bf16[1024,512]{1,0:T(8,128)(2,1)S(1)}, bf16[1024,512]{1,0:T(8,128)(2,1)S(1)}, u32[]{:S(2)}, u32[]{:S(2)}) collective-permute-start(bf16[1024,512]{1,0:T(8,128)(2,1)S(1)} %relay.3), channel_id=1, source_target_pairs={{0,4},{1,5},{6,2},{7,3},{8,12},{9,13},{14,10},{15,11},{16,20},{17,... | collective-permute-start | bytes 3145736 | tf_op jit(solution)/shard_map/ppermute | solution.py:388
  276.7 1.3 collective-permute-start.6
  278.0 54.9 %collective-permute-done.5.dv_outer = bf16[1024,512]{1,0:T(8,128)(2,1)S(1)} collective-permute-done((bf16[1024,512]{1,0:T(8,128)(2,1)S(1)}, bf16[1024,512]{1,0:T(8,128)(2,1)S(1)}, u32[]{:S(2)}, u32[]{:S(2)}) %collective-permute-start.5) | collective-permute-done | bytes 1048608 | tf_op jit(solution)/shard_map/ppermute | solution.py:388
  332.9 0.0 collective-permute-done.4.dv_inner
  332.9 22.5 %collective-permute-done.7.dk_outer = bf16[1024,512]{1,0:T(8,128)(2,1)S(1)} collective-permute-done((bf16[1024,512]{1,0:T(8,128)(2,1)S(1)}, bf16[1024,512]{1,0:T(8,128)(2,1)S(1)}, u32[]{:S(2)}, u32[]{:S(2)}) %collective-permute-start.7) | collective-permute-done | bytes 1048608 | tf_op jit(solution)/shard_map/ppermute | solution.py:388
  355.3 7.2 %collective-permute-done.6.dk_inner = bf16[1024,512]{1,0:T(8,128)(2,1)S(1)} collective-permute-done((bf16[1024,512]{1,0:T(8,128)(2,1)S(1)}, bf16[1024,512]{1,0:T(8,128)(2,1)S(1)}, u32[]{:S(2)}, u32[]{:S(2)}) %collective-permute-start.6) | collective-permute-done | bytes 1048608 | tf_op jit(solution)/shard_map/ppermute | solution.py:388
  362.6 1.0 copy-done.1
  363.6 0.0 all-to-all-done.6
  363.6 1.2 copy-done.2
  364.8 6.7 %finish.1 = (f32[1024,512]{1,0:T(8,128)}, f32[1024,512]{1,0:T(8,128)}) custom-call(s32[128]{0:T(128)S(1)} %squeeze.13.tab, bf16[256,64,128]{2,1,0:T(8,128)(2,1)} %bitcast.19.back, bf16[1024,512]{1,0:T(8,128)(2,1)S(1)} %collective-permute-done.4.dv_inner, bf16[1024,512]{1,0:T(8,128)(2,1)S(1)} %collective-permute-done.5.dv_outer, ...), custom_call_target="tpu_custom_call" | custom-call | flops 8000000 | bytes 12000000 | tf_op jit(solution)/shard_map/finish/pallas_call | solution.py:135
  (11 shorter events, 0.1 us)
Async XLA Ops:
  2.8 1.2 copy-start.3
  7.0 5.7 %copy-start.5 = (bf16[1024,512]{1,0:T(8,128)(2,1)S(1)}, bf16[1024,512]{1,0:T(8,128)(2,1)}, u32[]{:S(2)}) copy-start(bf16[1024,512]{1,0:T(8,128)(2,1)} %shard.3) | copy-start | bytes 3145732
  7.0 31.5 %all-to-all-start = ((bf16[16,512,128]{2,1,0:T(8,128)(2,1)}), bf16[16,512,128]{2,1,0:T(8,128)(2,1)S(1)}, u32[]{:S(2)}, u32[]{:S(2)}) async-start(bf16[16,512,128]{2,1,0:T(8,128)(2,1)} %bitcast.5), calls=%async_computation | async-start | bytes 4194304 | tf_op jit(solution)/shard_map/all_to_all | solution.py:394
  38.4 1.3 copy-start.7
  39.7 5.9 %copy-start.4 = (bf16[1024,512]{1,0:T(8,128)(2,1)S(1)}, bf16[1024,512]{1,0:T(8,128)(2,1)}, u32[]{:S(2)}) copy-start(bf16[1024,512]{1,0:T(8,128)(2,1)} %shard.2) | copy-start | bytes 3145732
  39.7 62.6 %all-to-all-start.1 = ((bf16[16,512,128]{2,1,0:T(8,128)(2,1)}), bf16[16,512,128]{2,1,0:T(8,128)(2,1)}, u32[]{:S(2)}, u32[]{:S(2)}) async-start(bf16[16,512,128]{2,1,0:T(8,128)(2,1)} %bitcast.8), calls=%async_computation.1 | async-start | bytes 4194304 | tf_op jit(solution)/shard_map/all_to_all | solution.py:394
  45.7 45.6 %collective-permute-start.1 = (bf16[1024,512]{1,0:T(8,128)(2,1)S(1)}, bf16[1024,512]{1,0:T(8,128)(2,1)S(1)}, u32[]{:S(2)}, u32[]{:S(2)}) collective-permute-start(bf16[1024,512]{1,0:T(8,128)(2,1)S(1)} %copy-done.4), channel_id=1, source_target_pairs={{0,4},{1,5},{6,2},{7,3},{8,12},{9,13},{14,10},{15,11},{16,20},{17,... | collective-permute-start | bytes 3145736 | tf_op jit(solution)/shard_map/ppermute | solution.py:388
  49.9 49.4 %collective-permute-start = (bf16[1024,512]{1,0:T(8,128)(2,1)S(1)}, bf16[1024,512]{1,0:T(8,128)(2,1)S(1)}, u32[]{:S(2)}, u32[]{:S(2)}) collective-permute-start(bf16[1024,512]{1,0:T(8,128)(2,1)S(1)} %copy-done.4), channel_id=1, source_target_pairs={{2,6},{3,7},{4,0},{5,1},{10,14},{11,15},{12,8},{13,9},{18,22},{19,... | collective-permute-start | bytes 3145736 | tf_op jit(solution)/shard_map/ppermute | solution.py:388
  102.4 5.1 %copy-start.6 = (bf16[1024,512]{1,0:T(8,128)(2,1)S(1)}, bf16[1024,512]{1,0:T(8,128)(2,1)}, u32[]{:S(2)}) copy-start(bf16[1024,512]{1,0:T(8,128)(2,1)} %shard.3) | copy-start | bytes 3145732
  102.4 59.9 %all-to-all-start.2 = ((bf16[16,512,128]{2,1,0:T(8,128)(2,1)}), bf16[16,512,128]{2,1,0:T(8,128)(2,1)S(1)}, u32[]{:S(2)}, u32[]{:S(2)}) async-start(bf16[16,512,128]{2,1,0:T(8,128)(2,1)} %bitcast.10), calls=%async_computation.2 | async-start | bytes 4194304 | tf_op jit(solution)/shard_map/all_to_all | solution.py:394
  107.5 45.6 %collective-permute-start.3 = (bf16[1024,512]{1,0:T(8,128)(2,1)S(1)}, bf16[1024,512]{1,0:T(8,128)(2,1)S(1)}, u32[]{:S(2)}, u32[]{:S(2)}) collective-permute-start(bf16[1024,512]{1,0:T(8,128)(2,1)S(1)} %copy-done.6), channel_id=1, source_target_pairs={{0,4},{1,5},{6,2},{7,3},{8,12},{9,13},{14,10},{15,11},{16,20},{17,... | collective-permute-start | bytes 3145736 | tf_op jit(solution)/shard_map/ppermute | solution.py:388
  109.8 49.4 %collective-permute-start.2 = (bf16[1024,512]{1,0:T(8,128)(2,1)S(1)}, bf16[1024,512]{1,0:T(8,128)(2,1)S(1)}, u32[]{:S(2)}, u32[]{:S(2)}) collective-permute-start(bf16[1024,512]{1,0:T(8,128)(2,1)S(1)} %copy-done.6), channel_id=1, source_target_pairs={{2,6},{3,7},{4,0},{5,1},{10,14},{11,15},{12,8},{13,9},{18,22},{19,... | collective-permute-start | bytes 3145736 | tf_op jit(solution)/shard_map/ppermute | solution.py:388
  162.2 1.3 copy-start.8
  163.6 31.6 %all-to-all-start.3 = ((bf16[16,512,128]{2,1,0:T(8,128)(2,1)}), bf16[16,512,128]{2,1,0:T(8,128)(2,1)}, u32[]{:S(2)}, u32[]{:S(2)}) async-start(bf16[16,512,128]{2,1,0:T(8,128)(2,1)} %bitcast.12), calls=%async_computation.3 | async-start | bytes 4194304 | tf_op jit(solution)/shard_map/all_to_all | solution.py:394
  195.2 31.0 %all-to-all-start.4 = ((bf16[16,512,128]{2,1,0:T(8,128)(2,1)}), bf16[16,512,128]{2,1,0:T(8,128)(2,1)S(1)}, u32[]{:S(2)}, u32[]{:S(2)}) async-start(bf16[16,512,128]{2,1,0:T(8,128)(2,1)} %bitcast.30), calls=%async_computation.4 | async-start | bytes 4194304 | tf_op jit(solution)/shard_map/all_to_all | solution.py:394
  257.1 106.5 %all-to-all-start.6 = ((bf16[16,1024,128]{2,1,0:T(8,128)(2,1)}), bf16[16,1024,128]{2,1,0:T(8,128)(2,1)}, u32[]{:S(2)}, u32[]{:S(2)}) async-start(bf16[16,1024,128]{2,1,0:T(8,128)(2,1)} %bitcast.25), calls=%async_computation.6 | async-start | bytes 8388608 | tf_op jit(solution)/shard_map/all_to_all | solution.py:394
  262.5 7.0 %copy-start = (bf16[16,512,128]{2,1,0:T(8,128)(2,1)S(1)}, bf16[16,512,128]{2,1,0:T(8,128)(2,1)}, u32[]{:S(2)}) copy-start(bf16[16,512,128]{2,1,0:T(8,128)(2,1)} %all_to_all.35) | copy-start | bytes 6291460
  264.6 68.3 %collective-permute-start.5 = (bf16[1024,512]{1,0:T(8,128)(2,1)S(1)}, bf16[1024,512]{1,0:T(8,128)(2,1)S(1)}, u32[]{:S(2)}, u32[]{:S(2)}) collective-permute-start(bf16[1024,512]{1,0:T(8,128)(2,1)S(1)} %relay.2), channel_id=1, source_target_pairs={{0,4},{1,5},{6,2},{7,3},{8,12},{9,13},{14,10},{15,11},{16,20},{17,... | collective-permute-start | bytes 3145736 | tf_op jit(solution)/shard_map/ppermute | solution.py:388
  268.2 64.7 %collective-permute-start.4 = (bf16[1024,512]{1,0:T(8,128)(2,1)S(1)}, bf16[1024,512]{1,0:T(8,128)(2,1)S(1)}, u32[]{:S(2)}, u32[]{:S(2)}) collective-permute-start(bf16[1024,512]{1,0:T(8,128)(2,1)S(1)} %relay.2), channel_id=1, source_target_pairs={{2,6},{3,7},{4,0},{5,1},{10,14},{11,15},{12,8},{13,9},{18,22},{19,... | collective-permute-start | bytes 3145736 | tf_op jit(solution)/shard_map/ppermute | solution.py:388
  271.6 83.7 %collective-permute-start.7 = (bf16[1024,512]{1,0:T(8,128)(2,1)S(1)}, bf16[1024,512]{1,0:T(8,128)(2,1)S(1)}, u32[]{:S(2)}, u32[]{:S(2)}) collective-permute-start(bf16[1024,512]{1,0:T(8,128)(2,1)S(1)} %relay.3), channel_id=1, source_target_pairs={{0,4},{1,5},{6,2},{7,3},{8,12},{9,13},{14,10},{15,11},{16,20},{17,... | collective-permute-start | bytes 3145736 | tf_op jit(solution)/shard_map/ppermute | solution.py:388
  276.7 85.9 %collective-permute-start.6 = (bf16[1024,512]{1,0:T(8,128)(2,1)S(1)}, bf16[1024,512]{1,0:T(8,128)(2,1)S(1)}, u32[]{:S(2)}, u32[]{:S(2)}) collective-permute-start(bf16[1024,512]{1,0:T(8,128)(2,1)S(1)} %relay.3), channel_id=1, source_target_pairs={{2,6},{3,7},{4,0},{5,1},{10,14},{11,15},{12,8},{13,9},{18,22},{19,... | collective-permute-start | bytes 3145736 | tf_op jit(solution)/shard_map/ppermute | solution.py:388
  362.6 1.0 copy-start.1
  363.6 1.2 copy-start.2

commit v5 on v4

--- a/solution.py
+++ b/solution.py
@@ -114,29 +114,46 @@
     )(tab, slots)
 
 
-def finish_kernel(capacity, tab, back, dv_inner, dv_outer, dk_inner, dk_outer, d_values, d_keys):
-    d_values[...] = dv_inner[...].astype(F32) + dv_outer[...].astype(F32)
-    d_keys[...] = dk_inner[...].astype(F32) + dk_outer[...].astype(F32)
-
-    def step(slot, carry):
-        code = tab[slot]
-        spot = slot // capacity * (2 * capacity) + slot % capacity
-        for shift, out in ((0, d_values), (capacity, d_keys)):
-            tile = tile_at(out, jnp.maximum(code, 0))
-            term = back[spot + shift].astype(F32)
+def finish_kernel(
+    capacity, tab, back, dv_inner, dv_outer, dk_inner, dk_outer, d_values, d_keys, terms, sum_values, sum_keys, sems
+):
+    arrive = pltpu.make_async_copy(back, terms, sems.at[0])
+    arrive.start()
+    sum_values[...] = dv_inner[...].astype(F32) + dv_outer[...].astype(F32)
+    sum_keys[...] = dk_inner[...].astype(F32) + dk_outer[...].astype(F32)
+    arrive.wait()
+    leave = []
+    for shift, total, out, sem in ((0, sum_values, d_values, 1), (capacity, sum_keys, d_keys, 2)):
+
+        def step(slot, carry):
+            code = tab[slot]
+            tile = tile_at(total, jnp.maximum(code, 0))
+            term = terms[slot // capacity * (2 * capacity) + slot % capacity + shift].astype(F32)
             tile[...] += jnp.where(code >= 0, term, jnp.zeros_like(term))
-        return carry
-
-    lax.fori_loop(0, tab.shape[0], step, 0, unroll=4)
+            return carry
+
+        lax.fori_loop(0, tab.shape[0], step, 0, unroll=8)
+        copy = pltpu.make_async_copy(total, out, sems.at[sem])
+        copy.start()
+        leave.append(copy)
+    for copy in leave:
+        copy.wait()
 
 
 def finish(tab, capacity, back, dv_far, dk_far):
     shape = jax.ShapeDtypeStruct(dv_far[0].shape, F32)
+    held = pl.BlockSpec(memory_space=pl.ANY)
     return pl.pallas_call(
         functools.partial(finish_kernel, capacity),
         out_shape=(shape, shape),
-        in_specs=[pl.BlockSpec(memory_space=SMEM)] + [pl.BlockSpec(memory_space=VMEM)] * 5,
-        out_specs=[pl.BlockSpec(memory_space=VMEM)] * 2,
+        in_specs=[pl.BlockSpec(memory_space=SMEM), held] + [pl.BlockSpec(memory_space=VMEM)] * 4,
+        out_specs=[held] * 2,
+        scratch_shapes=[
+            VMEM(back.shape, back.dtype),
+            VMEM(shape.shape, F32),
+            VMEM(shape.shape, F32),
+            pltpu.SemaphoreType.DMA((3,)),
+        ],
         compiler_params=params(),
         cost_estimate=pl.CostEstimate(flops=8_000_000, bytes_accessed=12_000_000, transcendentals=0),
         name="finish",

time: 375 us -> 375 us (level)
  no operation moved by 1% of the time
where the time goes in v5:
time: 375 us; the launch traced here: 372 us
  waiting for transfers between devices  205 us (55%)
  Pallas kernels  72.7 us (19%)
  starting transfers between devices  53.3 us (14%)
  blocking collectives  30.9 us (8%)
  local copies, waits for them, and re-layouts  7.44 us (2%)
    ppermute x8, waiting for transfers between devices, across(): parts.append(lax.ppermute(x, ('cx', 'cy'), pairs))  181 us
    all_to_all x6, starting transfers between devices, among(): lax.all_to_all(x.reshape(mates, x.size // (mates * HD), HD), ('cx', 'cy')...  32.9 us
    all_to_all x1, blocking collectives, among(): lax.all_to_all(x.reshape(mates, x.size // (mates * HD), HD), ('cx', 'cy')...  30.9 us
    pallas_call x1, Pallas kernels, second(): pl.pallas_call(functools.partial(second_kernel, capacity), grid=(QB_DEV,...  25.9 us
    all_to_all x6, waiting for transfers between devices, among(): lax.all_to_all(x.reshape(mates, x.size // (mates * HD), HD), ('cx', 'cy')...  24.4 us
    pallas_call x1, Pallas kernels, first(): pl.pallas_call(functools.partial(first_kernel, capacity), grid=(QB_DEV, K...  23.4 us
    ppermute x8, starting transfers between devices, across(): parts.append(lax.ppermute(x, ('cx', 'cy'), pairs))  20.4 us
  transfers between devices with their start and end apart: 14, of which 9 were waited for; matrix products, arithmetic and copies ran while one was open for 0% of the time, Pallas kernels for 17%

profile of v5, /device:TPU:3, one launch (start us, length us, event | category | flops | bytes accessed | tf_op | source)
XLA Modules:
  0.0 372.2 jit_solution(17827030366886649025)
XLA Ops:
  0.7 0.9 copy.11
  1.6 0.2 reshape.238
  1.8 0.1 fusion.14
  1.9 0.1 broadcast_compare_fusion
  2.0 0.1 convolution_convert_fusion
  2.1 0.6 select_reduce_fusion
  2.8 0.1 squeeze.13.tab
  2.8 0.0 copy-start.3
  2.9 1.2 copy-done.3
  4.1 2.9 pack.2
  7.0 0.0 copy-start.5
  7.0 5.7 %all-to-all-start = ((bf16[16,512,128]{2,1,0:T(8,128)(2,1)}), bf16[16,512,128]{2,1,0:T(8,128)(2,1)S(1)}, u32[]{:S(2)}, u32[]{:S(2)}) async-start(bf16[16,512,128]{2,1,0:T(8,128)(2,1)} %bitcast.5), calls=%async_computation | async-start | bytes 4194304 | tf_op jit(solution)/shard_map/all_to_all | solution.py:411
  12.7 0.0 copy-done.5
  12.7 2.9 pack.3
  15.5 22.9 %all-to-all-done = bf16[16,512,128]{2,1,0:T(8,128)(2,1)S(1)} async-done(((bf16[16,512,128]{2,1,0:T(8,128)(2,1)}), bf16[16,512,128]{2,1,0:T(8,128)(2,1)S(1)}, u32[]{:S(2)}, u32[]{:S(2)}) %all-to-all-start) | async-done | bytes 2097184 | tf_op jit(solution)/shard_map/all_to_all | solution.py:411
  38.4 0.0 copy-start.7
  38.4 1.3 copy-done.7
  39.7 0.0 copy-start.4
  39.7 5.9 %all-to-all-start.1 = ((bf16[16,512,128]{2,1,0:T(8,128)(2,1)}), bf16[16,512,128]{2,1,0:T(8,128)(2,1)}, u32[]{:S(2)}, u32[]{:S(2)}) async-start(bf16[16,512,128]{2,1,0:T(8,128)(2,1)} %bitcast.8), calls=%async_computation.1 | async-start | bytes 4194304 | tf_op jit(solution)/shard_map/all_to_all | solution.py:411
  45.6 0.0 copy-done.4
  45.7 4.3 %collective-permute-start.1 = (bf16[1024,512]{1,0:T(8,128)(2,1)S(1)}, bf16[1024,512]{1,0:T(8,128)(2,1)S(1)}, u32[]{:S(2)}, u32[]{:S(2)}) collective-permute-start(bf16[1024,512]{1,0:T(8,128)(2,1)S(1)} %copy-done.4), channel_id=1, source_target_pairs={{0,4},{1,5},{6,2},{7,3},{8,12},{9,13},{14,10},{15,11},{16,20},{17,... | collective-permute-start | bytes 3145736 | tf_op jit(solution)/shard_map/ppermute | solution.py:405
  49.9 1.3 collective-permute-start
  51.3 0.1 squeeze.14.tab
  51.3 39.9 %collective-permute-done.1.outer_part = bf16[1024,512]{1,0:T(8,128)(2,1)S(1)} collective-permute-done((bf16[1024,512]{1,0:T(8,128)(2,1)S(1)}, bf16[1024,512]{1,0:T(8,128)(2,1)S(1)}, u32[]{:S(2)}, u32[]{:S(2)}) %collective-permute-start.1) | collective-permute-done | bytes 1048608 | tf_op jit(solution)/shard_map/ppermute | solution.py:405
  91.2 8.2 %collective-permute-done.inner_part = bf16[1024,512]{1,0:T(8,128)(2,1)S(1)} collective-permute-done((bf16[1024,512]{1,0:T(8,128)(2,1)S(1)}, bf16[1024,512]{1,0:T(8,128)(2,1)S(1)}, u32[]{:S(2)}, u32[]{:S(2)}) %collective-permute-start) | collective-permute-done | bytes 1048608 | tf_op jit(solution)/shard_map/ppermute | solution.py:405
  99.4 3.0 pack_far.2
  102.3 0.0 all-to-all-done.1
  102.4 0.0 copy-start.6
  102.4 5.1 %all-to-all-start.2 = ((bf16[16,512,128]{2,1,0:T(8,128)(2,1)}), bf16[16,512,128]{2,1,0:T(8,128)(2,1)S(1)}, u32[]{:S(2)}, u32[]{:S(2)}) async-start(bf16[16,512,128]{2,1,0:T(8,128)(2,1)} %bitcast.10), calls=%async_computation.2 | async-start | bytes 4194304 | tf_op jit(solution)/shard_map/all_to_all | solution.py:411
  107.5 0.0 copy-done.6
  107.5 2.3 collective-permute-start.3
  109.8 1.3 collective-permute-start.2
  111.1 41.9 %collective-permute-done.3.outer_part = bf16[1024,512]{1,0:T(8,128)(2,1)S(1)} collective-permute-done((bf16[1024,512]{1,0:T(8,128)(2,1)S(1)}, bf16[1024,512]{1,0:T(8,128)(2,1)S(1)}, u32[]{:S(2)}, u32[]{:S(2)}) %collective-permute-start.3) | collective-permute-done | bytes 1048608 | tf_op jit(solution)/shard_map/ppermute | solution.py:405
  153.1 6.2 %collective-permute-done.2.inner_part = bf16[1024,512]{1,0:T(8,128)(2,1)S(1)} collective-permute-done((bf16[1024,512]{1,0:T(8,128)(2,1)S(1)}, bf16[1024,512]{1,0:T(8,128)(2,1)S(1)}, u32[]{:S(2)}, u32[]{:S(2)}) %collective-permute-start.2) | collective-permute-done | bytes 1048608 | tf_op jit(solution)/shard_map/ppermute | solution.py:405
  159.2 3.0 pack_far.3
  162.2 0.0 all-to-all-done.2
  162.2 0.0 copy-start.8
  162.2 1.3 copy-done.8
  163.6 5.7 %all-to-all-start.3 = ((bf16[16,512,128]{2,1,0:T(8,128)(2,1)}), bf16[16,512,128]{2,1,0:T(8,128)(2,1)}, u32[]{:S(2)}, u32[]{:S(2)}) async-start(bf16[16,512,128]{2,1,0:T(8,128)(2,1)} %bitcast.12), calls=%async_computation.3 | async-start | bytes 4194304 | tf_op jit(solution)/shard_map/all_to_all | solution.py:411
  169.2 0.1 reshape.237
  169.4 0.2 convert_reduce_fusion
  169.6 0.6 multiply_add_fusion.idx
  170.2 23.4 %first.1 = (bf16[256,64,128]{2,1,0:T(8,128)(2,1)}, bf16[128,64,128]{2,1,0:T(8,128)(2,1)}, f32[12,8,512]{2,1,0:T(8,128)}) custom-call(s32[192]{0:T(256)} %multiply_add_fusion.idx, bf16[192,4096]{1,0:T(8,128)(2,1)} %q_ref.3, bf16[192,4096]{1,0:T(8,128)(2,1)} %o_ref.3, bf16[128,64,128]{2,1,0:T(8,128)(2,1)} %bitcast.26, bf16[128,64,128]{2,1,0:T(8,128)(2,1)} %bitcast.28), custom_call_target="tpu_custom_call" | custom-call | flops 3221225472 | bytes 8388608 | tf_op jit(solution)/shard_map/first/pallas_call | solution.py:254
  193.6 1.5 all-to-all-done.3
  195.2 5.1 %all-to-all-start.4 = ((bf16[16,512,128]{2,1,0:T(8,128)(2,1)}), bf16[16,512,128]{2,1,0:T(8,128)(2,1)S(1)}, u32[]{:S(2)}, u32[]{:S(2)}) async-start(bf16[16,512,128]{2,1,0:T(8,128)(2,1)} %bitcast.30), calls=%async_computation.4 | async-start | bytes 4194304 | tf_op jit(solution)/shard_map/all_to_all | solution.py:411
  200.2 25.9 %second.1 = (bf16[256,64,128]{2,1,0:T(8,128)(2,1)}, bf16[128,64,128]{2,1,0:T(8,128)(2,1)}, f32[192,4096]{1,0:T(8,128)}) custom-call(s32[192]{0:T(256)} %multiply_add_fusion.idx, bf16[192,4096]{1,0:T(8,128)(2,1)} %q_ref.3, bf16[192,4096]{1,0:T(8,128)(2,1)} %o_ref.3, f32[12,8,512]{2,1,0:T(8,128)} %get-tuple-element.19.stats, ...), custom_call_target="tpu_custom_call", output_to_operand_aliasing={{0}: (8, {})} | custom-call | flops 6442450944 | bytes 16777216 | tf_op jit(solution)/shard_map/second/pallas_call | solution.py:314
  226.2 0.0 all-to-all-done.4
  226.2 30.9 %all_to_all.35 = bf16[16,512,128]{2,1,0:T(8,128)(2,1)} all-to-all(bf16[16,512,128]{2,1,0:T(8,128)(2,1)} %bitcast.31), channel_id=1, replica_groups={{0,1,2,3,8,9,10,11,16,17,18,19,24,25,26,27},{4,5,6,7,12,13,14,15,20,21,..., dimensions={0} | all-to-all | bytes 4194304 | tf_op jit(solution)/shard_map/all_to_all | solution.py:411
  257.1 5.4 %all-to-all-start.6 = ((bf16[16,1024,128]{2,1,0:T(8,128)(2,1)}), bf16[16,1024,128]{2,1,0:T(8,128)(2,1)}, u32[]{:S(2)}, u32[]{:S(2)}) async-start(bf16[16,1024,128]{2,1,0:T(8,128)(2,1)} %bitcast.25), calls=%async_computation.6 | async-start | bytes 8388608 | tf_op jit(solution)/shard_map/all_to_all | solution.py:411
  262.5 2.1 relay.2
  264.6 3.6 collective-permute-start.5
  268.2 1.3 collective-permute-start.4
  269.5 0.0 copy-done
  269.5 2.1 relay.3
  271.6 5.0 %collective-permute-start.7 = (bf16[1024,512]{1,0:T(8,128)(2,1)S(1)}, bf16[1024,512]{1,0:T(8,128)(2,1)S(1)}, u32[]{:S(2)}, u32[]{:S(2)}) collective-permute-start(bf16[1024,512]{1,0:T(8,128)(2,1)S(1)} %relay.3), channel_id=1, source_target_pairs={{0,4},{1,5},{6,2},{7,3},{8,12},{9,13},{14,10},{15,11},{16,20},{17,... | collective-permute-start | bytes 3145736 | tf_op jit(solution)/shard_map/ppermute | solution.py:405
  276.7 1.3 collective-permute-start.6
  278.0 54.9 %collective-permute-done.5.dv_outer = bf16[1024,512]{1,0:T(8,128)(2,1)S(1)} collective-permute-done((bf16[1024,512]{1,0:T(8,128)(2,1)S(1)}, bf16[1024,512]{1,0:T(8,128)(2,1)S(1)}, u32[]{:S(2)}, u32[]{:S(2)}) %collective-permute-start.5) | collective-permute-done | bytes 1048608 | tf_op jit(solution)/shard_map/ppermute | solution.py:405
  332.9 0.0 collective-permute-done.4.dv_inner
  332.9 22.5 %collective-permute-done.7.dk_outer = bf16[1024,512]{1,0:T(8,128)(2,1)S(1)} collective-permute-done((bf16[1024,512]{1,0:T(8,128)(2,1)S(1)}, bf16[1024,512]{1,0:T(8,128)(2,1)S(1)}, u32[]{:S(2)}, u32[]{:S(2)}) %collective-permute-start.7) | collective-permute-done | bytes 1048608 | tf_op jit(solution)/shard_map/ppermute | solution.py:405
  355.3 7.2 %collective-permute-done.6.dk_inner = bf16[1024,512]{1,0:T(8,128)(2,1)S(1)} collective-permute-done((bf16[1024,512]{1,0:T(8,128)(2,1)S(1)}, bf16[1024,512]{1,0:T(8,128)(2,1)S(1)}, u32[]{:S(2)}, u32[]{:S(2)}) %collective-permute-start.6) | collective-permute-done | bytes 1048608 | tf_op jit(solution)/shard_map/ppermute | solution.py:405
  362.6 1.0 copy-done.1
  363.6 0.0 all-to-all-done.6
  363.6 1.2 copy-done.2
  364.8 7.4 %finish.1 = (f32[1024,512]{1,0:T(8,128)}, f32[1024,512]{1,0:T(8,128)}) custom-call(s32[128]{0:T(128)S(1)} %squeeze.13.tab, bf16[256,64,128]{2,1,0:T(8,128)(2,1)} %bitcast.19.back, bf16[1024,512]{1,0:T(8,128)(2,1)S(1)} %collective-permute-done.4.dv_inner, bf16[1024,512]{1,0:T(8,128)(2,1)S(1)} %collective-permute-done.5.dv_outer, ...), custom_call_target="tpu_custom_call" | custom-call | flops 8000000 | bytes 12000000 | tf_op jit(solution)/shard_map/finish/pallas_call | solution.py:146
  (11 shorter events, 0.1 us)
Async XLA Ops:
  2.8 1.2 copy-start.3
  7.0 5.7 %copy-start.5 = (bf16[1024,512]{1,0:T(8,128)(2,1)S(1)}, bf16[1024,512]{1,0:T(8,128)(2,1)}, u32[]{:S(2)}) copy-start(bf16[1024,512]{1,0:T(8,128)(2,1)} %shard.3) | copy-start | bytes 3145732
  7.0 31.5 %all-to-all-start = ((bf16[16,512,128]{2,1,0:T(8,128)(2,1)}), bf16[16,512,128]{2,1,0:T(8,128)(2,1)S(1)}, u32[]{:S(2)}, u32[]{:S(2)}) async-start(bf16[16,512,128]{2,1,0:T(8,128)(2,1)} %bitcast.5), calls=%async_computation | async-start | bytes 4194304 | tf_op jit(solution)/shard_map/all_to_all | solution.py:411
  38.4 1.3 copy-start.7
  39.7 5.9 %copy-start.4 = (bf16[1024,512]{1,0:T(8,128)(2,1)S(1)}, bf16[1024,512]{1,0:T(8,128)(2,1)}, u32[]{:S(2)}) copy-start(bf16[1024,512]{1,0:T(8,128)(2,1)} %shard.2) | copy-start | bytes 3145732
  39.7 62.6 %all-to-all-start.1 = ((bf16[16,512,128]{2,1,0:T(8,128)(2,1)}), bf16[16,512,128]{2,1,0:T(8,128)(2,1)}, u32[]{:S(2)}, u32[]{:S(2)}) async-start(bf16[16,512,128]{2,1,0:T(8,128)(2,1)} %bitcast.8), calls=%async_computation.1 | async-start | bytes 4194304 | tf_op jit(solution)/shard_map/all_to_all | solution.py:411
  45.7 45.6 %collective-permute-start.1 = (bf16[1024,512]{1,0:T(8,128)(2,1)S(1)}, bf16[1024,512]{1,0:T(8,128)(2,1)S(1)}, u32[]{:S(2)}, u32[]{:S(2)}) collective-permute-start(bf16[1024,512]{1,0:T(8,128)(2,1)S(1)} %copy-done.4), channel_id=1, source_target_pairs={{0,4},{1,5},{6,2},{7,3},{8,12},{9,13},{14,10},{15,11},{16,20},{17,... | collective-permute-start | bytes 3145736 | tf_op jit(solution)/shard_map/ppermute | solution.py:405
  49.9 49.4 %collective-permute-start = (bf16[1024,512]{1,0:T(8,128)(2,1)S(1)}, bf16[1024,512]{1,0:T(8,128)(2,1)S(1)}, u32[]{:S(2)}, u32[]{:S(2)}) collective-permute-start(bf16[1024,512]{1,0:T(8,128)(2,1)S(1)} %copy-done.4), channel_id=1, source_target_pairs={{2,6},{3,7},{4,0},{5,1},{10,14},{11,15},{12,8},{13,9},{18,22},{19,... | collective-permute-start | bytes 3145736 | tf_op jit(solution)/shard_map/ppermute | solution.py:405
  102.4 5.1 %copy-start.6 = (bf16[1024,512]{1,0:T(8,128)(2,1)S(1)}, bf16[1024,512]{1,0:T(8,128)(2,1)}, u32[]{:S(2)}) copy-start(bf16[1024,512]{1,0:T(8,128)(2,1)} %shard.3) | copy-start | bytes 3145732
  102.4 59.9 %all-to-all-start.2 = ((bf16[16,512,128]{2,1,0:T(8,128)(2,1)}), bf16[16,512,128]{2,1,0:T(8,128)(2,1)S(1)}, u32[]{:S(2)}, u32[]{:S(2)}) async-start(bf16[16,512,128]{2,1,0:T(8,128)(2,1)} %bitcast.10), calls=%async_computation.2 | async-start | bytes 4194304 | tf_op jit(solution)/shard_map/all_to_all | solution.py:411
  107.5 45.6 %collective-permute-start.3 = (bf16[1024,512]{1,0:T(8,128)(2,1)S(1)}, bf16[1024,512]{1,0:T(8,128)(2,1)S(1)}, u32[]{:S(2)}, u32[]{:S(2)}) collective-permute-start(bf16[1024,512]{1,0:T(8,128)(2,1)S(1)} %copy-done.6), channel_id=1, source_target_pairs={{0,4},{1,5},{6,2},{7,3},{8,12},{9,13},{14,10},{15,11},{16,20},{17,... | collective-permute-start | bytes 3145736 | tf_op jit(solution)/shard_map/ppermute | solution.py:405
  109.8 49.4 %collective-permute-start.2 = (bf16[1024,512]{1,0:T(8,128)(2,1)S(1)}, bf16[1024,512]{1,0:T(8,128)(2,1)S(1)}, u32[]{:S(2)}, u32[]{:S(2)}) collective-permute-start(bf16[1024,512]{1,0:T(8,128)(2,1)S(1)} %copy-done.6), channel_id=1, source_target_pairs={{2,6},{3,7},{4,0},{5,1},{10,14},{11,15},{12,8},{13,9},{18,22},{19,... | collective-permute-start | bytes 3145736 | tf_op jit(solution)/shard_map/ppermute | solution.py:405
  162.2 1.3 copy-start.8
  163.6 31.6 %all-to-all-start.3 = ((bf16[16,512,128]{2,1,0:T(8,128)(2,1)}), bf16[16,512,128]{2,1,0:T(8,128)(2,1)}, u32[]{:S(2)}, u32[]{:S(2)}) async-start(bf16[16,512,128]{2,1,0:T(8,128)(2,1)} %bitcast.12), calls=%async_computation.3 | async-start | bytes 4194304 | tf_op jit(solution)/shard_map/all_to_all | solution.py:411
  195.2 31.0 %all-to-all-start.4 = ((bf16[16,512,128]{2,1,0:T(8,128)(2,1)}), bf16[16,512,128]{2,1,0:T(8,128)(2,1)S(1)}, u32[]{:S(2)}, u32[]{:S(2)}) async-start(bf16[16,512,128]{2,1,0:T(8,128)(2,1)} %bitcast.30), calls=%async_computation.4 | async-start | bytes 4194304 | tf_op jit(solution)/shard_map/all_to_all | solution.py:411
  257.1 106.5 %all-to-all-start.6 = ((bf16[16,1024,128]{2,1,0:T(8,128)(2,1)}), bf16[16,1024,128]{2,1,0:T(8,128)(2,1)}, u32[]{:S(2)}, u32[]{:S(2)}) async-start(bf16[16,1024,128]{2,1,0:T(8,128)(2,1)} %bitcast.25), calls=%async_computation.6 | async-start | bytes 8388608 | tf_op jit(solution)/shard_map/all_to_all | solution.py:411
  262.5 7.0 %copy-start = (bf16[16,512,128]{2,1,0:T(8,128)(2,1)S(1)}, bf16[16,512,128]{2,1,0:T(8,128)(2,1)}, u32[]{:S(2)}) copy-start(bf16[16,512,128]{2,1,0:T(8,128)(2,1)} %all_to_all.35) | copy-start | bytes 6291460
  264.6 68.3 %collective-permute-start.5 = (bf16[1024,512]{1,0:T(8,128)(2,1)S(1)}, bf16[1024,512]{1,0:T(8,128)(2,1)S(1)}, u32[]{:S(2)}, u32[]{:S(2)}) collective-permute-start(bf16[1024,512]{1,0:T(8,128)(2,1)S(1)} %relay.2), channel_id=1, source_target_pairs={{0,4},{1,5},{6,2},{7,3},{8,12},{9,13},{14,10},{15,11},{16,20},{17,... | collective-permute-start | bytes 3145736 | tf_op jit(solution)/shard_map/ppermute | solution.py:405
  268.2 64.7 %collective-permute-start.4 = (bf16[1024,512]{1,0:T(8,128)(2,1)S(1)}, bf16[1024,512]{1,0:T(8,128)(2,1)S(1)}, u32[]{:S(2)}, u32[]{:S(2)}) collective-permute-start(bf16[1024,512]{1,0:T(8,128)(2,1)S(1)} %relay.2), channel_id=1, source_target_pairs={{2,6},{3,7},{4,0},{5,1},{10,14},{11,15},{12,8},{13,9},{18,22},{19,... | collective-permute-start | bytes 3145736 | tf_op jit(solution)/shard_map/ppermute | solution.py:405
  271.6 83.7 %collective-permute-start.7 = (bf16[1024,512]{1,0:T(8,128)(2,1)S(1)}, bf16[1024,512]{1,0:T(8,128)(2,1)S(1)}, u32[]{:S(2)}, u32[]{:S(2)}) collective-permute-start(bf16[1024,512]{1,0:T(8,128)(2,1)S(1)} %relay.3), channel_id=1, source_target_pairs={{0,4},{1,5},{6,2},{7,3},{8,12},{9,13},{14,10},{15,11},{16,20},{17,... | collective-permute-start | bytes 3145736 | tf_op jit(solution)/shard_map/ppermute | solution.py:405
  276.7 85.9 %collective-permute-start.6 = (bf16[1024,512]{1,0:T(8,128)(2,1)S(1)}, bf16[1024,512]{1,0:T(8,128)(2,1)S(1)}, u32[]{:S(2)}, u32[]{:S(2)}) collective-permute-start(bf16[1024,512]{1,0:T(8,128)(2,1)S(1)} %relay.3), channel_id=1, source_target_pairs={{2,6},{3,7},{4,0},{5,1},{10,14},{11,15},{12,8},{13,9},{18,22},{19,... | collective-permute-start | bytes 3145736 | tf_op jit(solution)/shard_map/ppermute | solution.py:405
  362.6 1.0 copy-start.1
  363.6 1.2 copy-start.2
